TPU v7x, 256 devices: a whole 4x4x8 slice. The times are simulated.
256 devices in a mesh: tp: 8 (over x, core), cp: 32 (over z, y).
Axes of the slice: x: 4, y: 4, z: 8, core: 2. Of those that a mesh axis runs over, the one named last changes fastest.
Arguments:
- tokens: bfloat16 [1024, 8192], P(('cp', 'tp')), may hold values from -6 to 6
- attention_gain: float32 [8192], replicated, may hold values from 0.1 to 1.9
- query_weight: bfloat16 [8192, 8192], P('cp', 'tp'), may hold values from -0.0625 to 0.0625
- key_weight: bfloat16 [8192, 1024], P('cp', 'tp'), may hold values from -0.0625 to 0.0625
- value_weight: bfloat16 [8192, 1024], P('cp', 'tp'), may hold values from -0.0625 to 0.0625
- out_weight: bfloat16 [8192, 8192], P('tp', 'cp'), may hold values from -0.0625 to 0.0625
- feed_gain: float32 [8192], replicated, may hold values from 0.1 to 1.9
- gate_weight: bfloat16 [8192, 28672], P('tp', 'cp'), may hold values from -0.0625 to 0.0625
- up_weight: bfloat16 [8192, 28672], P('tp', 'cp'), may hold values from -0.0625 to 0.0625
- down_weight: bfloat16 [28672, 8192], P('cp', 'tp'), may hold values from -0.03125 to 0.03125
Outputs:
- attended: bfloat16 [1024, 8192], P(('cp', 'tp'))
- mixed: bfloat16 [1024, 8192], P(('cp', 'tp'))
All inputs are finite; a program needn't handle non-finite values.
Results may differ from a plain program's by a relative error of at most 0.035.
Values may be sent and summed in bfloat16 or wider, within the bound.
A program may use at most 64 MiB of HBM per device.

v0:
```python
import jax
import jax.numpy as jnp
from jax import lax
from jax.sharding import Mesh
from jax.sharding import PartitionSpec as P

HD = 128
CP = ("cp_0", "cp_1")
CP_TP = ("cp_0", "cp_1", "tp")


epsilon = 1e-05
rope_base = 500000.0
masked = -1e30


def summed_rows(product, extent, axes):
    total = product(jnp.int32(0), extent * lax.axis_size(axes)).astype(jnp.bfloat16)
    for axis in axes:
        total = lax.psum_scatter(total, axis, scatter_dimension=0, tiled=True)
    return total.astype(jnp.float32)


def gathered_by_axis(shard, axes, dim):
    for axis in reversed(axes):
        shard = lax.all_gather(shard, axis, axis=dim, tiled=True)
    return shard


def over_axes(shard, axes, dim, take_in, carry):
    everything = jax.tree.map(lambda part: gathered_by_axis(part, axes, dim), shard)
    return take_in(carry, everything, jnp.int32(0))


def worked_whole(shard, axes, dim, work):
    everything = gathered_by_axis(shard, axes, dim)
    return work(everything, jnp.int32(0))


def padded_to(lines, length):
    spare = -lines.shape[0] % length
    if not spare:
        return lines
    return jnp.concatenate([lines, jnp.zeros((spare, *lines.shape[1:]), lines.dtype)])


def sum_by_parts(shard, axis):
    lines = shard.reshape(-1, *shard.shape[1:][-1:])
    own = lax.psum_scatter(
        padded_to(lines, lax.axis_size(axis)), axis, scatter_dimension=0, tiled=True
    )
    whole = lax.all_gather(own, axis).reshape(-1, *lines.shape[1:])
    return lax.slice_in_dim(whole, 0, len(lines)).reshape(shard.shape)


def normalize(values, gain):
    widened = values.astype(jnp.float32)
    mean_square = jnp.mean(widened * widened, axis=-1, keepdims=True)
    return (widened * lax.rsqrt(mean_square + epsilon) * gain).astype(jnp.bfloat16)


def rotate(values, positions):
    row_count = values.shape[0]
    heads = values.reshape(row_count, -1, HD)
    half = HD // 2
    inverse = rope_base ** (-(jnp.arange(half, dtype=jnp.float32) * 2.0 / HD))
    angles = positions.astype(jnp.float32)[:, None] * inverse[None, :]
    cosine = jnp.cos(angles)[:, None, :]
    sine = jnp.sin(angles)[:, None, :]
    first = heads[..., :half]
    second = heads[..., half:]
    turned = jnp.concatenate(
        [first * cosine - second * sine, second * cosine + first * sine], axis=-1
    )
    return turned.reshape(row_count, -1)


def activate(units, unit_width):
    return (jax.nn.silu(units[:, :unit_width]) * units[:, unit_width:]).astype(jnp.bfloat16)


def on_device(
    tokens,
    attention_gain,
    query_weight,
    key_weight,
    value_weight,
    out_weight,
    feed_gain,
    gate_weight,
    up_weight,
    down_weight,
):
    tensor_ways = lax.axis_size("tp")
    context_ways = lax.axis_size(CP)
    local_rows = tokens.shape[0]
    block_rows = local_rows * tensor_ways
    normed = normalize(tokens, attention_gain)
    scattered = lax.all_to_all(normed, CP, split_axis=1, concat_axis=0, tiled=True)
    grouped = lax.all_gather(scattered, "tp", axis=0, tiled=True)
    column_width = grouped.shape[1]
    columns = (
        grouped.reshape(tensor_ways, context_ways, local_rows, column_width)
        .transpose(1, 0, 2, 3)
        .reshape(-1, column_width)
    )
    query_width = query_weight.shape[1]
    key_width = key_weight.shape[1]

    def project(start, count):
        picked = lax.dynamic_slice_in_dim(columns, start, count, 0)
        return jnp.concatenate(
            [
                jnp.dot(picked, query_weight, preferred_element_type=jnp.float32),
                jnp.dot(picked, key_weight, preferred_element_type=jnp.float32),
                jnp.dot(picked, value_weight, preferred_element_type=jnp.float32),
            ],
            axis=1,
        )

    summed = summed_rows(project, block_rows, CP)
    positions = lax.axis_index(CP) * block_rows + jnp.arange(block_rows, dtype=jnp.int32)
    query = rotate(summed[:, :query_width], positions).astype(jnp.bfloat16)
    keys = rotate(summed[:, query_width : query_width + key_width], positions).astype(jnp.bfloat16)
    values = summed[:, query_width + key_width :].astype(jnp.bfloat16)
    shared_heads = key_width // HD
    group_size = query_width // key_width
    query_heads = query.reshape(block_rows, shared_heads, group_size, HD)
    scale = HD ** (-0.5)

    def attend(carry, piece, start):
        running_top, running_total, weighted = carry
        key_piece, value_piece = piece
        piece_rows = key_piece.shape[0]
        key_heads = key_piece.reshape(piece_rows, shared_heads, HD)
        value_heads = value_piece.reshape(piece_rows, shared_heads, HD)
        scores = (
            jnp.einsum("qkgd,skd->kgqs", query_heads, key_heads, preferred_element_type=jnp.float32)
            * scale
        )
        key_positions = start + jnp.arange(piece_rows, dtype=jnp.int32)
        allowed = key_positions[None, :] <= positions[:, None]
        scores = jnp.where(allowed, scores, masked)
        new_top = jnp.maximum(running_top, jnp.max(scores, axis=-1))
        weights = jnp.where(allowed, jnp.exp(scores - new_top[..., None]), 0.0)
        factor = jnp.exp(running_top - new_top)
        new_total = running_total * factor + jnp.sum(weights, axis=-1)
        new_weighted = weighted * factor[..., None] + jnp.einsum(
            "kgqs,skd->kgqd",
            weights,
            value_heads.astype(jnp.float32),
            precision=lax.Precision.HIGHEST,
        )
        return (new_top, new_total, new_weighted)

    head_shape = (shared_heads, group_size, block_rows)
    initial = (
        jnp.full(head_shape, masked, jnp.float32),
        jnp.zeros(head_shape, jnp.float32),
        jnp.zeros(head_shape + (HD,), jnp.float32),
    )
    final_top, final_total, final_weighted = over_axes((keys, values), CP, 0, attend, initial)
    attention = (
        (final_weighted / final_total[..., None])
        .transpose(2, 0, 1, 3)
        .reshape(block_rows, query_width)
        .astype(jnp.bfloat16)
    )

    def output_rows(piece, start):
        return jnp.dot(piece, out_weight, preferred_element_type=jnp.float32)

    partial_out = worked_whole(attention, CP, 0, output_rows)
    regrouped = lax.all_to_all(
        partial_out.astype(jnp.bfloat16), CP, split_axis=0, concat_axis=1, tiled=True
    ).astype(partial_out.dtype)
    projected = lax.psum_scatter(
        regrouped.astype(jnp.bfloat16), "tp", scatter_dimension=0, tiled=True
    ).astype(jnp.float32)
    attended = (tokens.astype(jnp.float32) + projected).astype(jnp.bfloat16)
    normed_feed = normalize(attended, feed_gain)
    spread_rows = lax.all_to_all(normed_feed, "tp", split_axis=1, concat_axis=0, tiled=True)
    unit_width = gate_weight.shape[1]

    def unit_rows(piece, start):
        return jnp.concatenate(
            [
                jnp.dot(piece, gate_weight, preferred_element_type=jnp.float32),
                jnp.dot(piece, up_weight, preferred_element_type=jnp.float32),
            ],
            axis=1,
        )

    partial_units = worked_whole(spread_rows, CP, 0, unit_rows)
    units = sum_by_parts(partial_units.astype(jnp.bfloat16), "tp").astype(jnp.float32)
    hidden = activate(units, unit_width)

    def down_rows(start, count):
        picked = lax.dynamic_slice_in_dim(hidden, start, count, 0)
        return jnp.dot(picked, down_weight, preferred_element_type=jnp.float32)

    reduced = summed_rows(down_rows, block_rows, CP)
    lowered = lax.all_to_all(
        reduced.astype(jnp.bfloat16), "tp", split_axis=0, concat_axis=1, tiled=True
    ).astype(reduced.dtype)
    mixed = (attended.astype(jnp.float32) + lowered).astype(jnp.bfloat16)
    return (attended, mixed)


def solution(mesh):
    split = Mesh(mesh.devices.reshape(mesh.shape["tp"], 8, 4), ("tp", "cp_0", "cp_1"))
    in_specs = (
        P(CP_TP, None),
        P(),
        P(CP, "tp"),
        P(CP, "tp"),
        P(CP, "tp"),
        P("tp", CP),
        P(),
        P("tp", CP),
        P("tp", CP),
        P(CP, "tp"),
    )
    out_specs = (P(CP_TP, None), P(CP_TP, None))
    return jax.shard_map(
        on_device, mesh=split, in_specs=in_specs, out_specs=out_specs, check_vma=False
    )
```

profile of v0, /device:TPU:1, one launch (start us, length us, event | category | flops | bytes accessed | tf_op | source)
XLA Modules:
  0.0 578.9 jit_solution(12624802839477399914)
XLA Ops:
  7.2 1.1 fusion.14
  9.4 20.5 %all_to_all.70 = bf16[4,32,256]{2,0,1:T(4,128)(2,1)S(1)} all-to-all(bf16[4,32,256]{2,0,1:T(4,128)(2,1)S(1)} %bitcast.71), channel_id=1, replica_groups=mesh['tp'=8,'cp_0'=8,'cp_1'=4] {'cp_0','cp_1'}, dimensions={1} | all-to-all | bytes 131072 | tf_op jit(solution)/shard_map/all_to_all | solution.py:99
  29.9 15.4 %all_gather.33 = bf16[1024,256]{1,0:T(8,128)(2,1)S(1)} all-gather(bf16[128,256]{1,0:T(8,128)(2,1)S(1)} %all_to_all.55), channel_id=1, replica_groups=mesh['tp'=8,'cp_0'=8,'cp_1'=4] {'tp'}, dimensions={0}, use_global_device_ids=true | all-gather | bytes 589824 | tf_op jit(solution)/shard_map/all_gather | solution.py:100
  46.5 1.8 convolution_convert_fusion.1
  48.3 1.8 pad_maximum_fusion.1
  50.0 4.4 copy.59
  54.5 34.0 %reduce-scatter.16.cloned.1.call-done = bf16[128,1280]{1,0:T(8,128)(2,1)} async-done(((bf16[1024,1280]{1,0:T(8,128)(2,1)}), bf16[128,1280]{1,0:T(8,128)(2,1)}) %reduce-scatter.16.cloned.1.call-update) | async-done | bytes 327696
  88.9 26.8 %reduce-scatter.18.cloned.1.call-done = bf16[32,1280]{1,0:T(8,128)(2,1)} async-done(((bf16[128,1280]{1,0:T(8,128)(2,1)}), bf16[32,1280]{1,0:T(8,128)(2,1)}) %reduce-scatter.18.cloned.1.call-update) | async-done | bytes 81936 | tf_op jit(solution)/shard_map/reduce_scatter | solution.py:20
  117.4 8.9 %all_gather.36 = bf16[128,128]{1,0:T(8,128)(2,1)S(1)} all-gather(bf16[32,128]{1,0:T(8,128)(2,1)S(1)} %slice.43), channel_id=1, replica_groups=mesh['tp'=8,'cp_0'=8,'cp_1'=4] {'cp_1'}, dimensions={0}, use_global_device_ids=true | all-gather | bytes 40960 | tf_op jit(solution)/shard_map/all_gather | solution.py:26
  126.5 8.9 %all-gather = bf16[128,1,128]{2,0,1:T(8,128)(2,1)S(1)} all-gather(bf16[32,1,128]{2,0,1:T(8,128)(2,1)S(1)} %pad_maximum_fusion.2), channel_id=2, replica_groups=mesh['tp'=8,'cp_0'=8,'cp_1'=4] {'cp_1'}, dimensions={0}, use_global_device_ids=true | all-gather | bytes 40960 | tf_op jit(solution)/shard_map/all_gather | solution.py:26
  135.6 20.2 %all-gather.1 = bf16[1024,1,128]{2,0,1:T(8,128)(2,1)S(1)} all-gather(bf16[128,1,128]{2,0,1:T(8,128)(2,1)S(1)} %all-gather), channel_id=3, replica_groups=mesh['tp'=8,'cp_0'=8,'cp_1'=4] {'cp_0'}, dimensions={0}, use_global_device_ids=true | all-gather | bytes 294912 | tf_op jit(solution)/shard_map/all_gather | solution.py:26
  155.8 18.8 %all_gather.37 = bf16[1024,128]{1,0:T(8,128)(2,1)S(1)} all-gather(bf16[128,128]{1,0:T(8,128)(2,1)S(1)} %all_gather.36), channel_id=1, replica_groups=mesh['tp'=8,'cp_0'=8,'cp_1'=4] {'cp_0'}, dimensions={0}, use_global_device_ids=true | all-gather | bytes 294912 | tf_op jit(solution)/shard_map/all_gather | solution.py:26
  176.3 10.1 %all_gather.38 = bf16[128,1024]{1,0:T(8,128)(2,1)} all-gather(bf16[32,1024]{1,0:T(8,128)(2,1)S(1)} %bitcast.70), channel_id=1, replica_groups=mesh['tp'=8,'cp_0'=8,'cp_1'=4] {'cp_1'}, dimensions={0}, use_global_device_ids=true | all-gather | bytes 327680 | tf_op jit(solution)/shard_map/all_gather | solution.py:26
  186.5 57.9 %all-gather.7.cloned.1.call-done = bf16[1024,1024]{1,0:T(8,128)(2,1)} async-done(((bf16[128,1024]{1,0:T(8,128)(2,1)}), bf16[1024,1024]{1,0:T(8,128)(2,1)}) %all-gather.7.cloned.1.call-update) | async-done | bytes 2097168 | tf_op jit(solution)/shard_map/all_gather | solution.py:26
  244.4 2.3 convolution_convert_fusion.4
  246.7 19.5 %all_to_all.71 = bf16[32,32,256]{2,1,0:T(8,128)(2,1)S(1)} all-to-all(bf16[32,32,256]{2,1,0:T(8,128)(2,1)S(1)} %bitcast.68), channel_id=1, replica_groups=mesh['tp'=8,'cp_0'=8,'cp_1'=4] {'cp_0','cp_1'}, dimensions={0} | all-to-all | bytes 1048576 | tf_op jit(solution)/shard_map/all_to_all | solution.py:174
  268.4 64.0 %all-reduce.3.cloned.1.call-done = bf16[32,8192]{1,0:T(8,128)(2,1)} async-done(((bf16[32,8192]{1,0:T(8,128)(2,1)}), bf16[32,8192]{1,0:T(8,128)(2,1)}) %all-reduce.3.cloned.1.call-update) | async-done | bytes 524304
  333.7 10.0 %all_to_all.72 = bf16[4,8,1024]{2,0,1:T(4,128)(2,1)S(1)} all-to-all(bf16[4,8,1024]{2,0,1:T(4,128)(2,1)S(1)} %bitcast.74), channel_id=1, replica_groups=mesh['tp'=8,'cp_0'=8,'cp_1'=4] {'tp'}, dimensions={1} | all-to-all | bytes 131072 | tf_op jit(solution)/shard_map/all_to_all | solution.py:182
  343.7 10.9 %all_gather.40 = bf16[128,1024]{1,0:T(8,128)(2,1)} all-gather(bf16[32,1024]{1,0:T(8,128)(2,1)S(1)} %all_to_all.63), channel_id=1, replica_groups=mesh['tp'=8,'cp_0'=8,'cp_1'=4] {'cp_1'}, dimensions={0}, use_global_device_ids=true | all-gather | bytes 327680 | tf_op jit(solution)/shard_map/all_gather | solution.py:26
  354.8 37.9 %all-gather.9.cloned.1.call-done = bf16[1024,1024]{1,0:T(8,128)(2,1)} async-done(((bf16[128,1024]{1,0:T(8,128)(2,1)}), bf16[1024,1024]{1,0:T(8,128)(2,1)}) %all-gather.9.cloned.1.call-update) | async-done | bytes 2097168 | tf_op jit(solution)/shard_map/all_gather | solution.py:26
  392.7 4.4 convolution_convert_fusion.2
  397.1 2.1 convolution_convert_fusion.3
  399.3 2.2 pad_maximum_fusion
  401.5 6.0 %copy.63 = bf16[1024,1792]{1,0:T(8,128)(2,1)} copy(bf16[1024,1792]{0,1:T(8,128)(2,1)} %pad_maximum_fusion) | data formatting | bytes 7340032
  407.5 39.9 %reduce-scatter.20.cloned.1.call-done = bf16[128,1792]{1,0:T(8,128)(2,1)} async-done(((bf16[1024,1792]{1,0:T(8,128)(2,1)}), bf16[128,1792]{1,0:T(8,128)(2,1)}) %reduce-scatter.20.cloned.1.call-update) | async-done | bytes 458768
  447.4 2.0 copy.64
  449.5 37.2 %all-gather.11.cloned.1.call-done = bf16[1024,1792]{0,1:T(8,128)(2,1)} async-done(((bf16[128,1792]{0,1:T(8,128)(2,1)}), bf16[1024,1792]{0,1:T(8,128)(2,1)}) %all-gather.11.cloned.1.call-update) | async-done | bytes 3670032 | tf_op jit(solution)/shard_map/all_gather | solution.py:52
  486.7 2.9 convert_element_type.110
  489.6 3.9 convolution_convert_fusion
  493.5 38.4 %reduce-scatter.12.cloned.1.call-done = bf16[128,1024]{1,0:T(8,128)(2,1)} async-done(((bf16[1024,1024]{1,0:T(8,128)(2,1)}), bf16[128,1024]{1,0:T(8,128)(2,1)}) %reduce-scatter.12.cloned.1.call-update) | async-done | bytes 262160 | tf_op jit(solution)/shard_map/reduce_scatter | solution.py:20
  531.9 27.0 %reduce-scatter.14.cloned.1.call-done = bf16[32,1024]{1,0:T(8,128)(2,1)} async-done(((bf16[128,1024]{1,0:T(8,128)(2,1)}), bf16[32,1024]{1,0:T(8,128)(2,1)}) %reduce-scatter.14.cloned.1.call-update) | async-done | bytes 65552 | tf_op jit(solution)/shard_map/reduce_scatter | solution.py:20
  559.8 11.9 %all_to_all.73 = bf16[8,4,1024]{2,1,0:T(4,128)(2,1)S(1)} all-to-all(bf16[8,4,1024]{2,1,0:T(4,128)(2,1)S(1)} %all_to_all.64), channel_id=1, replica_groups=mesh['tp'=8,'cp_0'=8,'cp_1'=4] {'tp'}, dimensions={0} | all-to-all | bytes 131072 | tf_op jit(solution)/shard_map/all_to_all | solution.py:203
  (76 shorter events, 10.9 us)
Async XLA Ops:
  7.2 482.4 %copy-start = (bf16[896,1024]{1,0:T(8,128)(2,1)S(1)}, bf16[896,1024]{1,0:T(8,128)(2,1)}, u32[]{:S(2)}) copy-start(bf16[896,1024]{1,0:T(8,128)(2,1)} %param.19) | copy-start | bytes 5505028
  7.2 38.7 %copy-start.3 = (bf16[256,128]{1,0:T(8,128)(2,1)S(1)}, bf16[256,128]{1,0:T(8,128)(2,1)}, u32[]{:S(2)}) copy-start(bf16[256,128]{1,0:T(8,128)(2,1)} %param.14) | copy-start | bytes 196612
  7.2 39.0 %copy-start.4 = (bf16[256,128]{1,0:T(8,128)(2,1)S(1)}, bf16[256,128]{1,0:T(8,128)(2,1)}, u32[]{:S(2)}) copy-start(bf16[256,128]{1,0:T(8,128)(2,1)} %param.13) | copy-start | bytes 196612
  7.2 81.4 %reduce-scatter.16.cloned.1.call-start = ((), (), s32[]{:S(2)}) async-start(), calls=%async_computation.14 | async-start | bytes 2949120
  54.5 61.3 %reduce-scatter.18.cloned.1.call-start = ((), (), s32[]{:S(2)}) async-start(), calls=%async_computation.15 | async-start | bytes 409600 | tf_op jit(solution)/shard_map/reduce_scatter | solution.py:20
  88.6 155.8 %all-gather.7.cloned.1.call-start = ((), (), s32[]{:S(2)}) async-start(), calls=%async_computation.9 | async-start | bytes 2359296 | tf_op jit(solution)/shard_map/all_gather | solution.py:26
  174.6 69.8 %copy-start.8 = (bf16[1024,256]{1,0:T(8,128)(2,1)S(1)}, bf16[1024,256]{1,0:T(8,128)(2,1)}, u32[]{:S(2)}) copy-start(bf16[1024,256]{1,0:T(8,128)(2,1)} %param.15) | copy-start | bytes 1572868
  186.4 146.0 %all-reduce.3.cloned.1.call-start = ((), (), s32[]{:S(2)}) async-start(), calls=%async_computation.17 | async-start | bytes 1048576
  246.7 20.5 %copy-start.9 = (u32[256]{0:T(256)S(1)}, u32[256]{0:T(256)}, u32[]{:S(2)}) copy-start(u32[256]{0:T(256)} %constant.43) | copy-start | bytes 3076
  246.7 85.7 %copy-start.1 = (bf16[4,8192]{1,0:T(4,128)(2,1)S(1)}, bf16[4,8192]{1,0:T(4,128)(2,1)}, u32[]{:S(2)}) copy-start(bf16[4,8192]{1,0:T(4,128)(2,1)} %param.10) | copy-start | bytes 196612
  246.7 86.8 %copy-start.5 = (f32[8192]{0:T(1024)S(1)}, f32[8192]{0:T(1024)}, u32[]{:S(2)}) copy-start(f32[8192]{0:T(1024)} %param.16) | copy-start | bytes 98308
  267.1 125.6 %all-gather.9.cloned.1.call-start = ((), (), s32[]{:S(2)}) async-start(), calls=%async_computation.10 | async-start | bytes 2359296 | tf_op jit(solution)/shard_map/all_gather | solution.py:26
  333.5 238.2 %copy-start.2 = (bf16[4,8192]{1,0:T(4,128)(2,1)}, bf16[4,8192]{1,0:T(4,128)(2,1)S(1)}, u32[]{:S(2)}) copy-start(bf16[4,8192]{1,0:T(4,128)(2,1)S(1)} %get-tuple-element.3) | copy-start | bytes 196612
  354.6 92.8 %reduce-scatter.20.cloned.1.call-start = ((), (), s32[]{:S(2)}) async-start(), calls=%async_computation.16 | async-start | bytes 4128768
  392.7 4.4 copy-start.6
  392.7 4.4 copy-start.7
  407.5 79.2 %all-gather.11.cloned.1.call-start = ((), (), s32[]{:S(2)}) async-start(), calls=%async_computation.13 | async-start | bytes 4128768 | tf_op jit(solution)/shard_map/all_gather | solution.py:52
  449.4 82.5 %reduce-scatter.12.cloned.1.call-start = ((), (), s32[]{:S(2)}) async-start(), calls=%async_computation.11 | async-start | bytes 2359296 | tf_op jit(solution)/shard_map/reduce_scatter | solution.py:20
  493.5 65.4 %reduce-scatter.14.cloned.1.call-start = ((), (), s32[]{:S(2)}) async-start(), calls=%async_computation.12 | async-start | bytes 327680 | tf_op jit(solution)/shard_map/reduce_scatter | solution.py:20
Sparse Core Ops, SparseCore 0:
  54.6 33.9 reduce-scatter.15
  91.1 24.5 reduce-scatter.17
  186.6 57.7 all-gather.6
  267.2 65.1 all-reduce.2
  354.7 37.9 all-gather.8
  407.6 39.7 reduce-scatter.19
  449.5 37.0 all-gather.10
  493.6 38.2 reduce-scatter.11
  534.4 24.4 reduce-scatter.13
where the time goes:
time: 580 us; the launch traced here: 579 us
  waiting for transfers between devices  363 us (63%)
  blocking collectives  155 us (27%)
  matrix products  16.3 us (3%)
  local copies, waits for them, and re-layouts  16.2 us (3%)
  between operations  14.8 us (3%)
  other arithmetic  12.6 us (2%)
    unnamed x12, waiting for transfers between devices  138 us
    all_gather x2, waiting for transfers between devices, gathered_by_axis(): shard = lax.all_gather(shard, axis, axis=dim, tiled=True)  95.8 us
    reduce_scatter x3, waiting for transfers between devices, summed_rows(): total = lax.psum_scatter(total, axis, scatter_dimension=0, tiled=True)  92.2 us
    all_gather x6, blocking collectives, gathered_by_axis(): shard = lax.all_gather(shard, axis, axis=dim, tiled=True)  77.9 us
    all_gather x1, waiting for transfers between devices, sum_by_parts(): whole = lax.all_gather(own, axis).reshape(-1, *lines.shape[1:])  37.2 us
    all_to_all x1, blocking collectives, on_device(): lax.all_to_all(normed, CP, split_axis=1, concat_axis=0, tiled=True)  20.5 us
    all_to_all x1, blocking collectives, on_device(): lax.all_to_all(partial_out.astype(jnp.bfloat16), CP, split_axis=0, concat...  19.5 us
    all_gather x1, blocking collectives, on_device(): grouped = lax.all_gather(scattered, 'tp', axis=0, tiled=True)  15.4 us
  transfers between devices with their start and end apart: 9, of which 9 were waited for; matrix products, arithmetic and copies ran while one was open for 0% of the time, Pallas kernels for 0%

commit v1 on v0

v1 whole, which is shorter than its diff:
```python
import collections
import functools

import jax
import jax.numpy as jnp
from jax import lax
from jax.experimental import pallas as pl
from jax.experimental.pallas import tpu as pltpu
from jax.sharding import PartitionSpec as P

HD = 128
NZ, NY, NX = 8, 4, 4
CP, TP = NZ * NY, NX * 2
MESH = pl.DeviceIdType.MESH
F32, BF16 = jnp.float32, jnp.bfloat16

epsilon = 1e-05
rope_base = 500000.0
masked = -1e30


class Wires:
    def __init__(self, send, recv):
        self.send, self.recv, self.used, self.sent = send, recv, 0, []

    def copy(self, src, dst, device):
        i = self.used
        self.used += 1
        c = pltpu.make_async_remote_copy(
            src_ref=src,
            dst_ref=dst,
            send_sem=self.send.at[i],
            recv_sem=self.recv.at[i],
            device_id=device,
            device_id_type=MESH,
        )
        c.start()
        self.sent.append(c)
        return c

    def drain(self):
        for c in self.sent:
            c.wait_send()


class Steps:
    def __init__(self):
        self.queue = collections.deque()

    def add(self, gen):
        if next(gen, self) is not self:
            self.queue.append(gen)

    def run(self):
        while self.queue:
            self.add(self.queue.popleft())


class Place:
    def __init__(self):
        self.cp, self.tp = lax.axis_index("cp"), lax.axis_index("tp")
        self.z, self.y = self.cp // NY, self.cp % NY
        self.x, self.core = self.tp // 2, self.tp % 2

    def along_z(self, z):
        return {"cp": z * NY + self.y}

    def along_y(self, y):
        return {"cp": self.z * NY + y}

    def along_x(self, x):
        return {"tp": x * 2 + self.core}

    def partner(self):
        return {"tp": self.x * 2 + 1 - self.core}


def ring(n, me, device_of):
    return device_of((me + 1) % n), device_of((me + n - 1) % n)


def greet(devices):
    barrier = pltpu.get_barrier_semaphore()
    for device in devices:
        pl.semaphore_signal(barrier, inc=1, device_id=device, device_id_type=MESH)
    return len(devices)


def greet_group(axis, n, me):
    barrier = pltpu.get_barrier_semaphore()

    def signal(off, carry):
        pl.semaphore_signal(
            barrier, inc=1, device_id={axis: (me + off) % n}, device_id_type=MESH
        )
        return carry

    lax.fori_loop(1, n, signal, 0)
    return n - 1


def await_greetings(count):
    pl.semaphore_wait(pltpu.get_barrier_semaphore(), count)


def half_of(ref, h):
    d = ref.shape[0] // 2
    return ref.at[pl.ds(h * d, d)]


def ring_gather(wires, block, n, me, device_of, arrived=None):
    right, left = ring(n, me, device_of)
    last = n // 2 - 1

    def send(k):
        r, l = block((me + n - k) % n), block((me + k) % n)
        if k == last:
            r, l = half_of(r, 0), half_of(l, 1)
        return wires.copy(r, r, right), wires.copy(l, l, left)

    flying = send(0)
    if arrived:
        arrived(me)
    for k in range(1, n // 2 + 1):
        yield
        for c in flying:
            c.wait_recv()
        if k <= last:
            flying = send(k)
            if arrived:
                arrived((me + n - k) % n)
                arrived((me + k) % n)
        elif arrived:
            arrived((me + n // 2) % n)


def add_rows(dst, terms, finish=None):
    if len(dst.shape) == 3:
        for i in range(dst.shape[0]):
            add_rows(dst.at[i], [t.at[i] for t in terms])
        return
    rows = dst.shape[0]
    step = min(rows, 16)

    def body(i, carry):
        at = pl.ds(pl.multiple_of(i * step, step), step)
        total = terms[0][at, :].astype(F32)
        for t in terms[1:]:
            total = total + t[at, :].astype(F32)
        dst[at, :] = total.astype(dst.dtype)
        return carry

    lax.fori_loop(0, rows // step, body, 0)


def ring_scatter(wires, own, out, from_left, from_right, n, me, device_of):
    right, left = ring(n, me, device_of)
    m = n // 2
    far = own((me + m) % n)
    r = wires.copy(half_of(far, 0), half_of(from_left.at[0], 0), right)
    l = wires.copy(half_of(far, 1), half_of(from_right.at[0], 1), left)
    for k in range(1, m):
        yield
        to_right, to_left = own((me + m - k) % n), own((me + n - m + k) % n)
        got_left, got_right = from_left.at[k - 1], from_right.at[k - 1]
        r.wait_recv()
        if k == 1:
            add_rows(half_of(got_left, 0), [half_of(got_left, 0), half_of(to_right, 0)])
            add_rows(half_of(got_left, 1), [half_of(to_right, 1)])
        else:
            add_rows(got_left, [got_left, to_right])
        r = wires.copy(got_left, from_left.at[k], right)
        l.wait_recv()
        if k == 1:
            add_rows(half_of(got_right, 1), [half_of(got_right, 1), half_of(to_left, 1)])
            add_rows(half_of(got_right, 0), [half_of(to_left, 0)])
        else:
            add_rows(got_right, [got_right, to_left])
        l = wires.copy(got_right, from_right.at[k], left)
    yield
    r.wait_recv()
    l.wait_recv()
    add_rows(out, [own(me), from_left.at[m - 1], from_right.at[m - 1]])


def exchange(send_sem, recv_sem, source, target, axis, n, me, meanwhile=None):
    def copy(off):
        peer = (me + off) % n
        return pltpu.make_async_remote_copy(
            src_ref=source(peer),
            dst_ref=target(me),
            send_sem=send_sem.at[off],
            recv_sem=recv_sem.at[off],
            device_id={axis: peer},
            device_id_type=MESH,
        )

    def start(off, carry):
        copy(off).start()
        return carry

    def wait(off, carry):
        copy(off).wait()
        return carry

    lax.fori_loop(1, n, start, 0)
    if meanwhile:
        meanwhile()
    lax.fori_loop(1, n, wait, 0)


VMEM = pl.BlockSpec(memory_space=pltpu.VMEM)


def call(kernel, out_shape, inputs, scratch, collective_id, name):
    return pl.pallas_call(
        kernel,
        out_shape=out_shape,
        in_specs=[VMEM] * len(inputs),
        out_specs=jax.tree.map(lambda _: VMEM, out_shape),
        scratch_shapes=scratch,
        compiler_params=pltpu.CompilerParams(
            collective_id=collective_id,
            has_side_effects=True,
            vmem_limit_bytes=56 * 1024 * 1024,
        ),
        name=name,
    )(*inputs)


def dma(count):
    return pltpu.SemaphoreType.DMA((count,))


def spread_kernel(x_ref, out_ref, got, s0, r0, s1, r1):
    at = Place()
    await_greetings(greet_group("cp", CP, at.cp) + greet_group("tp", TP, at.tp))

    def keep():
        got[at.cp] = x_ref[at.cp]

    exchange(s0, r0, lambda p: x_ref.at[p], lambda p: got.at[p], "cp", CP, at.cp, keep)

    def keep_too():
        out_ref[at.tp] = got[...]

    exchange(s1, r1, lambda p: got, lambda p: out_ref.at[p], "tp", TP, at.tp, keep_too)


def spread(x, collective_id):
    return call(
        spread_kernel,
        jax.ShapeDtypeStruct((TP, *x.shape), x.dtype),
        (x,),
        [pltpu.VMEM(x.shape, x.dtype), dma(CP), dma(CP), dma(TP), dma(TP)],
        collective_id,
        "spread",
    )


def collect_kernel(x_ref, out_ref, got, total, s0, r0, s1, r1):
    at = Place()
    await_greetings(greet_group("cp", CP, at.cp) + greet_group("tp", TP, at.tp))

    def keep():
        got[at.tp] = x_ref[at.tp]

    exchange(s0, r0, lambda p: x_ref.at[p], lambda p: got.at[p], "tp", TP, at.tp, keep)

    def body(i, carry):
        parts = got[0, i].astype(F32)
        for t in range(1, TP):
            parts = parts + got[t, i].astype(F32)
        total[i] = parts.astype(BF16)
        return carry

    lax.fori_loop(0, CP, body, 0)

    def keep_too():
        out_ref[at.cp] = total[at.cp]

    exchange(s1, r1, lambda p: total.at[p], lambda p: out_ref.at[p], "cp", CP, at.cp, keep_too)


def collect(x, collective_id):
    return call(
        collect_kernel,
        jax.ShapeDtypeStruct(x.shape[1:], x.dtype),
        (x,),
        [
            pltpu.VMEM(x.shape, x.dtype),
            pltpu.VMEM(x.shape[1:], x.dtype),
            dma(TP),
            dma(TP),
            dma(CP),
            dma(CP),
        ],
        collective_id,
        "collect",
    )


def swap_kernel(x_ref, out_ref, s0, r0):
    at = Place()
    await_greetings(greet_group("tp", TP, at.tp))

    def keep():
        out_ref[at.tp] = x_ref[at.tp]

    exchange(s0, r0, lambda p: x_ref.at[p], lambda p: out_ref.at[p], "tp", TP, at.tp, keep)


def swap(x, collective_id):
    return call(
        swap_kernel,
        jax.ShapeDtypeStruct(x.shape, x.dtype),
        (x,),
        [dma(TP), dma(TP)],
        collective_id,
        "swap",
    )


def greet_context(at):
    return greet([*ring(NZ, at.z, at.along_z), *ring(NY, at.y, at.along_y)])


def gather_rows(wires, steps, at, out_ref, split):
    first, rest = pl.ds(0, split), pl.ds(split, out_ref.shape[-1] - split)

    def y_first():
        yield from ring_gather(
            wires, lambda j: out_ref.at[at.z, j, :, rest], NY, at.y, at.along_y
        )
        yield from ring_gather(
            wires, lambda i: out_ref.at[i, :, :, rest], NZ, at.z, at.along_z
        )

    def to_y(i):
        steps.add(
            ring_gather(wires, lambda j: out_ref.at[i, j, :, first], NY, at.y, at.along_y)
        )

    steps.add(y_first())
    steps.add(
        ring_gather(
            wires, lambda i: out_ref.at[i, at.y, :, first], NZ, at.z, at.along_z, to_y
        )
    )


GATHER_COPIES = 2 * (NY // 2 + NZ // 2) + NZ + NZ * NY


def gather_kernel(split, x_ref, out_ref, send, recv):
    at = Place()
    greeted = greet_context(at)
    out_ref[at.z, at.y] = x_ref[...]
    await_greetings(greeted)
    wires, steps = Wires(send, recv), Steps()
    gather_rows(wires, steps, at, out_ref, split)
    steps.run()
    wires.drain()


def gather(x, split, collective_id):
    return call(
        functools.partial(gather_kernel, split),
        jax.ShapeDtypeStruct((NZ, NY, *x.shape), x.dtype),
        (x,),
        [dma(GATHER_COPIES), dma(GATHER_COPIES)],
        collective_id,
        "gather",
    )


def product_into(part, x_ref, w_ref, start):
    width = w_ref.shape[1]
    tile = min(width, 256)

    def body(i, carry):
        at = pl.multiple_of(i * tile, tile)
        p = jnp.dot(x_ref[...], w_ref[:, pl.ds(at, tile)], preferred_element_type=F32)
        part[:, :, :, pl.ds(pl.multiple_of(start + at, 128), tile)] = p.astype(BF16).reshape(
            *part.shape[:3], tile
        )
        return carry

    lax.fori_loop(0, width // tile, body, 0)


def scatter_rows(wires, steps, at, part, out, split, bufs):
    zl, zr, yl, yr, y_sum, yl2, yr2, zl2, zr2, z_sum = bufs
    first, rest = pl.ds(0, split), pl.ds(split, part.shape[-1] - split)

    def z_first():
        yield from ring_scatter(
            wires, lambda i: part.at[i, :, :, first], y_sum, zl, zr, NZ, at.z, at.along_z
        )
        yield from ring_scatter(
            wires, lambda j: y_sum.at[j], out.at[:, first], yl, yr, NY, at.y, at.along_y
        )

    def y_first():
        yield from ring_scatter(
            wires, lambda j: part.at[:, j, :, rest], z_sum, yl2, yr2, NY, at.y, at.along_y
        )
        yield from ring_scatter(
            wires, lambda i: z_sum.at[i], out.at[:, rest], zl2, zr2, NZ, at.z, at.along_z
        )

    steps.add(y_first())
    steps.add(z_first())


SCATTER_COPIES = 2 * (NZ + NY)


def scatter_scratch(rows, width, split):
    a, b = split, width - split

    def both(*shape):
        return [pltpu.VMEM(shape, BF16), pltpu.VMEM(shape, BF16)]

    return [
        *both(NZ // 2, NY, rows, a),
        *both(NY // 2, rows, a),
        pltpu.VMEM((NY, rows, a), BF16),
        *both(NY // 2, NZ, rows, b),
        *both(NZ // 2, rows, b),
        pltpu.VMEM((NZ, rows, b), BF16),
    ]


def project_kernel(split, count, *refs):
    x_ref, weights, out_ref = refs[0], refs[1 : 1 + count], refs[1 + count]
    part, *bufs = refs[2 + count : -2]
    send, recv = refs[-2:]
    at = Place()
    greeted = greet_context(at)
    start = 0
    for w_ref in weights:
        product_into(part, x_ref, w_ref, start)
        start += w_ref.shape[1]
    await_greetings(greeted)
    wires, steps = Wires(send, recv), Steps()
    scatter_rows(wires, steps, at, part, out_ref, split, bufs)
    steps.run()
    wires.drain()


def project(x, weights, split, collective_id):
    rows = x.shape[0] // CP
    width = sum(w.shape[1] for w in weights)
    return call(
        functools.partial(project_kernel, split, len(weights)),
        jax.ShapeDtypeStruct((rows, width), F32),
        (x, *weights),
        [
            pltpu.VMEM((NZ, NY, rows, width), BF16),
            *scatter_scratch(rows, width, split),
            dma(SCATTER_COPIES),
            dma(SCATTER_COPIES),
        ],
        collective_id,
        "project",
    )


UNITS = 2


def feed_kernel(x_ref, gate_ref, up_ref, out_ref, part, held, fl, fr, total, send, recv):
    at = Place()
    partner = at.partner()
    await_greetings(greet([*ring(NX, at.x, at.along_x), partner]))
    wires, steps = Wires(send, recv), Steps()
    units = gate_ref.shape[1]
    block = part.shape[2]
    rows = block // UNITS
    other = 1 - at.core

    def product(i):
        x = x_ref.at[pl.ds(pl.multiple_of(i * 2 * block, 2 * block), 2 * block)]

        def tile(w_ref, col, width, start):
            p = jnp.dot(x[...], w_ref[:, pl.ds(col, width)], preferred_element_type=F32)
            part[i, :, :, pl.ds(start + col, width)] = p.astype(BF16).reshape(2, block, width)

        def body(t, carry):
            col = pl.multiple_of(t * 256, 256)
            tile(gate_ref, col, 256, 0)
            tile(up_ref, col, 256, units)
            return carry

        lax.fori_loop(0, units // 256, body, 0)
        if units % 256:
            tile(gate_ref, units // 256 * 256, units % 256, 0)
            tile(up_ref, units // 256 * 256, units % 256, units)
        return wires.copy(part.at[i, other], held.at[i], partner)

    def combine(i, c):
        c.wait_recv()
        add_rows(held.at[i], [held.at[i], part.at[i, at.core]])

    def line(u):
        at_rows = pl.ds(u * rows, rows)
        yield from ring_scatter(
            wires,
            lambda i: held.at[i, at_rows],
            total.at[u],
            fl.at[u],
            fr.at[u],
            NX,
            at.x,
            at.along_x,
        )

        def body(i, carry):
            r = pl.ds(pl.multiple_of(i * 16, 16), 16)
            gate, up = total[u, r, pl.ds(0, units)], total[u, r, pl.ds(units, units)]
            out_ref[at.x, at.core, pl.ds(pl.multiple_of(u * rows + i * 16, 16), 16), :] = (
                jax.nn.silu(gate) * up
            ).astype(BF16)
            return carry

        lax.fori_loop(0, rows // 16, body, 0)

        def hand_over(i):
            ref = out_ref.at[i, at.core, at_rows]
            handed.append(wires.copy(ref, ref, partner))

        yield from ring_gather(
            wires, lambda i: out_ref.at[i, at.core, at_rows], NX, at.x, at.along_x, hand_over
        )

    handed = []
    order = [(at.x + 2) % NX, (at.x + 1) % NX, (at.x + 3) % NX, at.x]
    copies = [product(order[0])]
    copies.append(product(order[1]))
    combine(order[0], copies[0])
    for u in range(UNITS):
        steps.add(line(u))
    copies.append(product(order[2]))
    combine(order[1], copies[1])
    copies.append(product(order[3]))
    combine(order[2], copies[2])
    combine(order[3], copies[3])
    steps.run()
    for c in handed:
        c.wait_recv()
    wires.drain()


def feed(x, gate, up, collective_id):
    block = x.shape[0] // TP
    units = gate.shape[1]
    copies = NX + UNITS * (2 * NX + NX)
    steps = NX // 2
    return call(
        feed_kernel,
        jax.ShapeDtypeStruct((NX, 2, block, units), BF16),
        (x, gate, up),
        [
            pltpu.VMEM((NX, 2, block, 2 * units), BF16),
            pltpu.VMEM((NX, block, 2 * units), BF16),
            pltpu.VMEM((UNITS, steps, block // UNITS, 2 * units), BF16),
            pltpu.VMEM((UNITS, steps, block // UNITS, 2 * units), BF16),
            pltpu.VMEM((UNITS, block // UNITS, 2 * units), F32),
            dma(copies),
            dma(copies),
        ],
        collective_id,
        "feed",
    )


def normalize(values, gain):
    widened = values.astype(F32)
    mean_square = jnp.mean(widened * widened, axis=-1, keepdims=True)
    return (widened * lax.rsqrt(mean_square + epsilon) * gain).astype(BF16)


def rotate(values, positions):
    row_count = values.shape[0]
    heads = values.reshape(row_count, -1, HD)
    half = HD // 2
    inverse = rope_base ** (-(jnp.arange(half, dtype=F32) * 2.0 / HD))
    angles = positions.astype(F32)[:, None] * inverse[None, :]
    cosine = jnp.cos(angles)[:, None, :]
    sine = jnp.sin(angles)[:, None, :]
    first = heads[..., :half]
    second = heads[..., half:]
    turned = jnp.concatenate(
        [first * cosine - second * sine, second * cosine + first * sine], axis=-1
    )
    return turned.reshape(row_count, -1)


def attend(query, keys, values, positions):
    block_rows, query_width = query.shape
    everywhere = keys.shape[0]
    shared_heads = keys.shape[1] // HD
    query_heads = query.reshape(block_rows, shared_heads, -1, HD)
    key_heads = keys.reshape(everywhere, shared_heads, HD)
    value_heads = values.reshape(everywhere, shared_heads, HD)
    scores = jnp.einsum("qkgd,skd->kgqs", query_heads, key_heads, preferred_element_type=F32)
    scores = scores * HD ** (-0.5)
    allowed = jnp.arange(everywhere, dtype=jnp.int32)[None, :] <= positions[:, None]
    scores = jnp.where(allowed, scores, masked)
    top = jnp.max(scores, axis=-1)
    weights = jnp.where(allowed, jnp.exp(scores - top[..., None]), 0.0)
    total = jnp.sum(weights, axis=-1)
    weighted = jnp.einsum(
        "kgqs,skd->kgqd",
        weights,
        value_heads.astype(F32),
        precision=lax.Precision.HIGHEST,
    )
    mean = weighted / total[..., None]
    return mean.transpose(2, 0, 1, 3).reshape(block_rows, query_width).astype(BF16)


def on_device(
    tokens,
    attention_gain,
    query_weight,
    key_weight,
    value_weight,
    out_weight,
    feed_gain,
    gate_weight,
    up_weight,
    down_weight,
):
    local_rows, model = tokens.shape
    block_rows = local_rows * TP
    rows = block_rows * CP
    query_width, key_width = query_weight.shape[1], key_weight.shape[1]

    normed = normalize(tokens, attention_gain)
    slices = normed.reshape(local_rows, CP, -1).transpose(1, 0, 2)
    columns = spread(slices, 0).transpose(1, 0, 2, 3).reshape(rows, -1)
    summed = project(columns, (query_weight, key_weight, value_weight), 640, 1)
    positions = lax.axis_index("cp") * block_rows + jnp.arange(block_rows, dtype=jnp.int32)
    query = rotate(summed[:, :query_width], positions).astype(BF16)
    keys = rotate(summed[:, query_width : query_width + key_width], positions).astype(BF16)
    values = summed[:, query_width + key_width :].astype(BF16)
    shared = gather(jnp.concatenate([keys, values], axis=1), key_width, 2)
    shared = shared.reshape(rows, 2 * key_width)
    attention = attend(query, shared[:, :key_width], shared[:, key_width:], positions)

    everywhere = gather(attention, 640, 3).reshape(rows, -1)
    partial_out = jnp.dot(everywhere, out_weight, preferred_element_type=F32).astype(BF16)
    by_owner = partial_out.reshape(CP, TP, local_rows, -1).transpose(1, 0, 2, 3)
    projected = collect(by_owner, 4).transpose(1, 0, 2).reshape(local_rows, model)
    attended = (tokens.astype(F32) + projected.astype(F32)).astype(BF16)

    normed_feed = normalize(attended, feed_gain)
    by_width = normed_feed.reshape(local_rows, TP, -1).transpose(1, 0, 2)
    block = swap(by_width, 5).reshape(block_rows, -1)
    stream = gather(block, 640, 6).reshape(rows, -1)
    hidden = feed(stream, gate_weight, up_weight, 7).reshape(rows, -1)
    reduced = project(hidden, (down_weight,), 512, 8)
    by_token = reduced.astype(BF16).reshape(TP, local_rows, -1)
    lowered = swap(by_token, 9).transpose(1, 0, 2).reshape(local_rows, model)
    mixed = (attended.astype(F32) + lowered.astype(F32)).astype(BF16)
    return attended, mixed


def solution(mesh):
    in_specs = (
        P(("cp", "tp"), None),
        P(),
        P("cp", "tp"),
        P("cp", "tp"),
        P("cp", "tp"),
        P("tp", "cp"),
        P(),
        P("tp", "cp"),
        P("tp", "cp"),
        P("cp", "tp"),
    )
    out_specs = (P(("cp", "tp"), None), P(("cp", "tp"), None))
    return jax.shard_map(
        on_device, mesh=mesh, in_specs=in_specs, out_specs=out_specs, check_vma=False
    )
```

time: 580 us -> 278 us (0.48)
  waiting for transfers between devices: 363 us -> 0 us
  Pallas kernels: 0 us -> 255 us
  blocking collectives: 155 us -> 0 us
  between operations: 14.8 us -> 0.9 us
  matrix products: 16.3 us -> 4.52 us
  local copies, waits for them, and re-layouts: 16.2 us -> 8.65 us
    pallas_call x0 -> x10, Pallas kernels: none -> 255 us  [call(): pl.pallas_call(kernel, out_shape=out_shape, in_specs=[VMEM] * len(inputs)...]
    unnamed x12 -> x0, waiting for transfers between devices: 138 us -> none
    all_gather x3 -> x0, waiting for transfers between devices: 133 us -> none  [the longest x2 95.8 us: gathered_by_axis(): shard = lax.all_gather(shard, axis, axis=dim, tiled=True)]
    all_gather x7 -> x0, blocking collectives: 93.3 us -> none  [the longest x6 77.9 us: gathered_by_axis(): shard = lax.all_gather(shard, axis, axis=dim, tiled=True)]
    reduce_scatter x3 -> x0, waiting for transfers between devices: 92.2 us -> none  [summed_rows(): total = lax.psum_scatter(total, axis, scatter_dimension=0, tiled=True)]
    all_to_all x4 -> x0, blocking collectives: 61.9 us -> none  [the longest x1 20.5 us: on_device(): lax.all_to_all(normed, CP, split_axis=1, concat_axis=0, tiled=True)]
    dot_general x8 -> x2, matrix products: 15.9 us -> 3.09 us  [the longest x1 2.3 us: on_device(): jnp.dot(everywhere, out_weight, preferred_element_type=F32).astype(BF16)]
    unnamed x27 -> x13, local copies, waits for them, and re-layouts: 13.1 us -> 1.61 us
  transfers between devices with their start and end apart: 9 -> 0, of which waited for: 9 -> 0; matrix products, arithmetic and copies ran while one was open for 0% -> 0% of each run, Pallas kernels for 0% -> 0%
where the time goes in v1:
time: 278 us; the launch traced here: 277 us
  Pallas kernels  255 us (92%)
  local copies, waits for them, and re-layouts  8.65 us (3%)
  other arithmetic  8.33 us (3%)
  matrix products  4.52 us (2%)
    pallas_call x10, Pallas kernels, call(): pl.pallas_call(kernel, out_shape=out_shape, in_specs=[VMEM] * len(inputs)...  255 us

profile of v1, /device:TPU:1, one launch (start us, length us, event | category | flops | bytes accessed | tf_op | source)
XLA Modules:
  0.0 277.4 jit_solution(3658580830445912562)
XLA Ops:
  0.7 1.1 fusion.9
  2.0 1.6 fusion.11
  3.6 25.8 %spread.1 = bf16[8,32,4,256]{3,2,1,0:T(4,128)(2,1)} custom-call(bf16[32,4,256]{2,1,0:T(4,128)(2,1)} %bitcast.66), custom_call_target="tpu_custom_call" | custom-call | tf_op jit(solution)/shard_map/spread/pallas_call | solution.py:216
  29.4 1.3 copy.16
  30.7 0.9 reshape.204.refs_0_
  31.6 33.2 %project.2 = f32[32,1280]{1,0:T(8,128)} custom-call(bf16[1024,256]{1,0:T(8,128)(2,1)} %reshape.204.refs_0_, bf16[256,1024]{1,0:T(8,128)(2,1)} %refs_1_.2, bf16[256,128]{1,0:T(8,128)(2,1)} %refs_2_.1, bf16[256,128]{1,0:T(8,128)(2,1)} %refs_3_.1), custom_call_target="tpu_custom_call" | custom-call | tf_op jit(solution)/shard_map/project/pallas_call | solution.py:216
  64.8 0.7 slice.55
  65.5 0.7 slice_bitcast_fusion.5
  66.3 0.9 slice_bitcast_fusion.4
  67.4 0.6 pad_maximum_fusion.x_ref
  68.2 20.8 %gather.3 = bf16[8,4,32,256]{3,2,1,0:T(8,128)(2,1)} custom-call(bf16[32,256]{1,0:T(8,128)(2,1)} %pad_maximum_fusion.x_ref), custom_call_target="tpu_custom_call" | custom-call | tf_op jit(solution)/shard_map/gather/pallas_call | solution.py:216
  89.1 1.4 fusion.33
  90.5 0.3 fusion.5
  90.9 0.8 fusion.3
  91.7 0.6 copy.32
  92.3 25.0 %gather.4 = bf16[8,4,32,1024]{3,2,1,0:T(8,128)(2,1)} custom-call(bf16[32,1024]{1,0:T(8,128)(2,1)} %bitcast.67), custom_call_target="tpu_custom_call" | custom-call | tf_op jit(solution)/shard_map/gather/pallas_call | solution.py:216
  117.3 2.3 convolution_convert_fusion
  119.8 1.0 copy.31
  120.8 32.1 %collect.1 = bf16[32,4,256]{2,1,0:T(4,128)(2,1)} custom-call(bf16[8,32,4,256]{3,2,1,0:T(4,128)(2,1)} %bitcast.60), custom_call_target="tpu_custom_call" | custom-call | tf_op jit(solution)/shard_map/collect/pallas_call | solution.py:216
  152.9 0.9 convert_element_type.92
  153.7 0.2 fusion.13
  154.0 0.7 fusion.15
  154.7 7.4 %swap.2 = bf16[8,4,1024]{2,1,0:T(4,128)(2,1)} custom-call(bf16[8,4,1024]{2,1,0:T(4,128)(2,1)} %bitcast.69), custom_call_target="tpu_custom_call" | custom-call | tf_op jit(solution)/shard_map/swap/pallas_call | solution.py:216
  162.1 1.5 reshape.212.x_ref
  163.6 24.9 %gather.5 = bf16[8,4,32,1024]{3,2,1,0:T(8,128)(2,1)} custom-call(bf16[32,1024]{1,0:T(8,128)(2,1)} %reshape.212.x_ref), custom_call_target="tpu_custom_call" | custom-call | tf_op jit(solution)/shard_map/gather/pallas_call | solution.py:216
  188.5 44.1 %feed.1 = bf16[4,2,128,896]{3,2,1,0:T(8,128)(2,1)} custom-call(bf16[1024,1024]{1,0:T(8,128)(2,1)} %bitcast.56, bf16[1024,896]{1,0:T(8,128)(2,1)} %gate_ref.1, bf16[1024,896]{1,0:T(8,128)(2,1)} %up_ref.1), custom_call_target="tpu_custom_call" | custom-call | tf_op jit(solution)/shard_map/feed/pallas_call | solution.py:216
  232.6 30.5 %project.3 = f32[32,1024]{1,0:T(8,128)} custom-call(bf16[1024,896]{1,0:T(8,128)(2,1)} %bitcast.57, bf16[896,1024]{1,0:T(8,128)(2,1)} %refs_1_.3), custom_call_target="tpu_custom_call" | custom-call | tf_op jit(solution)/shard_map/project/pallas_call | solution.py:216
  263.1 0.9 convert_element_type.85
  264.0 0.7 reshape.215.x_ref
  264.7 11.2 %swap.3 = bf16[8,4,1024]{2,1,0:T(4,128)(2,1)} custom-call(bf16[8,4,1024]{2,1,0:T(4,128)(2,1)} %reshape.215.x_ref), custom_call_target="tpu_custom_call" | custom-call | tf_op jit(solution)/shard_map/swap/pallas_call | solution.py:216
  275.9 0.9 convert_element_type.93
  276.7 0.7 fusion.16
  (23 shorter events, 0.8 us)
Async XLA Ops:
  0.6 116.7 %copy-start = (bf16[1024,256]{1,0:T(8,128)(2,1)S(1)}, bf16[1024,256]{1,0:T(8,128)(2,1)}, u32[]{:S(2)}) copy-start(bf16[1024,256]{1,0:T(8,128)(2,1)} %param.15) | copy-start | bytes 1572868
  89.1 1.8 copy-start.1
  119.7 34.1 %copy-start.2 = (bf16[4,8192]{1,0:T(4,128)(2,1)S(1)}, bf16[4,8192]{1,0:T(4,128)(2,1)}, u32[]{:S(2)}) copy-start(bf16[4,8192]{1,0:T(4,128)(2,1)} %param.10) | copy-start | bytes 196612
  119.7 34.3 %copy-start.4 = (f32[8192]{0:T(1024)S(1)}, f32[8192]{0:T(1024)}, u32[]{:S(2)}) copy-start(f32[8192]{0:T(1024)} %param.16) | copy-start | bytes 98308
  153.9 122.8 %copy-start.3 = (bf16[4,8192]{1,0:T(4,128)(2,1)}, bf16[4,8192]{1,0:T(4,128)(2,1)S(1)}, u32[]{:S(2)}) copy-start(bf16[4,8192]{1,0:T(4,128)(2,1)S(1)} %get-tuple-element.3) | copy-start | bytes 196612

commit v2 on v1

v2 whole, which is shorter than its diff:
```python
import collections
import functools

import jax
import jax.numpy as jnp
from jax import lax
from jax.experimental import pallas as pl
from jax.experimental.pallas import tpu as pltpu
from jax.sharding import PartitionSpec as P

HD = 128
NZ, NY, NX = 8, 4, 4
CP, TP = NZ * NY, NX * 2
MESH = pl.DeviceIdType.MESH
F32, BF16 = jnp.float32, jnp.bfloat16

epsilon = 1e-05
rope_base = 500000.0
masked = -1e30


class Wires:
    def __init__(self, send, recv):
        self.send, self.recv, self.used, self.sent = send, recv, 0, []

    def copy(self, src, dst, device):
        i = self.used
        self.used += 1
        c = pltpu.make_async_remote_copy(
            src_ref=src,
            dst_ref=dst,
            send_sem=self.send.at[i],
            recv_sem=self.recv.at[i],
            device_id=device,
            device_id_type=MESH,
        )
        c.start()
        self.sent.append(c)
        return c

    def drain(self):
        for c in self.sent:
            c.wait_send()


class Steps:
    def __init__(self):
        self.queue = collections.deque()

    def add(self, gen):
        if next(gen, self) is not self:
            self.queue.append(gen)

    def run(self):
        while self.queue:
            self.add(self.queue.popleft())


class Place:
    def __init__(self):
        self.cp, self.tp = lax.axis_index("cp"), lax.axis_index("tp")
        self.z, self.y = self.cp // NY, self.cp % NY
        self.x, self.core = self.tp // 2, self.tp % 2

    def along_z(self, z):
        return {"cp": z * NY + self.y}

    def along_y(self, y):
        return {"cp": self.z * NY + y}

    def along_x(self, x):
        return {"tp": x * 2 + self.core}

    def partner(self):
        return {"tp": self.x * 2 + 1 - self.core}


def ring(n, me, device_of):
    return device_of((me + 1) % n), device_of((me + n - 1) % n)


def greet(devices):
    barrier = pltpu.get_barrier_semaphore()
    for device in devices:
        pl.semaphore_signal(barrier, inc=1, device_id=device, device_id_type=MESH)
    return len(devices)


def greet_group(axis, n, me):
    barrier = pltpu.get_barrier_semaphore()

    def signal(off, carry):
        pl.semaphore_signal(
            barrier, inc=1, device_id={axis: (me + off) % n}, device_id_type=MESH
        )
        return carry

    lax.fori_loop(1, n, signal, 0)
    return n - 1


def await_greetings(count):
    pl.semaphore_wait(pltpu.get_barrier_semaphore(), count)


def half_of(ref, h):
    d = ref.shape[0] // 2
    return ref.at[pl.ds(h * d, d)]


def ring_gather(wires, block, n, me, device_of, arrived=None):
    right, left = ring(n, me, device_of)
    last = n // 2 - 1

    def send(k):
        r, l = block((me + n - k) % n), block((me + k) % n)
        if k == last:
            r, l = half_of(r, 0), half_of(l, 1)
        return wires.copy(r, r, right), wires.copy(l, l, left)

    flying = send(0)
    if arrived:
        arrived(me)
    for k in range(1, n // 2 + 1):
        yield
        for c in flying:
            c.wait_recv()
        if k <= last:
            flying = send(k)
            if arrived:
                arrived((me + n - k) % n)
                arrived((me + k) % n)
        elif arrived:
            arrived((me + n // 2) % n)


def add_rows(dst, terms, finish=None):
    if len(dst.shape) == 3:
        for i in range(dst.shape[0]):
            add_rows(dst.at[i], [t.at[i] for t in terms])
        return
    rows = dst.shape[0]
    step = min(rows, 16)

    def body(i, carry):
        at = pl.ds(pl.multiple_of(i * step, step), step)
        total = terms[0][at, :].astype(F32)
        for t in terms[1:]:
            total = total + t[at, :].astype(F32)
        dst[at, :] = total.astype(dst.dtype)
        return carry

    lax.fori_loop(0, rows // step, body, 0)


def ring_scatter(wires, own, out, from_left, from_right, n, me, device_of):
    right, left = ring(n, me, device_of)
    m = n // 2
    far = own((me + m) % n)
    r = wires.copy(half_of(far, 0), half_of(from_left.at[0], 0), right)
    l = wires.copy(half_of(far, 1), half_of(from_right.at[0], 1), left)
    for k in range(1, m):
        yield
        to_right, to_left = own((me + m - k) % n), own((me + n - m + k) % n)
        got_left, got_right = from_left.at[k - 1], from_right.at[k - 1]
        r.wait_recv()
        if k == 1:
            add_rows(half_of(got_left, 0), [half_of(got_left, 0), half_of(to_right, 0)])
            add_rows(half_of(got_left, 1), [half_of(to_right, 1)])
        else:
            add_rows(got_left, [got_left, to_right])
        r = wires.copy(got_left, from_left.at[k], right)
        l.wait_recv()
        if k == 1:
            add_rows(half_of(got_right, 1), [half_of(got_right, 1), half_of(to_left, 1)])
            add_rows(half_of(got_right, 0), [half_of(to_left, 0)])
        else:
            add_rows(got_right, [got_right, to_left])
        l = wires.copy(got_right, from_right.at[k], left)
    yield
    r.wait_recv()
    l.wait_recv()
    add_rows(out, [own(me), from_left.at[m - 1], from_right.at[m - 1]])


def far_gather(wires, block, n, me, device_of, arrived):
    def to(off):
        return device_of((me + n + off) % n)

    def whole(off):
        return block((me + n + off) % n)

    def send(ref, off):
        return wires.copy(ref, ref, to(off))

    own = block(me)
    p2, m2, p1, m1 = send(own, 2), send(own, -2), send(own, 1), send(own, -1)
    arrived(me)
    yield
    p2.wait_recv()
    p3, p4 = send(whole(-2), 1), send(half_of(whole(-2), 0), 2)
    m2.wait_recv()
    m3, m4 = send(whole(2), -1), send(half_of(whole(2), 1), -2)
    p1.wait_recv()
    arrived((me + n - 1) % n)
    m1.wait_recv()
    arrived((me + 1) % n)
    arrived((me + n - 2) % n)
    arrived((me + 2) % n)
    yield
    p3.wait_recv()
    arrived((me + n - 3) % n)
    m3.wait_recv()
    arrived((me + 3) % n)
    p4.wait_recv()
    m4.wait_recv()
    arrived((me + 4) % n)


def far_scatter(wires, own, out, bufs, n, me, device_of):
    near_l, near_r, turn_l, turn_r, far_l, far_r, sum_l, sum_r = [bufs.at[i] for i in range(8)]

    def to(off):
        return device_of((me + n + off) % n)

    def term(off):
        return own((me + n + off) % n)

    opposite = term(4)
    f_l = wires.copy(half_of(opposite, 0), half_of(far_l, 0), to(2))
    f_r = wires.copy(half_of(opposite, 1), half_of(far_r, 1), to(-2))
    t_l = wires.copy(term(3), turn_l, to(1))
    t_r = wires.copy(term(-3), turn_r, to(-1))
    n_l = wires.copy(term(1), near_l, to(1))
    n_r = wires.copy(term(-1), near_r, to(-1))
    yield
    t_l.wait_recv()
    f_l.wait_recv()
    mine = term(2)
    add_rows(half_of(turn_l, 0), [half_of(r, 0) for r in (turn_l, far_l, mine)])
    add_rows(half_of(turn_l, 1), [half_of(r, 1) for r in (turn_l, mine)])
    s_l = wires.copy(turn_l, sum_l, to(2))
    t_r.wait_recv()
    f_r.wait_recv()
    mine = term(-2)
    add_rows(half_of(turn_r, 1), [half_of(r, 1) for r in (turn_r, far_r, mine)])
    add_rows(half_of(turn_r, 0), [half_of(r, 0) for r in (turn_r, mine)])
    s_r = wires.copy(turn_r, sum_r, to(-2))
    yield
    for c in (n_l, n_r, s_l, s_r):
        c.wait_recv()
    add_rows(out, [own(me), near_l, near_r, sum_l, sum_r])


def exchange(send_sem, recv_sem, source, target, axis, n, me, meanwhile=None):
    def copy(off):
        peer = (me + off) % n
        return pltpu.make_async_remote_copy(
            src_ref=source(peer),
            dst_ref=target(me),
            send_sem=send_sem.at[off],
            recv_sem=recv_sem.at[off],
            device_id={axis: peer},
            device_id_type=MESH,
        )

    def start(off, carry):
        copy(off).start()
        return carry

    def wait(off, carry):
        copy(off).wait()
        return carry

    lax.fori_loop(1, n, start, 0)
    if meanwhile:
        meanwhile()
    lax.fori_loop(1, n, wait, 0)


UNITS = 2
Z_FIRST, Y_FIRST = "z", "y"
QKV_PARTS = ((0, 256, Y_FIRST), (256, 256, Y_FIRST), (512, 384, Y_FIRST), (896, 384, Z_FIRST))
DOWN_PARTS = ((0, 384, Y_FIRST), (384, 384, Y_FIRST), (768, 256, Z_FIRST))
GATHER_SPLIT = 768


def gather_rows(wires, steps, at, out_ref, split):
    first, rest = pl.ds(0, split), pl.ds(split, out_ref.shape[-1] - split)

    def y_first():
        yield from ring_gather(
            wires, lambda j: out_ref.at[at.z, j, :, rest], NY, at.y, at.along_y
        )
        yield from far_gather(
            wires, lambda i: out_ref.at[i, :, :, rest], NZ, at.z, at.along_z, lambda i: None
        )

    def to_y(i):
        steps.add(
            ring_gather(wires, lambda j: out_ref.at[i, j, :, first], NY, at.y, at.along_y)
        )

    steps.add(y_first())
    steps.add(
        far_gather(
            wires, lambda i: out_ref.at[i, at.y, :, first], NZ, at.z, at.along_z, to_y
        )
    )


def gather_small(wires, at, ref):
    handed = []

    def to_y(i):
        block = ref.at[i, at.y]
        for off in (1, 3, 2):
            handed.append(wires.copy(block, block, at.along_y((at.y + off) % NY)))

    own = ref.at[at.z, at.y]
    order = (4, 3, 5, 2, 6, 1, 7)
    copies = {off: wires.copy(own, own, at.along_z((at.z + off) % NZ)) for off in order}
    to_y(at.z)
    yield
    for off in (1, 7, 2, 6, 3, 5, 4):
        copies[off].wait_recv()
        to_y((at.z + NZ - off) % NZ)
    yield
    for c in handed:
        c.wait_recv()


def scatter_part(wires, at, part, out, columns, way, bufs):
    if way == Z_FIRST:
        z_bufs, y_left, y_right, y_sum = bufs
        yield from far_scatter(
            wires, lambda i: part.at[i, :, :, columns], y_sum, z_bufs, NZ, at.z, at.along_z
        )
        yield from ring_scatter(
            wires,
            lambda j: y_sum.at[j],
            out.at[:, columns],
            y_left,
            y_right,
            NY,
            at.y,
            at.along_y,
        )
    else:
        z_bufs, y_left, y_right, z_sum = bufs
        yield from ring_scatter(
            wires,
            lambda j: part.at[:, j, :, columns],
            z_sum,
            y_left,
            y_right,
            NY,
            at.y,
            at.along_y,
        )
        yield from far_scatter(
            wires, lambda i: z_sum.at[i], out.at[:, columns], z_bufs, NZ, at.z, at.along_z
        )


def scatter_scratch(prefix, parts, rows):
    scratch = {}
    for n, (_, width, way) in enumerate(parts):
        if way == Z_FIRST:
            shapes = (
                (NZ, NY, rows, width),
                (NY // 2, rows, width),
                (NY // 2, rows, width),
                (NY, rows, width),
            )
        else:
            shapes = (
                (NZ, rows, width),
                (NY // 2, NZ, rows, width),
                (NY // 2, NZ, rows, width),
                (NZ, rows, width),
            )
        for m, shape in enumerate(shapes):
            scratch[f"{prefix}{n}{m}"] = pltpu.VMEM(shape, BF16)
    return scratch


def product_into(part, x, w_ref, start):
    width = w_ref.shape[1]
    tile = min(width, 256)

    def body(i, carry):
        at = pl.multiple_of(i * tile, tile)
        p = jnp.dot(x(), w_ref[:, pl.ds(at, tile)], preferred_element_type=F32)
        part[:, :, :, pl.ds(pl.multiple_of(start + at, 128), tile)] = p.astype(BF16).reshape(
            *part.shape[:3], tile
        )
        return carry

    lax.fori_loop(0, width // tile, body, 0)


def feed(wires, steps, at, stream, gate_ref, up_ref, out_ref, part, held, fl, fr, total):
    partner = at.partner()
    units = gate_ref.shape[1]
    block = part.shape[2]
    rows = block // UNITS
    other = 1 - at.core
    zs = NZ // NX

    def product(i):
        def tile(w_ref, col, width, start):
            x = stream[pl.ds(i * zs, zs)].reshape(2 * block, -1)
            p = jnp.dot(x, w_ref[:, pl.ds(col, width)], preferred_element_type=F32)
            part[i, :, :, pl.ds(start + col, width)] = p.astype(BF16).reshape(2, block, width)

        def body(t, carry):
            col = pl.multiple_of(t * 256, 256)
            tile(gate_ref, col, 256, 0)
            tile(up_ref, col, 256, units)
            return carry

        lax.fori_loop(0, units // 256, body, 0)
        if units % 256:
            tile(gate_ref, units // 256 * 256, units % 256, 0)
            tile(up_ref, units // 256 * 256, units % 256, units)
        return wires.copy(part.at[i, other], held.at[i], partner)

    def combine(i, c):
        c.wait_recv()
        add_rows(held.at[i], [held.at[i], part.at[i, at.core]])

    def line(u):
        at_rows = pl.ds(u * rows, rows)
        yield from ring_scatter(
            wires,
            lambda i: held.at[i, at_rows],
            total.at[u],
            fl.at[u],
            fr.at[u],
            NX,
            at.x,
            at.along_x,
        )

        def body(i, carry):
            r = pl.ds(pl.multiple_of(i * 16, 16), 16)
            gate, up = total[u, r, pl.ds(0, units)], total[u, r, pl.ds(units, units)]
            out_ref[at.x, at.core, pl.ds(pl.multiple_of(u * rows + i * 16, 16), 16), :] = (
                jax.nn.silu(gate) * up
            ).astype(BF16)
            return carry

        lax.fori_loop(0, rows // 16, body, 0)

        def hand_over(i):
            ref = out_ref.at[i, at.core, at_rows]
            handed.append(wires.copy(ref, ref, partner))

        yield from ring_gather(
            wires, lambda i: out_ref.at[i, at.core, at_rows], NX, at.x, at.along_x, hand_over
        )

    handed = []
    order = [(at.x + 2) % NX, (at.x + 1) % NX, (at.x + 3) % NX, at.x]
    copies = [product(order[0])]
    copies.append(product(order[1]))
    combine(order[0], copies[0])
    for u in range(UNITS):
        steps.add(line(u))
    copies.append(product(order[2]))
    combine(order[1], copies[1])
    copies.append(product(order[3]))
    combine(order[2], copies[2])
    combine(order[3], copies[3])
    steps.run()
    for c in handed:
        c.wait_recv()


def normalize(values, gain):
    mean_square = jnp.mean(values * values, axis=-1, keepdims=True)
    return (values * lax.rsqrt(mean_square + epsilon) * gain).astype(BF16)


WEIGHTS = ("key", "value", "query", "out", "gate", "up", "down")


def layer_kernel(names, *refs):
    r = dict(zip(names, refs))
    at = Place()
    wires, steps = Wires(r["send"], r["recv"]), Steps()
    tokens, attended, mixed = r["tokens"], r["attended"], r["mixed"]
    local_rows, model = tokens.shape
    cos, sin = r["cos"], r["sin"]

    greeted = greet_group("cp", CP, at.cp) + greet_group("tp", TP, at.tp)
    loads = {}
    for n, name in enumerate(WEIGHTS):
        loads[name] = pltpu.make_async_copy(
            r[name + "_weight"], r[name], r["load"].at[n]
        )
        loads[name].start()

    normed = normalize(tokens[...].astype(F32), r["attention_gain"][...])
    slices, got, columns = r["slices"], r["got"], r["columns"]
    width = slices.shape[-1]
    for c in range(CP):
        slices[c] = normed[:, c * width : (c + 1) * width]
    await_greetings(greeted)

    def keep_slice():
        got[at.cp] = slices[at.cp]

    exchange(
        r["s0"], r["r0"], lambda p: slices.at[p], lambda p: got.at[p], "cp", CP, at.cp, keep_slice
    )

    def keep_columns():
        columns[at.tp] = got[...]

    exchange(
        r["s1"], r["r1"], lambda p: got, lambda p: columns.at[p], "tp", TP, at.tp, keep_columns
    )
    rows_in = r["rows_in"]

    def in_order(b, carry):
        parts = [columns[t, b].astype(F32) for t in range(TP)]
        rows_in[b] = jnp.concatenate(parts, axis=0).astype(BF16)
        return carry

    lax.fori_loop(0, CP, in_order, 0)

    part, summed, shared = r["qkv_part"], r["summed"], r["shared"]

    def x():
        return rows_in[...].reshape(-1, width)

    def turned(v):
        return (v * cos[...] + pltpu.roll(v, HD // 2, 1) * sin[...]).astype(BF16)

    def unit(n, out, parts, partial, prefix):
        start, extent, way = parts[n]
        bufs = [r[f"{prefix}{n}{m}"] for m in range(4)]
        return scatter_part(wires, at, partial, out, pl.ds(start, extent), way, bufs)

    def keys_and_values():
        yield from unit(0, summed, QKV_PARTS, part, "q")
        shared[at.z, at.y, :, pl.ds(0, HD)] = turned(summed[:, pl.ds(0, HD)])
        shared[at.z, at.y, :, pl.ds(HD, HD)] = summed[:, pl.ds(HD, HD)].astype(BF16)
        yield from gather_small(wires, at, shared)

    loads["key"].wait()
    loads["value"].wait()
    product_into(part, x, r["key"], 0)
    product_into(part, x, r["value"], HD)
    steps.add(keys_and_values())
    loads["query"].wait()
    product_into(part, x, r["query"], 2 * HD)
    for n in range(1, len(QKV_PARTS)):
        steps.add(unit(n, summed, QKV_PARTS, part, "q"))
    steps.run()

    every = r["every"]
    heads = (summed.shape[1] - 2 * HD) // HD
    block = summed.shape[0]
    query = jnp.concatenate(
        [turned(summed[:, (2 + h) * HD : (3 + h) * HD]) for h in range(heads)], axis=0
    )
    keys = shared[:, :, :, 0:HD].reshape(-1, HD)
    values = shared[:, :, :, HD : 2 * HD].reshape(-1, HD)
    scores = lax.dot_general(
        query, keys, (((1,), (1,)), ((), ())), preferred_element_type=F32
    ) * HD ** (-0.5)
    key_at = lax.broadcasted_iota(jnp.int32, scores.shape, 1)
    query_at = lax.broadcasted_iota(jnp.int32, scores.shape, 0) % block + at.cp * block
    allowed = key_at <= query_at
    scores = jnp.where(allowed, scores, masked)
    top = jnp.max(scores, axis=-1, keepdims=True)
    weights = jnp.where(allowed, jnp.exp(scores - top), 0.0)
    total = jnp.sum(weights, axis=-1, keepdims=True)
    mean = jnp.dot(weights.astype(BF16), values, preferred_element_type=F32) / total
    mean = mean.astype(BF16)
    for h in range(heads):
        every[at.z, at.y, :, h * HD : (h + 1) * HD] = mean[h * block : (h + 1) * block]

    gather_rows(wires, steps, at, every, GATHER_SPLIT)
    steps.run()

    out_part, out_got, out_total, projected = (
        r["out_part"],
        r["out_got"],
        r["out_total"],
        r["projected"],
    )
    loads["out"].wait()

    def out_rows(i, carry):
        p = jnp.dot(
            every[pl.ds(i * 2, 2)].reshape(2 * NY * block, -1),
            r["out"][...],
            preferred_element_type=F32,
        )
        for b in range(2 * NY):
            for t in range(TP):
                first = b * block + t * local_rows
                out_part[t, i * 2 * NY + b] = p[first : first + local_rows].astype(BF16)
        return carry

    lax.fori_loop(0, NZ // 2, out_rows, 0)

    def keep_part():
        out_got[at.tp] = out_part[at.tp]

    exchange(
        r["s2"],
        r["r2"],
        lambda p: out_part.at[p],
        lambda p: out_got.at[p],
        "tp",
        TP,
        at.tp,
        keep_part,
    )

    def sum_part(i, carry):
        parts = out_got[0, i].astype(F32)
        for t in range(1, TP):
            parts = parts + out_got[t, i].astype(F32)
        out_total[i] = parts.astype(BF16)
        return carry

    lax.fori_loop(0, CP, sum_part, 0)

    def keep_total():
        projected[at.cp] = out_total[at.cp]

    exchange(
        r["s3"],
        r["r3"],
        lambda p: out_total.at[p],
        lambda p: projected.at[p],
        "cp",
        CP,
        at.cp,
        keep_total,
    )
    for c in range(CP):
        cols = slice(c * width, (c + 1) * width)
        attended[:, cols] = (tokens[:, cols].astype(F32) + projected[c].astype(F32)).astype(BF16)

    normed = normalize(attended[...].astype(F32), r["feed_gain"][...])
    by_width, got_width, stream = r["by_width"], r["got_width"], r["stream"]
    wide = by_width.shape[-1]
    for t in range(TP):
        by_width[t] = normed[:, t * wide : (t + 1) * wide]

    def keep_width():
        got_width[at.tp] = by_width[at.tp]

    exchange(
        r["s4"],
        r["r4"],
        lambda p: by_width.at[p],
        lambda p: got_width.at[p],
        "tp",
        TP,
        at.tp,
        keep_width,
    )
    stream[at.z, at.y] = jnp.concatenate(
        [got_width[t].astype(F32) for t in range(TP)], axis=0
    ).astype(BF16)
    gather_rows(wires, steps, at, stream, GATHER_SPLIT)
    steps.run()

    loads["gate"].wait()
    loads["up"].wait()
    hidden = r["hidden"]
    feed(
        wires,
        steps,
        at,
        stream,
        r["gate"],
        r["up"],
        hidden,
        r["unit_part"],
        r["held"],
        r["from_left"],
        r["from_right"],
        r["unit_total"],
    )

    down_part, reduced = r["down_part"], r["reduced"]
    loads["down"].wait()
    product_into(down_part, lambda: hidden[...].reshape(-1, hidden.shape[-1]), r["down"], 0)
    for n in range(len(DOWN_PARTS)):
        steps.add(unit(n, reduced, DOWN_PARTS, down_part, "d"))
    steps.run()
    by_token, lowered = r["by_token"], r["lowered"]
    for t in range(TP):
        by_token[t] = reduced[pl.ds(t * local_rows, local_rows), :].astype(BF16)

    def keep_token():
        lowered[at.tp] = by_token[at.tp]

    exchange(
        r["s5"],
        r["r5"],
        lambda p: by_token.at[p],
        lambda p: lowered.at[p],
        "tp",
        TP,
        at.tp,
        keep_token,
    )
    for t in range(TP):
        cols = slice(t * wide, (t + 1) * wide)
        mixed[:, cols] = (attended[:, cols].astype(F32) + lowered[t].astype(F32)).astype(BF16)
    wires.drain()


VMEM = pl.BlockSpec(memory_space=pltpu.VMEM)
ANY = pl.BlockSpec(memory_space=pl.ANY)
COPIES = 320


def dma(count):
    return pltpu.SemaphoreType.DMA((count,))


def on_device(
    tokens,
    attention_gain,
    query_weight,
    key_weight,
    value_weight,
    out_weight,
    feed_gain,
    gate_weight,
    up_weight,
    down_weight,
):
    local_rows, model = tokens.shape
    block = local_rows * TP
    rows = block * CP
    qkv = query_weight.shape[1] + key_weight.shape[1] + value_weight.shape[1]
    units = gate_weight.shape[1]
    wide, width = model // TP, model // CP

    inverse = rope_base ** (-(jnp.arange(HD // 2, dtype=F32) * 2.0 / HD))
    positions = lax.axis_index("cp") * block + jnp.arange(block, dtype=jnp.int32)
    angles = positions.astype(F32)[:, None] * inverse[None, :]
    cosine, sine = jnp.cos(angles), jnp.sin(angles)

    inputs = {
        "tokens": tokens,
        "attention_gain": attention_gain[None],
        "feed_gain": feed_gain[None],
        "cos": jnp.concatenate([cosine, cosine], axis=1),
        "sin": jnp.concatenate([-sine, sine], axis=1),
        "key_weight": key_weight,
        "value_weight": value_weight,
        "query_weight": query_weight,
        "out_weight": out_weight,
        "gate_weight": gate_weight,
        "up_weight": up_weight,
        "down_weight": down_weight,
    }

    def buf(*shape, kind=BF16):
        return pltpu.VMEM(shape, kind)

    scratch = {name: buf(*inputs[name + "_weight"].shape) for name in WEIGHTS}
    scratch |= {
        "slices": buf(CP, local_rows, width),
        "got": buf(CP, local_rows, width),
        "columns": buf(TP, CP, local_rows, width),
        "rows_in": buf(CP, block, width),
        "qkv_part": buf(NZ, NY, block, qkv),
        "summed": buf(block, qkv, kind=F32),
        "shared": buf(NZ, NY, block, 2 * HD),
        "every": buf(NZ, NY, block, wide),
        "out_part": buf(TP, CP, local_rows, width),
        "out_got": buf(TP, CP, local_rows, width),
        "out_total": buf(CP, local_rows, width),
        "projected": buf(CP, local_rows, width),
        "by_width": buf(TP, local_rows, wide),
        "got_width": buf(TP, local_rows, wide),
        "stream": buf(NZ, NY, block, wide),
        "unit_part": buf(NX, 2, rows // TP, 2 * units),
        "held": buf(NX, rows // TP, 2 * units),
        "from_left": buf(UNITS, NX // 2, rows // TP // UNITS, 2 * units),
        "from_right": buf(UNITS, NX // 2, rows // TP // UNITS, 2 * units),
        "unit_total": buf(UNITS, rows // TP // UNITS, 2 * units, kind=F32),
        "hidden": buf(NX, 2, rows // TP, units),
        "down_part": buf(NZ, NY, block, wide),
        "reduced": buf(block, wide, kind=F32),
        "by_token": buf(TP, local_rows, wide),
        "lowered": buf(TP, local_rows, wide),
    }
    scratch |= scatter_scratch("q", QKV_PARTS, block)
    scratch |= scatter_scratch("d", DOWN_PARTS, block)
    for n, count in enumerate((CP, TP, TP, CP, TP, TP)):
        scratch |= {f"s{n}": dma(count), f"r{n}": dma(count)}
    scratch |= {"load": dma(len(WEIGHTS)), "send": dma(COPIES), "recv": dma(COPIES)}

    names = (*inputs, "attended", "mixed", *scratch)
    shape = jax.ShapeDtypeStruct(tokens.shape, BF16)
    return pl.pallas_call(
        functools.partial(layer_kernel, names),
        out_shape=(shape, shape),
        in_specs=[ANY if name.endswith("_weight") else VMEM for name in inputs],
        out_specs=(VMEM, VMEM),
        scratch_shapes=list(scratch.values()),
        compiler_params=pltpu.CompilerParams(
            collective_id=0,
            has_side_effects=True,
            vmem_limit_bytes=60 * 1024 * 1024,
        ),
        name="layer",
    )(*inputs.values())


def solution(mesh):
    in_specs = (
        P(("cp", "tp"), None),
        P(),
        P("cp", "tp"),
        P("cp", "tp"),
        P("cp", "tp"),
        P("tp", "cp"),
        P(),
        P("tp", "cp"),
        P("tp", "cp"),
        P("cp", "tp"),
    )
    out_specs = (P(("cp", "tp"), None), P(("cp", "tp"), None))
    return jax.shard_map(
        on_device, mesh=mesh, in_specs=in_specs, out_specs=out_specs, check_vma=False
    )
```

time: 278 us -> 194 us (0.70)
  Pallas kernels: 255 us -> 189 us
  other arithmetic: 8.33 us -> 0.85 us
  local copies, waits for them, and re-layouts: 8.65 us -> 2.98 us
  matrix products: 4.52 us -> 0 us
    pallas_call x10 -> x1, Pallas kernels: 255 us -> 189 us  [on_device(): pl.pallas_call(functools.partial(layer_kernel, names), out_shape=(shape,...]
    convert_element_type x7 -> x1, other arithmetic: 5.66 us -> 0.01 us  [on_device(): angles = positions.astype(F32)[:, None] * inverse[None, :]]
    reshape x6 -> x0, local copies, waits for them, and re-layouts: 4.9 us -> none  [the longest x1 1.49 us: on_device(): block = swap(by_width, 5).reshape(block_rows, -1)]
    dot_general x3 -> x0, matrix products: 4.52 us -> none  [the longest x1 2.3 us: on_device(): jnp.dot(everywhere, out_weight, preferred_element_type=F32).astype(BF16)]
where the time goes in v2:
time: 194 us
  Pallas kernels  189 us (97%)
  local copies, waits for them, and re-layouts  2.98 us (2%)
    pallas_call x1, Pallas kernels, on_device(): pl.pallas_call(functools.partial(layer_kernel, names), out_shape=(shape,...  189 us

profile of v2, /device:TPU:1, one launch (start us, length us, event | category | flops | bytes accessed | tf_op | source)
XLA Modules:
  0.0 193.8 jit_solution(12426421602243473654)
XLA Ops:
  0.7 0.1 fusion
  0.8 0.7 pad_maximum_fusion
  1.5 189.3 %layer.1 = (bf16[4,8192]{1,0:T(4,128)(2,1)}, bf16[4,8192]{1,0:T(4,128)(2,1)}) custom-call(bf16[4,8192]{1,0:T(4,128)(2,1)} %refs_0_.1, f32[1,8192]{1,0:T(1,128)} %bitcast.2, f32[1,8192]{1,0:T(1,128)} %bitcast.3, f32[32,128]{1,0:T(8,128)} %get-tuple-element.5.refs_3_, f32[32,128]{1,0:T(8,128)} %get-tuple-element.6.refs_4_, bf16[256,128]{1,0:T(8,128)(2,1)} %refs_5_.1, ...), custom_call_target="tpu_custom_call" | custom-call | tf_op jit(solution)/shard_map/layer/pallas_call | solution.py:811
  190.8 1.5 copy.14
  192.3 1.5 copy.15
  (2 shorter events, 0.0 us)

commit v3 on v2

--- a/solution.py
+++ b/solution.py
@@ -26,6 +26,7 @@
     def copy(self, src, dst, device):
         i = self.used
         self.used += 1
+        assert i < self.send.shape[0]
         c = pltpu.make_async_remote_copy(
             src_ref=src,
             dst_ref=dst,
@@ -41,19 +42,34 @@
     def drain(self):
         for c in self.sent:
             c.wait_send()
+        self.sent, self.used = [], 0
 
 
 class Steps:
     def __init__(self):
         self.queue = collections.deque()
 
-    def add(self, gen):
-        if next(gen, self) is not self:
-            self.queue.append(gen)
+    def add(self, gen, name="line", step=0):
+        with jax.named_scope(f"{name}_{step}"):
+            going = next(gen, self) is not self
+        if going:
+            self.queue.append((gen, name, step + 1))
 
     def run(self):
         while self.queue:
-            self.add(self.queue.popleft())
+            self.add(*self.queue.popleft())
+
+
+class Phases:
+    def __init__(self):
+        self.scope = None
+
+    def __call__(self, name):
+        if self.scope:
+            self.scope.__exit__(None, None, None)
+        self.scope = jax.named_scope(name) if name else None
+        if self.scope:
+            self.scope.__enter__()
 
 
 class Place:
@@ -195,26 +211,26 @@
 
     own = block(me)
     p2, m2, p1, m1 = send(own, 2), send(own, -2), send(own, 1), send(own, -1)
-    arrived(me)
+    arrived(0)
     yield
     p2.wait_recv()
     p3, p4 = send(whole(-2), 1), send(half_of(whole(-2), 0), 2)
     m2.wait_recv()
     m3, m4 = send(whole(2), -1), send(half_of(whole(2), 1), -2)
     p1.wait_recv()
-    arrived((me + n - 1) % n)
+    arrived(7)
     m1.wait_recv()
-    arrived((me + 1) % n)
-    arrived((me + n - 2) % n)
-    arrived((me + 2) % n)
+    arrived(1)
+    arrived(6)
+    arrived(2)
     yield
     p3.wait_recv()
-    arrived((me + n - 3) % n)
+    arrived(5)
     m3.wait_recv()
-    arrived((me + 3) % n)
+    arrived(3)
     p4.wait_recv()
     m4.wait_recv()
-    arrived((me + 4) % n)
+    arrived(4)
 
 
 def far_scatter(wires, own, out, bufs, n, me, device_of):
@@ -278,34 +294,50 @@
     lax.fori_loop(1, n, wait, 0)
 
 
-UNITS = 2
 Z_FIRST, Y_FIRST = "z", "y"
 QKV_PARTS = ((0, 256, Y_FIRST), (256, 256, Y_FIRST), (512, 384, Y_FIRST), (896, 384, Z_FIRST))
-DOWN_PARTS = ((0, 384, Y_FIRST), (384, 384, Y_FIRST), (768, 256, Z_FIRST))
 GATHER_SPLIT = 768
 
 
-def gather_rows(wires, steps, at, out_ref, split):
+CHUNKS = ((0, 7), (1, 6), (2, 5), (3, 4))
+
+
+def gather_rows(wires, steps, at, out_ref, split, ready):
     first, rest = pl.ds(0, split), pl.ds(split, out_ref.shape[-1] - split)
+    seen = collections.Counter()
+
+    def z_at(off):
+        return (at.z + off) % NZ
+
+    def mark(off):
+        seen[off] += 1
+        for c, chunk in enumerate(CHUNKS):
+            if off in chunk and all(seen[o] == 2 for o in chunk):
+                steps.add(ready(c), f"chunk{c}")
 
     def y_first():
         yield from ring_gather(
             wires, lambda j: out_ref.at[at.z, j, :, rest], NY, at.y, at.along_y
         )
         yield from far_gather(
-            wires, lambda i: out_ref.at[i, :, :, rest], NZ, at.z, at.along_z, lambda i: None
-        )
-
-    def to_y(i):
-        steps.add(
-            ring_gather(wires, lambda j: out_ref.at[i, j, :, first], NY, at.y, at.along_y)
-        )
-
-    steps.add(y_first())
+            wires, lambda i: out_ref.at[i, :, :, rest], NZ, at.z, at.along_z, mark
+        )
+
+    def to_y(off):
+        def line():
+            yield from ring_gather(
+                wires, lambda j: out_ref.at[z_at(off), j, :, first], NY, at.y, at.along_y
+            )
+            mark(off)
+
+        steps.add(line(), f"y{off}")
+
+    steps.add(y_first(), "yz")
     steps.add(
         far_gather(
             wires, lambda i: out_ref.at[i, at.y, :, first], NZ, at.z, at.along_z, to_y
-        )
+        ),
+        "z",
     )
 
 
@@ -400,82 +432,136 @@
     lax.fori_loop(0, width // tile, body, 0)
 
 
-def feed(wires, steps, at, stream, gate_ref, up_ref, out_ref, part, held, fl, fr, total):
+def chunk_rows(ref, at, c):
+    blocks = [ref[(at.z + off) % NZ] for off in CHUNKS[c]]
+    return jnp.concatenate([b.reshape(-1, b.shape[-1]) for b in blocks], axis=0)
+
+
+def feed_chunk(wires, at, r, c, finished):
     partner = at.partner()
-    units = gate_ref.shape[1]
-    block = part.shape[2]
-    rows = block // UNITS
-    other = 1 - at.core
-    zs = NZ // NX
-
-    def product(i):
-        def tile(w_ref, col, width, start):
-            x = stream[pl.ds(i * zs, zs)].reshape(2 * block, -1)
-            p = jnp.dot(x, w_ref[:, pl.ds(col, width)], preferred_element_type=F32)
-            part[i, :, :, pl.ds(start + col, width)] = p.astype(BF16).reshape(2, block, width)
-
-        def body(t, carry):
-            col = pl.multiple_of(t * 256, 256)
-            tile(gate_ref, col, 256, 0)
-            tile(up_ref, col, 256, units)
-            return carry
-
-        lax.fori_loop(0, units // 256, body, 0)
-        if units % 256:
-            tile(gate_ref, units // 256 * 256, units % 256, 0)
-            tile(up_ref, units // 256 * 256, units % 256, units)
-        return wires.copy(part.at[i, other], held.at[i], partner)
-
-    def combine(i, c):
-        c.wait_recv()
-        add_rows(held.at[i], [held.at[i], part.at[i, at.core]])
-
-    def line(u):
-        at_rows = pl.ds(u * rows, rows)
-        yield from ring_scatter(
-            wires,
-            lambda i: held.at[i, at_rows],
-            total.at[u],
-            fl.at[u],
-            fr.at[u],
-            NX,
-            at.x,
-            at.along_x,
-        )
-
-        def body(i, carry):
-            r = pl.ds(pl.multiple_of(i * 16, 16), 16)
-            gate, up = total[u, r, pl.ds(0, units)], total[u, r, pl.ds(units, units)]
-            out_ref[at.x, at.core, pl.ds(pl.multiple_of(u * rows + i * 16, 16), 16), :] = (
-                jax.nn.silu(gate) * up
-            ).astype(BF16)
-            return carry
-
-        lax.fori_loop(0, rows // 16, body, 0)
-
-        def hand_over(i):
-            ref = out_ref.at[i, at.core, at_rows]
-            handed.append(wires.copy(ref, ref, partner))
-
-        yield from ring_gather(
-            wires, lambda i: out_ref.at[i, at.core, at_rows], NX, at.x, at.along_x, hand_over
-        )
-
+    units = r["gate"].shape[1]
+    part, held, total, hidden = (
+        r["unit_part"].at[c],
+        r["held"].at[c],
+        r["unit_total"].at[c],
+        r["hidden"].at[c],
+    )
+    rows = total.shape[0]
+
+    def tile(w_ref, col, width, start):
+        p = jnp.dot(
+            chunk_rows(r["stream"], at, c), w_ref[:, pl.ds(col, width)], preferred_element_type=F32
+        )
+        part[:, :, :, pl.ds(start + col, width)] = p.astype(BF16).reshape(2, NY, rows, width)
+
+    def body(t, carry):
+        col = pl.multiple_of(t * 256, 256)
+        tile(r["gate"], col, 256, 0)
+        tile(r["up"], col, 256, units)
+        return carry
+
+    lax.fori_loop(0, units // 256, body, 0)
+    if units % 256:
+        tile(r["gate"], units // 256 * 256, units % 256, 0)
+        tile(r["up"], units // 256 * 256, units % 256, units)
+    copy = wires.copy(part.at[1 - at.core], held, partner)
+    yield
+    copy.wait_recv()
+    add_rows(held, [held, part.at[at.core]])
+    yield from ring_scatter(
+        wires,
+        lambda i: held.at[i],
+        total,
+        r["from_left"].at[c],
+        r["from_right"].at[c],
+        NX,
+        at.x,
+        at.along_x,
+    )
+
+    def activate(i, carry):
+        here = pl.ds(pl.multiple_of(i * 16, 16), 16)
+        gate, up = total[here, pl.ds(0, units)], total[here, pl.ds(units, units)]
+        hidden[at.core, at.x, here, :] = (jax.nn.silu(gate) * up).astype(BF16)
+        return carry
+
+    lax.fori_loop(0, rows // 16, activate, 0)
     handed = []
-    order = [(at.x + 2) % NX, (at.x + 1) % NX, (at.x + 3) % NX, at.x]
-    copies = [product(order[0])]
-    copies.append(product(order[1]))
-    combine(order[0], copies[0])
-    for u in range(UNITS):
-        steps.add(line(u))
-    copies.append(product(order[2]))
-    combine(order[1], copies[1])
-    copies.append(product(order[3]))
-    combine(order[2], copies[2])
-    combine(order[3], copies[3])
-    steps.run()
-    for c in handed:
-        c.wait_recv()
+
+    def hand_over(i):
+        ref = hidden.at[at.core, i]
+        handed.append(wires.copy(ref, ref, partner))
+
+    yield from ring_gather(
+        wires, lambda i: hidden.at[at.core, i], NX, at.x, at.along_x, hand_over
+    )
+    yield
+    for copy in handed:
+        copy.wait_recv()
+    down_part = r["down_part"].at[c]
+
+    def down(i, carry):
+        cols = pl.ds(pl.multiple_of(i * 256, 256), 256)
+        p = jnp.dot(
+            hidden[...].reshape(2 * NX * rows, units), r["down"][:, cols], preferred_element_type=F32
+        )
+        down_part[:, :, :, cols] = p.astype(BF16).reshape(2, NY, rows, 256)
+        return carry
+
+    lax.fori_loop(0, down_part.shape[-1] // 256, down, 0)
+    yield from ring_scatter(
+        wires,
+        lambda j: down_part.at[:, j],
+        r["down_sum"].at[c],
+        r["down_left"].at[c],
+        r["down_right"].at[c],
+        NY,
+        at.y,
+        at.along_y,
+    )
+    finished(c)
+
+
+def far_scatter_parts(wires, steps, own, out, bufs, device_of):
+    near_l, near_r, turn_l, turn_r, far_l, far_r, sum_l, sum_r = [bufs.at[i] for i in range(8)]
+    sent = {}
+
+    def last_round():
+        yield
+        for side, off, turn, far, into in (
+            ("l", 2, turn_l, far_l, sum_l),
+            ("r", 6, turn_r, far_r, sum_r),
+        ):
+            full, other = (0, 1) if side == "l" else (1, 0)
+            sent["t" + side].wait_recv()
+            sent["f" + side].wait_recv()
+            mine = own(off)
+            add_rows(half_of(turn, full), [half_of(x, full) for x in (turn, far, mine)])
+            add_rows(half_of(turn, other), [half_of(x, other) for x in (turn, mine)])
+            sent["s" + side] = wires.copy(turn, into, device_of(off))
+        yield
+        for name in ("nl", "nr", "sl", "sr"):
+            sent[name].wait_recv()
+        add_rows(out, [own(0), near_l, near_r, sum_l, sum_r])
+
+    def finished(c):
+        for off in CHUNKS[c]:
+            term = own(off)
+            if off == 1:
+                sent["nl"] = wires.copy(term, near_l, device_of(1))
+            elif off == 7:
+                sent["nr"] = wires.copy(term, near_r, device_of(7))
+            elif off == 3:
+                sent["tl"] = wires.copy(term, turn_l, device_of(1))
+            elif off == 5:
+                sent["tr"] = wires.copy(term, turn_r, device_of(7))
+            elif off == 4:
+                sent["fl"] = wires.copy(half_of(term, 0), half_of(far_l, 0), device_of(2))
+                sent["fr"] = wires.copy(half_of(term, 1), half_of(far_r, 1), device_of(6))
+        if c == len(CHUNKS) - 1:
+            steps.add(last_round(), "last")
+
+    return finished
 
 
 def normalize(values, gain):
@@ -489,11 +575,14 @@
 def layer_kernel(names, *refs):
     r = dict(zip(names, refs))
     at = Place()
-    wires, steps = Wires(r["send"], r["recv"]), Steps()
+    qkv_wires, wires, steps = Wires(r["send"], r["recv"]), Wires(r["send_2"], r["recv_2"]), Steps()
+    out_wires = wires
     tokens, attended, mixed = r["tokens"], r["attended"], r["mixed"]
     local_rows, model = tokens.shape
     cos, sin = r["cos"], r["sin"]
 
+    phase = Phases()
+    phase("greet")
     greeted = greet_group("cp", CP, at.cp) + greet_group("tp", TP, at.tp)
     loads = {}
     for n, name in enumerate(WEIGHTS):
@@ -507,8 +596,10 @@
     width = slices.shape[-1]
     for c in range(CP):
         slices[c] = normed[:, c * width : (c + 1) * width]
+    phase("barrier")
     await_greetings(greeted)
 
+    phase("spread_cp")
     def keep_slice():
         got[at.cp] = slices[at.cp]
 
@@ -516,12 +607,14 @@
         r["s0"], r["r0"], lambda p: slices.at[p], lambda p: got.at[p], "cp", CP, at.cp, keep_slice
     )
 
+    phase("spread_tp")
     def keep_columns():
         columns[at.tp] = got[...]
 
     exchange(
         r["s1"], r["r1"], lambda p: got, lambda p: columns.at[p], "tp", TP, at.tp, keep_columns
     )
+    phase("relayout")
     rows_in = r["rows_in"]
 
     def in_order(b, carry):
@@ -542,25 +635,29 @@
     def unit(n, out, parts, partial, prefix):
         start, extent, way = parts[n]
         bufs = [r[f"{prefix}{n}{m}"] for m in range(4)]
-        return scatter_part(wires, at, partial, out, pl.ds(start, extent), way, bufs)
+        return scatter_part(qkv_wires, at, partial, out, pl.ds(start, extent), way, bufs)
 
     def keys_and_values():
         yield from unit(0, summed, QKV_PARTS, part, "q")
         shared[at.z, at.y, :, pl.ds(0, HD)] = turned(summed[:, pl.ds(0, HD)])
         shared[at.z, at.y, :, pl.ds(HD, HD)] = summed[:, pl.ds(HD, HD)].astype(BF16)
-        yield from gather_small(wires, at, shared)
-
+        yield from gather_small(qkv_wires, at, shared)
+
+    phase("qkv")
     loads["key"].wait()
     loads["value"].wait()
     product_into(part, x, r["key"], 0)
     product_into(part, x, r["value"], HD)
-    steps.add(keys_and_values())
+    steps.add(keys_and_values(), "kv")
     loads["query"].wait()
     product_into(part, x, r["query"], 2 * HD)
+    phase("qkv_sum")
     for n in range(1, len(QKV_PARTS)):
-        steps.add(unit(n, summed, QKV_PARTS, part, "q"))
+        steps.add(unit(n, summed, QKV_PARTS, part, "q"), f"q{n}")
     steps.run()
-
+    qkv_wires.drain()
+
+    phase("attend")
     every = r["every"]
     heads = (summed.shape[1] - 2 * HD) // HD
     block = summed.shape[0]
@@ -584,9 +681,7 @@
     for h in range(heads):
         every[at.z, at.y, :, h * HD : (h + 1) * HD] = mean[h * block : (h + 1) * block]
 
-    gather_rows(wires, steps, at, every, GATHER_SPLIT)
-    steps.run()
-
+    phase("gather_att")
     out_part, out_got, out_total, projected = (
         r["out_part"],
         r["out_got"],
@@ -594,57 +689,48 @@
         r["projected"],
     )
     loads["out"].wait()
-
-    def out_rows(i, carry):
-        p = jnp.dot(
-            every[pl.ds(i * 2, 2)].reshape(2 * NY * block, -1),
-            r["out"][...],
-            preferred_element_type=F32,
-        )
-        for b in range(2 * NY):
+    owners = []
+
+    def out_chunk(c):
+        p = jnp.dot(chunk_rows(every, at, c), r["out"][...], preferred_element_type=F32)
+        blocks = 2 * NY
+        for b in range(blocks):
             for t in range(TP):
                 first = b * block + t * local_rows
-                out_part[t, i * 2 * NY + b] = p[first : first + local_rows].astype(BF16)
-        return carry
-
-    lax.fori_loop(0, NZ // 2, out_rows, 0)
-
-    def keep_part():
-        out_got[at.tp] = out_part[at.tp]
-
-    exchange(
-        r["s2"],
-        r["r2"],
-        lambda p: out_part.at[p],
-        lambda p: out_got.at[p],
-        "tp",
-        TP,
-        at.tp,
-        keep_part,
-    )
-
-    def sum_part(i, carry):
-        parts = out_got[0, i].astype(F32)
-        for t in range(1, TP):
-            parts = parts + out_got[t, i].astype(F32)
-        out_total[i] = parts.astype(BF16)
-        return carry
-
-    lax.fori_loop(0, CP, sum_part, 0)
-
-    def keep_total():
-        projected[at.cp] = out_total[at.cp]
-
-    exchange(
-        r["s3"],
-        r["r3"],
-        lambda p: out_total.at[p],
-        lambda p: projected.at[p],
-        "cp",
-        CP,
-        at.cp,
-        keep_total,
-    )
+                out_part[c, t, b] = p[first : first + local_rows].astype(BF16)
+        copies = []
+        for off in range(1, TP):
+            to = (at.tp + off) % TP
+            copies.append(out_wires.copy(out_part.at[c, to], out_got.at[c, at.tp], {"tp": to}))
+        yield
+        out_got[c, at.tp] = out_part[c, at.tp]
+        for copy in copies:
+            copy.wait_recv()
+
+        def sum_part(b, carry):
+            parts = out_got[c, 0, b].astype(F32)
+            for t in range(1, TP):
+                parts = parts + out_got[c, t, b].astype(F32)
+            out_total[c, b] = parts.astype(BF16)
+            return carry
+
+        lax.fori_loop(0, blocks, sum_part, 0)
+        for n, off in enumerate(CHUNKS[c]):
+            for turn in range(NY):
+                y = (at.y + turn) % NY
+                source = out_total.at[c, n * NY + y]
+                if off == 0 and turn == 0:
+                    projected[at.cp] = source[...]
+                else:
+                    to = {"cp": (at.z + off) % NZ * NY + y}
+                    owners.append(out_wires.copy(source, projected.at[at.cp], to))
+
+    gather_rows(wires, steps, at, every, GATHER_SPLIT, out_chunk)
+    steps.run()
+    phase("out_cp")
+    for copy in owners:
+        copy.wait_recv()
+    phase("norm_feed")
     for c in range(CP):
         cols = slice(c * width, (c + 1) * width)
         attended[:, cols] = (tokens[:, cols].astype(F32) + projected[c].astype(F32)).astype(BF16)
@@ -655,12 +741,13 @@
     for t in range(TP):
         by_width[t] = normed[:, t * wide : (t + 1) * wide]
 
+    phase("swap1")
     def keep_width():
         got_width[at.tp] = by_width[at.tp]
 
     exchange(
-        r["s4"],
-        r["r4"],
+        r["s2"],
+        r["r2"],
         lambda p: by_width.at[p],
         lambda p: got_width.at[p],
         "tp",
@@ -668,36 +755,32 @@
         at.tp,
         keep_width,
     )
+    phase("gather_feed")
     stream[at.z, at.y] = jnp.concatenate(
         [got_width[t].astype(F32) for t in range(TP)], axis=0
     ).astype(BF16)
-    gather_rows(wires, steps, at, stream, GATHER_SPLIT)
-    steps.run()
-
-    loads["gate"].wait()
-    loads["up"].wait()
-    hidden = r["hidden"]
-    feed(
-        wires,
+    for name in ("gate", "up", "down"):
+        loads[name].wait()
+    reduced = r["reduced"]
+    places = {off: (c, n) for c, chunk in enumerate(CHUNKS) for n, off in enumerate(chunk)}
+    finished = far_scatter_parts(
+        qkv_wires,
+        steps,
+        lambda off: r["down_sum"].at[places[off]],
+        reduced,
+        r["down_far"],
+        lambda off: at.along_z((at.z + off) % NZ),
+    )
+    gather_rows(
+        qkv_wires,
         steps,
         at,
         stream,
-        r["gate"],
-        r["up"],
-        hidden,
-        r["unit_part"],
-        r["held"],
-        r["from_left"],
-        r["from_right"],
-        r["unit_total"],
-    )
-
-    down_part, reduced = r["down_part"], r["reduced"]
-    loads["down"].wait()
-    product_into(down_part, lambda: hidden[...].reshape(-1, hidden.shape[-1]), r["down"], 0)
-    for n in range(len(DOWN_PARTS)):
-        steps.add(unit(n, reduced, DOWN_PARTS, down_part, "d"))
+        GATHER_SPLIT,
+        lambda c: feed_chunk(qkv_wires, at, r, c, finished),
+    )
     steps.run()
+    phase("swap2")
     by_token, lowered = r["by_token"], r["lowered"]
     for t in range(TP):
         by_token[t] = reduced[pl.ds(t * local_rows, local_rows), :].astype(BF16)
@@ -706,8 +789,8 @@
         lowered[at.tp] = by_token[at.tp]
 
     exchange(
-        r["s5"],
-        r["r5"],
+        r["s1"],
+        r["r1"],
         lambda p: by_token.at[p],
         lambda p: lowered.at[p],
         "tp",
@@ -718,12 +801,15 @@
     for t in range(TP):
         cols = slice(t * wide, (t + 1) * wide)
         mixed[:, cols] = (attended[:, cols].astype(F32) + lowered[t].astype(F32)).astype(BF16)
+    phase("drain")
     wires.drain()
+    qkv_wires.drain()
+    phase(None)
 
 
 VMEM = pl.BlockSpec(memory_space=pltpu.VMEM)
 ANY = pl.BlockSpec(memory_space=pl.ANY)
-COPIES = 320
+COPIES, COPIES_2 = 128, 112
 
 
 def dma(count):
@@ -748,6 +834,7 @@
     qkv = query_weight.shape[1] + key_weight.shape[1] + value_weight.shape[1]
     units = gate_weight.shape[1]
     wide, width = model // TP, model // CP
+    chunks = len(CHUNKS)
 
     inverse = rope_base ** (-(jnp.arange(HD // 2, dtype=F32) * 2.0 / HD))
     positions = lax.axis_index("cp") * block + jnp.arange(block, dtype=jnp.int32)
@@ -782,29 +869,33 @@
         "summed": buf(block, qkv, kind=F32),
         "shared": buf(NZ, NY, block, 2 * HD),
         "every": buf(NZ, NY, block, wide),
-        "out_part": buf(TP, CP, local_rows, width),
-        "out_got": buf(TP, CP, local_rows, width),
-        "out_total": buf(CP, local_rows, width),
+        "out_part": buf(chunks, TP, CP // chunks, local_rows, width),
+        "out_got": buf(chunks, TP, CP // chunks, local_rows, width),
+        "out_total": buf(chunks, CP // chunks, local_rows, width),
         "projected": buf(CP, local_rows, width),
         "by_width": buf(TP, local_rows, wide),
         "got_width": buf(TP, local_rows, wide),
         "stream": buf(NZ, NY, block, wide),
-        "unit_part": buf(NX, 2, rows // TP, 2 * units),
-        "held": buf(NX, rows // TP, 2 * units),
-        "from_left": buf(UNITS, NX // 2, rows // TP // UNITS, 2 * units),
-        "from_right": buf(UNITS, NX // 2, rows // TP // UNITS, 2 * units),
-        "unit_total": buf(UNITS, rows // TP // UNITS, 2 * units, kind=F32),
-        "hidden": buf(NX, 2, rows // TP, units),
-        "down_part": buf(NZ, NY, block, wide),
+        "unit_part": buf(chunks, 2, NY, block, 2 * units),
+        "held": buf(chunks, NX, block, 2 * units),
+        "from_left": buf(chunks, NX // 2, block, 2 * units),
+        "from_right": buf(chunks, NX // 2, block, 2 * units),
+        "unit_total": buf(chunks, block, 2 * units, kind=F32),
+        "hidden": buf(chunks, 2, NX, block, units),
+        "down_part": buf(chunks, 2, NY, block, wide),
+        "down_left": buf(chunks, NY // 2, 2, block, wide),
+        "down_right": buf(chunks, NY // 2, 2, block, wide),
+        "down_sum": buf(chunks, 2, block, wide),
+        "down_far": buf(8, block, wide),
         "reduced": buf(block, wide, kind=F32),
         "by_token": buf(TP, local_rows, wide),
         "lowered": buf(TP, local_rows, wide),
     }
     scratch |= scatter_scratch("q", QKV_PARTS, block)
-    scratch |= scatter_scratch("d", DOWN_PARTS, block)
-    for n, count in enumerate((CP, TP, TP, CP, TP, TP)):
+    for n, count in enumerate((CP, TP, TP)):
         scratch |= {f"s{n}": dma(count), f"r{n}": dma(count)}
     scratch |= {"load": dma(len(WEIGHTS)), "send": dma(COPIES), "recv": dma(COPIES)}
+    scratch |= {"send_2": dma(COPIES_2), "recv_2": dma(COPIES_2)}
 
     names = (*inputs, "attended", "mixed", *scratch)
     shape = jax.ShapeDtypeStruct(tokens.shape, BF16)

time: 194 us -> 186 us (0.959)
  Pallas kernels: 189 us -> 182 us
    pallas_call x1, Pallas kernels: 189 us -> 182 us  [on_device(): pl.pallas_call(functools.partial(layer_kernel, names), out_shape=(shape,...]
where the time goes in v3:
time: 186 us
  Pallas kernels  182 us (98%)
  local copies, waits for them, and re-layouts  2.98 us (2%)
    pallas_call x1, Pallas kernels, on_device(): pl.pallas_call(functools.partial(layer_kernel, names), out_shape=(shape,...  182 us

profile of v3, /device:TPU:1, one launch (start us, length us, event | category | flops | bytes accessed | tf_op | source)
XLA Modules:
  0.0 186.2 jit_solution(4379273907558395543)
XLA Ops:
  0.7 0.1 fusion
  0.8 0.7 pad_maximum_fusion
  1.5 181.7 %layer.1 = (bf16[4,8192]{1,0:T(4,128)(2,1)}, bf16[4,8192]{1,0:T(4,128)(2,1)}) custom-call(bf16[4,8192]{1,0:T(4,128)(2,1)} %refs_0_.1, f32[1,8192]{1,0:T(1,128)} %bitcast.2, f32[1,8192]{1,0:T(1,128)} %bitcast.3, f32[32,128]{1,0:T(8,128)} %get-tuple-element.5.refs_3_, f32[32,128]{1,0:T(8,128)} %get-tuple-element.6.refs_4_, bf16[256,128]{1,0:T(8,128)(2,1)} %refs_5_.1, ...), custom_call_target="tpu_custom_call" | custom-call | tf_op jit(solution)/shard_map/layer/pallas_call | solution.py:902
  183.3 1.5 copy.14
  184.7 1.5 copy.15
  (2 shorter events, 0.0 us)

commit v4 on v3

--- a/solution.py
+++ b/solution.py
@@ -45,19 +45,49 @@
         self.sent, self.used = [], 0
 
 
+class Now(list):
+    pass
+
+
+def advance(gen):
+    needs = next(gen, None)
+    while isinstance(needs, Now):
+        for c in needs:
+            c.wait_recv()
+        needs = next(gen, None)
+    return needs
+
+
 class Steps:
     def __init__(self):
         self.queue = collections.deque()
 
     def add(self, gen, name="line", step=0):
         with jax.named_scope(f"{name}_{step}"):
-            going = next(gen, self) is not self
-        if going:
-            self.queue.append((gen, name, step + 1))
-
-    def run(self):
-        while self.queue:
-            self.add(*self.queue.popleft())
+            needs = advance(gen)
+        if needs is not None:
+            self.queue.append((needs, gen, name, step + 1))
+
+    def go_on(self, entry):
+        needs, gen, name, step = entry
+        with jax.named_scope(f"wait_{name}_{step}"):
+            for c in needs:
+                c.wait_recv()
+        self.add(gen, name, step)
+
+    def run(self, until=lambda: False):
+        while self.queue and not until():
+            self.go_on(self.queue.popleft())
+
+    def play(self, order, begin=None):
+        for name in order.split():
+            if name.isupper():
+                begin(name)
+                continue
+            at = next(i for i, entry in enumerate(self.queue) if entry[2] == name)
+            entry = self.queue[at]
+            del self.queue[at]
+            self.go_on(entry)
 
 
 class Phases:
@@ -138,9 +168,7 @@
     if arrived:
         arrived(me)
     for k in range(1, n // 2 + 1):
-        yield
-        for c in flying:
-            c.wait_recv()
+        yield flying
         if k <= last:
             flying = send(k)
             if arrived:
@@ -176,96 +204,109 @@
     r = wires.copy(half_of(far, 0), half_of(from_left.at[0], 0), right)
     l = wires.copy(half_of(far, 1), half_of(from_right.at[0], 1), left)
     for k in range(1, m):
-        yield
         to_right, to_left = own((me + m - k) % n), own((me + n - m + k) % n)
         got_left, got_right = from_left.at[k - 1], from_right.at[k - 1]
-        r.wait_recv()
+        yield [r]
         if k == 1:
             add_rows(half_of(got_left, 0), [half_of(got_left, 0), half_of(to_right, 0)])
             add_rows(half_of(got_left, 1), [half_of(to_right, 1)])
         else:
             add_rows(got_left, [got_left, to_right])
         r = wires.copy(got_left, from_left.at[k], right)
-        l.wait_recv()
+        yield Now([l])
         if k == 1:
             add_rows(half_of(got_right, 1), [half_of(got_right, 1), half_of(to_left, 1)])
             add_rows(half_of(got_right, 0), [half_of(to_left, 0)])
         else:
             add_rows(got_right, [got_right, to_left])
         l = wires.copy(got_right, from_right.at[k], left)
-    yield
-    r.wait_recv()
-    l.wait_recv()
+    yield [r, l]
     add_rows(out, [own(me), from_left.at[m - 1], from_right.at[m - 1]])
 
 
 def far_gather(wires, block, n, me, device_of, arrived):
-    def to(off):
-        return device_of((me + n + off) % n)
+    def send(ref, off):
+        return wires.copy(ref, ref, device_of((me + n + off) % n))
 
     def whole(off):
         return block((me + n + off) % n)
-
-    def send(ref, off):
-        return wires.copy(ref, ref, to(off))
 
     own = block(me)
     p2, m2, p1, m1 = send(own, 2), send(own, -2), send(own, 1), send(own, -1)
     arrived(0)
-    yield
-    p2.wait_recv()
+    yield [p2]
     p3, p4 = send(whole(-2), 1), send(half_of(whole(-2), 0), 2)
-    m2.wait_recv()
+    yield Now([m2])
     m3, m4 = send(whole(2), -1), send(half_of(whole(2), 1), -2)
-    p1.wait_recv()
+    yield Now([p1])
     arrived(7)
-    m1.wait_recv()
-    arrived(1)
-    arrived(6)
-    arrived(2)
-    yield
-    p3.wait_recv()
+    yield Now([m1])
+    for off in (1, 6, 2):
+        arrived(off)
+    yield [p3]
     arrived(5)
-    m3.wait_recv()
+    yield Now([m3])
     arrived(3)
-    p4.wait_recv()
-    m4.wait_recv()
+    yield Now([p4, m4])
     arrived(4)
 
 
 def far_scatter(wires, own, out, bufs, n, me, device_of):
-    near_l, near_r, turn_l, turn_r, far_l, far_r, sum_l, sum_r = [bufs.at[i] for i in range(8)]
-
-    def to(off):
-        return device_of((me + n + off) % n)
-
-    def term(off):
-        return own((me + n + off) % n)
-
-    opposite = term(4)
-    f_l = wires.copy(half_of(opposite, 0), half_of(far_l, 0), to(2))
-    f_r = wires.copy(half_of(opposite, 1), half_of(far_r, 1), to(-2))
-    t_l = wires.copy(term(3), turn_l, to(1))
-    t_r = wires.copy(term(-3), turn_r, to(-1))
-    n_l = wires.copy(term(1), near_l, to(1))
-    n_r = wires.copy(term(-1), near_r, to(-1))
-    yield
-    t_l.wait_recv()
-    f_l.wait_recv()
-    mine = term(2)
-    add_rows(half_of(turn_l, 0), [half_of(r, 0) for r in (turn_l, far_l, mine)])
-    add_rows(half_of(turn_l, 1), [half_of(r, 1) for r in (turn_l, mine)])
-    s_l = wires.copy(turn_l, sum_l, to(2))
-    t_r.wait_recv()
-    f_r.wait_recv()
-    mine = term(-2)
-    add_rows(half_of(turn_r, 1), [half_of(r, 1) for r in (turn_r, far_r, mine)])
-    add_rows(half_of(turn_r, 0), [half_of(r, 0) for r in (turn_r, mine)])
-    s_r = wires.copy(turn_r, sum_r, to(-2))
-    yield
-    for c in (n_l, n_r, s_l, s_r):
-        c.wait_recv()
-    add_rows(out, [own(me), near_l, near_r, sum_l, sum_r])
+    lines = FarScatter(
+        wires,
+        lambda off: own((me + off) % n),
+        out,
+        bufs,
+        lambda off: device_of((me + off) % n),
+    )
+    for off in (4, 3, 5, 1, 7):
+        lines.send(off)
+    yield from lines.turns("l")
+    other = lines.turns("r")
+    yield Now(next(other))
+    next(other, None)
+    yield from lines.last_round()
+
+
+class FarScatter:
+    def __init__(self, wires, own, out, bufs, device_of):
+        self.wires, self.own, self.out, self.device_of = wires, own, out, device_of
+        self.bufs, self.sent = bufs, {}
+
+    def copy(self, name, src, dst, off):
+        self.sent[name] = self.wires.copy(src, dst, self.device_of(off))
+
+    def send(self, off):
+        near_l, near_r, turn_l, turn_r, far_l, far_r = [self.bufs.at[i] for i in range(6)]
+        term = self.own(off)
+        if off == 1:
+            self.copy("near_l", term, near_l, 1)
+        elif off == 7:
+            self.copy("near_r", term, near_r, 7)
+        elif off == 3:
+            self.copy("turn_l", term, turn_l, 1)
+        elif off == 5:
+            self.copy("turn_r", term, turn_r, 7)
+        elif off == 4:
+            self.copy("far_l", half_of(term, 0), half_of(far_l, 0), 2)
+            self.copy("far_r", half_of(term, 1), half_of(far_r, 1), 6)
+
+    def turn(self, side):
+        n, off, full = (0, 2, 0) if side == "l" else (1, 6, 1)
+        turn, far, into = self.bufs.at[2 + n], self.bufs.at[4 + n], self.bufs.at[6 + n]
+        mine = self.own(off)
+        add_rows(half_of(turn, full), [half_of(x, full) for x in (turn, far, mine)])
+        add_rows(half_of(turn, 1 - full), [half_of(x, 1 - full) for x in (turn, mine)])
+        self.copy("sum_" + side, turn, into, off)
+
+    def turns(self, side):
+        yield [self.sent["turn_" + side], self.sent["far_" + side]]
+        self.turn(side)
+
+    def last_round(self):
+        yield [self.sent[n] for n in ("near_l", "near_r", "sum_l", "sum_r")]
+        near_l, near_r, sum_l, sum_r = [self.bufs.at[i] for i in (0, 1, 6, 7)]
+        add_rows(self.out, [self.own(0), near_l, near_r, sum_l, sum_r])
 
 
 def exchange(send_sem, recv_sem, source, target, axis, n, me, meanwhile=None):
@@ -296,13 +337,16 @@
 
 Z_FIRST, Y_FIRST = "z", "y"
 QKV_PARTS = ((0, 256, Y_FIRST), (256, 256, Y_FIRST), (512, 384, Y_FIRST), (896, 384, Z_FIRST))
+QKV_ORDER = "k a b c k a c k b a k b c a k b c k"
 GATHER_SPLIT = 768
-
-
-CHUNKS = ((0, 7), (1, 6), (2, 5), (3, 4))
-
-
-def gather_rows(wires, steps, at, out_ref, split, ready):
+DOWN_SPLIT = 768
+
+
+CHUNKS = ((2, 6), (3, 4), (5, 7), (0, 1))
+OUT_CHUNKS = ((0, 7), (1, 6), (2, 5), (3, 4))
+
+
+def gather_rows(wires, steps, at, out_ref, split, chunks, ready):
     first, rest = pl.ds(0, split), pl.ds(split, out_ref.shape[-1] - split)
     seen = collections.Counter()
 
@@ -311,9 +355,9 @@
 
     def mark(off):
         seen[off] += 1
-        for c, chunk in enumerate(CHUNKS):
+        for c, chunk in enumerate(chunks):
             if off in chunk and all(seen[o] == 2 for o in chunk):
-                steps.add(ready(c), f"chunk{c}")
+                steps.add(ready(c), f"chunk{chunks[c][0]}{chunks[c][1]}")
 
     def y_first():
         yield from ring_gather(
@@ -344,22 +388,19 @@
 def gather_small(wires, at, ref):
     handed = []
 
-    def to_y(i):
-        block = ref.at[i, at.y]
+    def to_y(block):
         for off in (1, 3, 2):
             handed.append(wires.copy(block, block, at.along_y((at.y + off) % NY)))
 
     own = ref.at[at.z, at.y]
     order = (4, 3, 5, 2, 6, 1, 7)
     copies = {off: wires.copy(own, own, at.along_z((at.z + off) % NZ)) for off in order}
-    to_y(at.z)
-    yield
+    to_y(own)
+    yield []
     for off in (1, 7, 2, 6, 3, 5, 4):
-        copies[off].wait_recv()
-        to_y((at.z + NZ - off) % NZ)
-    yield
-    for c in handed:
-        c.wait_recv()
+        yield Now([copies[off]])
+        to_y(ref.at[(at.z + NZ - off) % NZ, at.y])
+    yield handed
 
 
 def scatter_part(wires, at, part, out, columns, way, bufs):
@@ -432,12 +473,18 @@
     lax.fori_loop(0, width // tile, body, 0)
 
 
-def chunk_rows(ref, at, c):
-    blocks = [ref[(at.z + off) % NZ] for off in CHUNKS[c]]
+def chunk_rows(ref, at, chunk):
+    blocks = [ref[(at.z + off) % NZ] for off in chunk]
     return jnp.concatenate([b.reshape(-1, b.shape[-1]) for b in blocks], axis=0)
 
 
-def feed_chunk(wires, at, r, c, finished):
+ORDER = (
+    "a B C b D c a d b a c d b a a c d b c a d b b c c "
+    "d d a b V v c d W w b T c U d N n t u L n l n"
+)
+
+
+def feed_chunk(wires, at, r, c, produced, finished):
     partner = at.partner()
     units = r["gate"].shape[1]
     part, held, total, hidden = (
@@ -450,23 +497,21 @@
 
     def tile(w_ref, col, width, start):
         p = jnp.dot(
-            chunk_rows(r["stream"], at, c), w_ref[:, pl.ds(col, width)], preferred_element_type=F32
+            chunk_rows(r["stream"], at, CHUNKS[c]), w_ref[:, pl.ds(col, width)], preferred_element_type=F32
         )
         part[:, :, :, pl.ds(start + col, width)] = p.astype(BF16).reshape(2, NY, rows, width)
 
-    def body(t, carry):
-        col = pl.multiple_of(t * 256, 256)
+    def body(t):
+        col = t * 256
         tile(r["gate"], col, 256, 0)
         tile(r["up"], col, 256, units)
-        return carry
-
-    lax.fori_loop(0, units // 256, body, 0)
+
+    for t in range(units // 256):
+        body(t)
     if units % 256:
         tile(r["gate"], units // 256 * 256, units % 256, 0)
         tile(r["up"], units // 256 * 256, units % 256, units)
-    copy = wires.copy(part.at[1 - at.core], held, partner)
-    yield
-    copy.wait_recv()
+    yield [wires.copy(part.at[1 - at.core], held, partner)]
     add_rows(held, [held, part.at[at.core]])
     yield from ring_scatter(
         wires,
@@ -495,9 +540,7 @@
     yield from ring_gather(
         wires, lambda i: hidden.at[at.core, i], NX, at.x, at.along_x, hand_over
     )
-    yield
-    for copy in handed:
-        copy.wait_recv()
+    yield handed
     down_part = r["down_part"].at[c]
 
     def down(i, carry):
@@ -509,9 +552,10 @@
         return carry
 
     lax.fori_loop(0, down_part.shape[-1] // 256, down, 0)
+    produced(c)
     yield from ring_scatter(
         wires,
-        lambda j: down_part.at[:, j],
+        lambda j: down_part.at[:, j, :, pl.ds(0, DOWN_SPLIT)],
         r["down_sum"].at[c],
         r["down_left"].at[c],
         r["down_right"].at[c],
@@ -522,48 +566,6 @@
     finished(c)
 
 
-def far_scatter_parts(wires, steps, own, out, bufs, device_of):
-    near_l, near_r, turn_l, turn_r, far_l, far_r, sum_l, sum_r = [bufs.at[i] for i in range(8)]
-    sent = {}
-
-    def last_round():
-        yield
-        for side, off, turn, far, into in (
-            ("l", 2, turn_l, far_l, sum_l),
-            ("r", 6, turn_r, far_r, sum_r),
-        ):
-            full, other = (0, 1) if side == "l" else (1, 0)
-            sent["t" + side].wait_recv()
-            sent["f" + side].wait_recv()
-            mine = own(off)
-            add_rows(half_of(turn, full), [half_of(x, full) for x in (turn, far, mine)])
-            add_rows(half_of(turn, other), [half_of(x, other) for x in (turn, mine)])
-            sent["s" + side] = wires.copy(turn, into, device_of(off))
-        yield
-        for name in ("nl", "nr", "sl", "sr"):
-            sent[name].wait_recv()
-        add_rows(out, [own(0), near_l, near_r, sum_l, sum_r])
-
-    def finished(c):
-        for off in CHUNKS[c]:
-            term = own(off)
-            if off == 1:
-                sent["nl"] = wires.copy(term, near_l, device_of(1))
-            elif off == 7:
-                sent["nr"] = wires.copy(term, near_r, device_of(7))
-            elif off == 3:
-                sent["tl"] = wires.copy(term, turn_l, device_of(1))
-            elif off == 5:
-                sent["tr"] = wires.copy(term, turn_r, device_of(7))
-            elif off == 4:
-                sent["fl"] = wires.copy(half_of(term, 0), half_of(far_l, 0), device_of(2))
-                sent["fr"] = wires.copy(half_of(term, 1), half_of(far_r, 1), device_of(6))
-        if c == len(CHUNKS) - 1:
-            steps.add(last_round(), "last")
-
-    return finished
-
-
 def normalize(values, gain):
     mean_square = jnp.mean(values * values, axis=-1, keepdims=True)
     return (values * lax.rsqrt(mean_square + epsilon) * gain).astype(BF16)
@@ -575,10 +577,12 @@
 def layer_kernel(names, *refs):
     r = dict(zip(names, refs))
     at = Place()
-    qkv_wires, wires, steps = Wires(r["send"], r["recv"]), Wires(r["send_2"], r["recv_2"]), Steps()
+    qkv_wires, wires = Wires(r["send"], r["recv"]), Wires(r["send"], r["recv_2"])
+    steps = Steps()
     out_wires = wires
-    tokens, attended, mixed = r["tokens"], r["attended"], r["mixed"]
+    tokens = r["tokens"]
     local_rows, model = tokens.shape
+    attended, mixed = r["streams"].at[0], r["streams"].at[1]
     cos, sin = r["cos"], r["sin"]
 
     phase = Phases()
@@ -604,7 +608,7 @@
         got[at.cp] = slices[at.cp]
 
     exchange(
-        r["s0"], r["r0"], lambda p: slices.at[p], lambda p: got.at[p], "cp", CP, at.cp, keep_slice
+        r["send"], r["recv_2"], lambda p: slices.at[p], lambda p: got.at[p], "cp", CP, at.cp, keep_slice
     )
 
     phase("spread_tp")
@@ -612,7 +616,7 @@
         columns[at.tp] = got[...]
 
     exchange(
-        r["s1"], r["r1"], lambda p: got, lambda p: columns.at[p], "tp", TP, at.tp, keep_columns
+        r["send"], r["r0"], lambda p: got, lambda p: columns.at[p], "tp", TP, at.tp, keep_columns
     )
     phase("relayout")
     rows_in = r["rows_in"]
@@ -648,12 +652,13 @@
     loads["value"].wait()
     product_into(part, x, r["key"], 0)
     product_into(part, x, r["value"], HD)
-    steps.add(keys_and_values(), "kv")
+    steps.add(keys_and_values(), "k")
     loads["query"].wait()
     product_into(part, x, r["query"], 2 * HD)
     phase("qkv_sum")
     for n in range(1, len(QKV_PARTS)):
-        steps.add(unit(n, summed, QKV_PARTS, part, "q"), f"q{n}")
+        steps.add(unit(n, summed, QKV_PARTS, part, "q"), "kabc"[n])
+    steps.play(QKV_ORDER)
     steps.run()
     qkv_wires.drain()
 
@@ -692,7 +697,7 @@
     owners = []
 
     def out_chunk(c):
-        p = jnp.dot(chunk_rows(every, at, c), r["out"][...], preferred_element_type=F32)
+        p = jnp.dot(chunk_rows(every, at, OUT_CHUNKS[c]), r["out"][...], preferred_element_type=F32)
         blocks = 2 * NY
         for b in range(blocks):
             for t in range(TP):
@@ -702,10 +707,8 @@
         for off in range(1, TP):
             to = (at.tp + off) % TP
             copies.append(out_wires.copy(out_part.at[c, to], out_got.at[c, at.tp], {"tp": to}))
-        yield
         out_got[c, at.tp] = out_part[c, at.tp]
-        for copy in copies:
-            copy.wait_recv()
+        yield copies
 
         def sum_part(b, carry):
             parts = out_got[c, 0, b].astype(F32)
@@ -715,7 +718,7 @@
             return carry
 
         lax.fori_loop(0, blocks, sum_part, 0)
-        for n, off in enumerate(CHUNKS[c]):
+        for n, off in enumerate(OUT_CHUNKS[c]):
             for turn in range(NY):
                 y = (at.y + turn) % NY
                 source = out_total.at[c, n * NY + y]
@@ -725,11 +728,12 @@
                     to = {"cp": (at.z + off) % NZ * NY + y}
                     owners.append(out_wires.copy(source, projected.at[at.cp], to))
 
-    gather_rows(wires, steps, at, every, GATHER_SPLIT, out_chunk)
+    gather_rows(wires, steps, at, every, GATHER_SPLIT, OUT_CHUNKS, out_chunk)
     steps.run()
     phase("out_cp")
-    for copy in owners:
-        copy.wait_recv()
+    for c in owners:
+        c.wait_recv()
+    wires.drain()
     phase("norm_feed")
     for c in range(CP):
         cols = slice(c * width, (c + 1) * width)
@@ -746,8 +750,8 @@
         got_width[at.tp] = by_width[at.tp]
 
     exchange(
-        r["s2"],
-        r["r2"],
+        r["send"],
+        r["r1"],
         lambda p: by_width.at[p],
         lambda p: got_width.at[p],
         "tp",
@@ -763,24 +767,75 @@
         loads[name].wait()
     reduced = r["reduced"]
     places = {off: (c, n) for c, chunk in enumerate(CHUNKS) for n, off in enumerate(chunk)}
-    finished = far_scatter_parts(
+    def to_z(off):
+        return at.along_z((at.z + off) % NZ)
+
+    lines = FarScatter(
         qkv_wires,
-        steps,
         lambda off: r["down_sum"].at[places[off]],
-        reduced,
+        reduced.at[:, pl.ds(0, DOWN_SPLIT)],
         r["down_far"],
-        lambda off: at.along_z((at.z + off) % NZ),
-    )
-    gather_rows(
+        to_z,
+    )
+    rest = pl.ds(DOWN_SPLIT, reduced.shape[1] - DOWN_SPLIT)
+    z_lines = FarScatter(
         qkv_wires,
-        steps,
-        at,
-        stream,
-        GATHER_SPLIT,
-        lambda c: feed_chunk(qkv_wires, at, r, c, finished),
-    )
+        lambda off: r["down_part"].at[*places[off], :, :, rest],
+        r["z_sum"],
+        r["z_far"],
+        to_z,
+    )
+    there = {}
+
+    def produced(c):
+        for off in CHUNKS[c]:
+            z_lines.send(off)
+
+    def finished(c):
+        for off in CHUNKS[c]:
+            lines.send(off)
+
+    def z_first_end():
+        yield from z_lines.last_round()
+        yield from ring_scatter(
+            qkv_wires,
+            lambda j: r["z_sum"].at[j],
+            reduced.at[:, rest],
+            r["z_left"],
+            r["z_right"],
+            NY,
+            at.y,
+            at.along_y,
+        )
+
+    later = {
+        "T": lambda: lines.turns("l"),
+        "U": lambda: lines.turns("r"),
+        "V": lambda: z_lines.turns("l"),
+        "W": lambda: z_lines.turns("r"),
+        "N": z_first_end,
+        "L": lines.last_round,
+    }
+
+    def begin(letter):
+        if letter in later:
+            gen = later[letter]()
+        else:
+            gen = feed_chunk(qkv_wires, at, r, "ABCD".index(letter), produced, finished)
+        steps.add(gen, letter.lower())
+
+    def chunk_there(c):
+        there[c] = True
+        if c == 0:
+            begin("A")
+        return iter(())
+
+    gather_rows(qkv_wires, steps, at, stream, GATHER_SPLIT, CHUNKS, chunk_there)
+    steps.run(lambda: len(there) == len(CHUNKS))
+    steps.play(ORDER, begin)
     steps.run()
     phase("swap2")
+    qkv_wires.drain()
     by_token, lowered = r["by_token"], r["lowered"]
     for t in range(TP):
         by_token[t] = reduced[pl.ds(t * local_rows, local_rows), :].astype(BF16)
@@ -789,8 +844,8 @@
         lowered[at.tp] = by_token[at.tp]
 
     exchange(
-        r["s1"],
-        r["r1"],
+        r["send"],
+        r["r0"],
         lambda p: by_token.at[p],
         lambda p: lowered.at[p],
         "tp",
@@ -801,15 +856,12 @@
     for t in range(TP):
         cols = slice(t * wide, (t + 1) * wide)
         mixed[:, cols] = (attended[:, cols].astype(F32) + lowered[t].astype(F32)).astype(BF16)
-    phase("drain")
-    wires.drain()
-    qkv_wires.drain()
     phase(None)
 
 
 VMEM = pl.BlockSpec(memory_space=pltpu.VMEM)
 ANY = pl.BlockSpec(memory_space=pl.ANY)
-COPIES, COPIES_2 = 128, 112
+COPIES, COPIES_2 = 140, 111
 
 
 def dma(count):
@@ -883,27 +935,29 @@
         "unit_total": buf(chunks, block, 2 * units, kind=F32),
         "hidden": buf(chunks, 2, NX, block, units),
         "down_part": buf(chunks, 2, NY, block, wide),
-        "down_left": buf(chunks, NY // 2, 2, block, wide),
-        "down_right": buf(chunks, NY // 2, 2, block, wide),
-        "down_sum": buf(chunks, 2, block, wide),
-        "down_far": buf(8, block, wide),
+        "down_left": buf(chunks, NY // 2, 2, block, DOWN_SPLIT),
+        "down_right": buf(chunks, NY // 2, 2, block, DOWN_SPLIT),
+        "down_sum": buf(chunks, 2, block, DOWN_SPLIT),
+        "down_far": buf(8, block, DOWN_SPLIT),
+        "z_far": buf(8, NY, block, wide - DOWN_SPLIT),
+        "z_sum": buf(NY, block, wide - DOWN_SPLIT),
+        "z_left": buf(NY // 2, block, wide - DOWN_SPLIT),
+        "z_right": buf(NY // 2, block, wide - DOWN_SPLIT),
         "reduced": buf(block, wide, kind=F32),
         "by_token": buf(TP, local_rows, wide),
         "lowered": buf(TP, local_rows, wide),
     }
     scratch |= scatter_scratch("q", QKV_PARTS, block)
-    for n, count in enumerate((CP, TP, TP)):
-        scratch |= {f"s{n}": dma(count), f"r{n}": dma(count)}
+    scratch |= {f"r{n}": dma(TP) for n in range(2)}
     scratch |= {"load": dma(len(WEIGHTS)), "send": dma(COPIES), "recv": dma(COPIES)}
-    scratch |= {"send_2": dma(COPIES_2), "recv_2": dma(COPIES_2)}
-
-    names = (*inputs, "attended", "mixed", *scratch)
-    shape = jax.ShapeDtypeStruct(tokens.shape, BF16)
-    return pl.pallas_call(
+    scratch |= {"recv_2": dma(COPIES_2)}
+
+    names = (*inputs, "streams", *scratch)
+    streams = pl.pallas_call(
         functools.partial(layer_kernel, names),
-        out_shape=(shape, shape),
+        out_shape=jax.ShapeDtypeStruct((2, *tokens.shape), BF16),
         in_specs=[ANY if name.endswith("_weight") else VMEM for name in inputs],
-        out_specs=(VMEM, VMEM),
+        out_specs=VMEM,
         scratch_shapes=list(scratch.values()),
         compiler_params=pltpu.CompilerParams(
             collective_id=0,
@@ -912,6 +966,7 @@
         ),
         name="layer",
     )(*inputs.values())
+    return streams[0], streams[1]
 
 
 def solution(mesh):

time: 186 us -> 173 us (0.930)
  Pallas kernels: 182 us -> 170 us
    pallas_call x1, Pallas kernels: 182 us -> 170 us  [on_device(): pl.pallas_call(functools.partial(layer_kernel, names), out_shape=jax.Shap...]
    unnamed x2 -> x0, local copies, waits for them, and re-layouts: 2.98 us -> none
where the time goes in v4:
time: 173 us
  Pallas kernels  170 us (98%)
    pallas_call x1, Pallas kernels, on_device(): pl.pallas_call(functools.partial(layer_kernel, names), out_shape=jax.Shap...  170 us

profile of v4, /device:TPU:1, one launch (start us, length us, event | category | flops | bytes accessed | tf_op | source)
XLA Modules:
  0.0 173.1 jit_solution(6118884055513182078)
XLA Ops:
  0.7 0.1 fusion
  0.8 0.7 pad_maximum_fusion
  1.5 170.0 %layer.1 = bf16[2,4,8192]{2,1,0:T(4,128)(2,1)} custom-call(bf16[4,8192]{1,0:T(4,128)(2,1)} %refs_0_.1, f32[1,8192]{1,0:T(1,128)} %bitcast.6, f32[1,8192]{1,0:T(1,128)} %bitcast.7, f32[32,128]{1,0:T(8,128)} %get-tuple-element.7.refs_3_, f32[32,128]{1,0:T(8,128)} %get-tuple-element.8.refs_4_, bf16[256,128]{1,0:T(8,128)(2,1)} %refs_5_.1, ...), custom_call_target="tpu_custom_call" | custom-call | tf_op jit(solution)/shard_map/layer/pallas_call | solution.py:956
  171.5 1.6 slice_bitcast_fusion
  (2 shorter events, 0.0 us)

commit v5 on v4

--- a/solution.py
+++ b/solution.py
@@ -24,13 +24,15 @@
         self.send, self.recv, self.used, self.sent = send, recv, 0, []
 
     def copy(self, src, dst, device):
-        i = self.used
+        i, slots = self.used, self.send.shape[0]
         self.used += 1
-        assert i < self.send.shape[0]
+        assert i < self.recv.shape[0]
+        if i >= slots:
+            self.sent[i - slots].wait_send()
         c = pltpu.make_async_remote_copy(
             src_ref=src,
             dst_ref=dst,
-            send_sem=self.send.at[i],
+            send_sem=self.send.at[i % slots],
             recv_sem=self.recv.at[i],
             device_id=device,
             device_id_type=MESH,
@@ -40,7 +42,7 @@
         return c
 
     def drain(self):
-        for c in self.sent:
+        for c in self.sent[-self.send.shape[0] :]:
             c.wait_send()
         self.sent, self.used = [], 0
 
@@ -60,7 +62,7 @@
 
 class Steps:
     def __init__(self):
-        self.queue = collections.deque()
+        self.queue, self.begun = collections.deque(), set()
 
     def add(self, gen, name="line", step=0):
         with jax.named_scope(f"{name}_{step}"):
@@ -79,15 +81,22 @@
         while self.queue and not until():
             self.go_on(self.queue.popleft())
 
-    def play(self, order, begin=None):
-        for name in order.split():
-            if name.isupper():
-                begin(name)
+    def play(self, order, begin):
+        for word in order.split():
+            if word.isupper():
+                if word not in self.begun:
+                    self.begun.add(word)
+                    begin(word)
                 continue
-            at = next(i for i, entry in enumerate(self.queue) if entry[2] == name)
-            entry = self.queue[at]
-            del self.queue[at]
-            self.go_on(entry)
+            name, step = word.split("/") if "/" in word else (word[0], word[1:])
+            step = int(step)
+            while True:
+                found = [i for i, e in enumerate(self.queue) if e[2] == name]
+                if not found or self.queue[found[0]][3] > step:
+                    break
+                entry = self.queue[found[0]]
+                del self.queue[found[0]]
+                self.go_on(entry)
 
 
 class Phases:
@@ -151,7 +160,12 @@
 
 def half_of(ref, h):
     d = ref.shape[0] // 2
-    return ref.at[pl.ds(h * d, d)]
+    if d:
+        return ref.at[pl.ds(h * d, d)]
+    width = ref.shape[-1]
+    d = -(-width // 256) * 128
+    cols = pl.ds(0, d) if h == 0 else pl.ds(d, width - d)
+    return ref.at[(slice(None),) * (len(ref.shape) - 1) + (cols,)]
 
 
 def ring_gather(wires, block, n, me, device_of, arrived=None):
@@ -179,7 +193,7 @@
 
 
 def add_rows(dst, terms, finish=None):
-    if len(dst.shape) == 3:
+    if len(dst.shape) > 2:
         for i in range(dst.shape[0]):
             add_rows(dst.at[i], [t.at[i] for t in terms])
         return
@@ -337,13 +351,13 @@
 
 Z_FIRST, Y_FIRST = "z", "y"
 QKV_PARTS = ((0, 256, Y_FIRST), (256, 256, Y_FIRST), (512, 384, Y_FIRST), (896, 384, Z_FIRST))
-QKV_ORDER = "k a b c k a c k b a k b c a k b c k"
+QKV_ORDER = "k1 A B k2 c1 a1 k3 b1 a2 c2 k4 a3 b2 c3 a4 c4 b3 k5 o1 b4 k6"
 GATHER_SPLIT = 768
 DOWN_SPLIT = 768
 
 
-CHUNKS = ((2, 6), (3, 4), (5, 7), (0, 1))
-OUT_CHUNKS = ((0, 7), (1, 6), (2, 5), (3, 4))
+CHUNKS = {"e": (0,), "b": (2, 6), "c": (3, 4), "d": (5,), "a": (1, 7)}
+OUT_CHUNKS = {0: (0, 7, 1, 6, 2), 1: (5, 3, 4)}
 
 
 def gather_rows(wires, steps, at, out_ref, split, chunks, ready):
@@ -355,9 +369,9 @@
 
     def mark(off):
         seen[off] += 1
-        for c, chunk in enumerate(chunks):
+        for c, chunk in chunks.items():
             if off in chunk and all(seen[o] == 2 for o in chunk):
-                steps.add(ready(c), f"chunk{chunks[c][0]}{chunks[c][1]}")
+                steps.add(ready(c), f"chunk{c}")
 
     def y_first():
         yield from ring_gather(
@@ -478,77 +492,62 @@
     return jnp.concatenate([b.reshape(-1, b.shape[-1]) for b in blocks], axis=0)
 
 
-ORDER = (
-    "a B C b D c a d b a c d b a a c d b c a d b b c c "
-    "d d a b V v c d W w b T c U d N n t u L n l n"
-)
+GATHER_ORDER = """yz/1 y0/1 z/1 yz/2 y0/2 E y7/1 y1/1 e1 y6/1 y2/1 z/2 yz/3 y7/2 e2 y1/2 y6/2 y2/2 B y5/1 y3/1 y4/1 yz/4 b1 e3 y5/2 y3/2 e4 y4/2"""
+ORDER = """b2 C D c1 d1 A b3 a1 c2 d2 b4 e5 a2 c3 d3 b5 e6 a3 b6 c4 d4 e7 a4 c5 c6 b7 d5 d6 a5 a6 e8 b8 c7 V v1 W w1 d7 a7 c8 d8 T U a8 N n1 t1 u1 n2 L l1 n3"""
 
 
 def feed_chunk(wires, at, r, c, produced, finished):
     partner = at.partner()
     units = r["gate"].shape[1]
-    part, held, total, hidden = (
-        r["unit_part"].at[c],
-        r["held"].at[c],
-        r["unit_total"].at[c],
-        r["hidden"].at[c],
-    )
-    rows = total.shape[0]
+    part, held, total, hidden, down_part = (
+        r[f"{name}_{c}"] for name in ("unit_part", "held", "unit_total", "hidden", "down_part")
+    )
 
     def tile(w_ref, col, width, start):
         p = jnp.dot(
             chunk_rows(r["stream"], at, CHUNKS[c]), w_ref[:, pl.ds(col, width)], preferred_element_type=F32
         )
-        part[:, :, :, pl.ds(start + col, width)] = p.astype(BF16).reshape(2, NY, rows, width)
-
-    def body(t):
-        col = t * 256
-        tile(r["gate"], col, 256, 0)
-        tile(r["up"], col, 256, units)
+        cols = pl.ds(start + col, width)
+        part[:, :, :, :, cols] = p.astype(BF16).reshape(*part.shape[:4], width)
 
     for t in range(units // 256):
-        body(t)
+        tile(r["gate"], t * 256, 256, 0)
+        tile(r["up"], t * 256, 256, units)
     if units % 256:
         tile(r["gate"], units // 256 * 256, units % 256, 0)
         tile(r["up"], units // 256 * 256, units % 256, units)
-    yield [wires.copy(part.at[1 - at.core], held, partner)]
-    add_rows(held, [held, part.at[at.core]])
+    yield [wires.copy(part.at[:, :, 1 - at.core], held, partner)]
+    add_rows(held, [held, part.at[:, :, at.core]])
     yield from ring_scatter(
         wires,
-        lambda i: held.at[i],
+        lambda i: held.at[:, i],
         total,
-        r["from_left"].at[c],
-        r["from_right"].at[c],
+        r[f"from_left_{c}"],
+        r[f"from_right_{c}"],
         NX,
         at.x,
         at.along_x,
     )
-
-    def activate(i, carry):
-        here = pl.ds(pl.multiple_of(i * 16, 16), 16)
-        gate, up = total[here, pl.ds(0, units)], total[here, pl.ds(units, units)]
-        hidden[at.core, at.x, here, :] = (jax.nn.silu(gate) * up).astype(BF16)
-        return carry
-
-    lax.fori_loop(0, rows // 16, activate, 0)
+    for n in range(total.shape[0]):
+        gate, up = total[n, :, pl.ds(0, units)], total[n, :, pl.ds(units, units)]
+        hidden[n, at.x, at.core] = (jax.nn.silu(gate) * up).astype(BF16)
     handed = []
 
     def hand_over(i):
-        ref = hidden.at[at.core, i]
+        ref = hidden.at[:, i, at.core]
         handed.append(wires.copy(ref, ref, partner))
 
     yield from ring_gather(
-        wires, lambda i: hidden.at[at.core, i], NX, at.x, at.along_x, hand_over
+        wires, lambda i: hidden.at[:, i, at.core], NX, at.x, at.along_x, hand_over
     )
     yield handed
-    down_part = r["down_part"].at[c]
 
     def down(i, carry):
         cols = pl.ds(pl.multiple_of(i * 256, 256), 256)
         p = jnp.dot(
-            hidden[...].reshape(2 * NX * rows, units), r["down"][:, cols], preferred_element_type=F32
-        )
-        down_part[:, :, :, cols] = p.astype(BF16).reshape(2, NY, rows, 256)
+            hidden[...].reshape(-1, units), r["down"][:, cols], preferred_element_type=F32
+        )
+        down_part[:, :, :, cols] = p.astype(BF16).reshape(*down_part.shape[:3], 256)
         return carry
 
     lax.fori_loop(0, down_part.shape[-1] // 256, down, 0)
@@ -556,9 +555,9 @@
     yield from ring_scatter(
         wires,
         lambda j: down_part.at[:, j, :, pl.ds(0, DOWN_SPLIT)],
-        r["down_sum"].at[c],
-        r["down_left"].at[c],
-        r["down_right"].at[c],
+        r[f"down_sum_{c}"],
+        r[f"down_left_{c}"],
+        r[f"down_right_{c}"],
         NY,
         at.y,
         at.along_y,
@@ -571,7 +570,7 @@
     return (values * lax.rsqrt(mean_square + epsilon) * gain).astype(BF16)
 
 
-WEIGHTS = ("key", "value", "query", "out", "gate", "up", "down")
+WEIGHTS = ("out", "key", "value", "query", "gate", "up", "down")
 
 
 def layer_kernel(names, *refs):
@@ -579,7 +578,6 @@
     at = Place()
     qkv_wires, wires = Wires(r["send"], r["recv"]), Wires(r["send"], r["recv_2"])
     steps = Steps()
-    out_wires = wires
     tokens = r["tokens"]
     local_rows, model = tokens.shape
     attended, mixed = r["streams"].at[0], r["streams"].at[1]
@@ -590,10 +588,16 @@
     greeted = greet_group("cp", CP, at.cp) + greet_group("tp", TP, at.tp)
     loads = {}
     for n, name in enumerate(WEIGHTS):
-        loads[name] = pltpu.make_async_copy(
-            r[name + "_weight"], r[name], r["load"].at[n]
-        )
+        held = r["out"].at[at.y] if name == "out" else r[name]
+        loads[name] = pltpu.make_async_copy(r[name + "_weight"], held, r["load"].at[n])
         loads[name].start()
+
+    block = cos.shape[0]
+    positions = at.cp * block + lax.broadcasted_iota(jnp.int32, (block, HD), 0)
+    angles = positions.astype(F32) * r["inverse"][...]
+    first_half = lax.broadcasted_iota(jnp.int32, (block, HD), 1) < HD // 2
+    cos[...] = jnp.cos(angles)
+    sin[...] = jnp.where(first_half, -jnp.sin(angles), jnp.sin(angles))
 
     normed = normalize(tokens[...].astype(F32), r["attention_gain"][...])
     slices, got, columns = r["slices"], r["got"], r["columns"]
@@ -604,7 +608,17 @@
     await_greetings(greeted)
 
     phase("spread_cp")
+    weight_wires = Wires(r["send_w"], r["recv_w"])
+    weight_ring = ring_gather(weight_wires, lambda j: r["out"].at[j], NY, at.y, at.along_y)
+    weight_flights = []
+
+    def out_weights():
+        yield weight_flights
+        yield advance(weight_ring)
+
     def keep_slice():
+        loads["out"].wait()
+        weight_flights.extend(advance(weight_ring))
         got[at.cp] = slices[at.cp]
 
     exchange(
@@ -656,10 +670,14 @@
     loads["query"].wait()
     product_into(part, x, r["query"], 2 * HD)
     phase("qkv_sum")
-    for n in range(1, len(QKV_PARTS)):
-        steps.add(unit(n, summed, QKV_PARTS, part, "q"), "kabc"[n])
-    steps.play(QKV_ORDER)
-    steps.run()
+    def query_part(letter):
+        n = "KABC".index(letter)
+        steps.add(unit(n, summed, QKV_PARTS, part, "q"), letter.lower())
+
+    steps.play("C", query_part)
+    steps.add(out_weights(), "o")
+    steps.play(QKV_ORDER, query_part)
+    steps.begun.clear()
     qkv_wires.drain()
 
     phase("attend")
@@ -684,60 +702,62 @@
     mean = jnp.dot(weights.astype(BF16), values, preferred_element_type=F32) / total
     mean = mean.astype(BF16)
     for h in range(heads):
-        every[at.z, at.y, :, h * HD : (h + 1) * HD] = mean[h * block : (h + 1) * block]
+        every[at.z, :, h * HD : (h + 1) * HD] = mean[h * block : (h + 1) * block]
 
     phase("gather_att")
-    out_part, out_got, out_total, projected = (
-        r["out_part"],
-        r["out_got"],
-        r["out_total"],
-        r["projected"],
-    )
-    loads["out"].wait()
-    owners = []
+    projected = r["projected"]
+    owners, seen = [], set()
 
     def out_chunk(c):
-        p = jnp.dot(chunk_rows(every, at, OUT_CHUNKS[c]), r["out"][...], preferred_element_type=F32)
-        blocks = 2 * NY
-        for b in range(blocks):
-            for t in range(TP):
-                first = b * block + t * local_rows
-                out_part[c, t, b] = p[first : first + local_rows].astype(BF16)
+        chunk = OUT_CHUNKS[c]
+        part, arrived, total = r[f"out_part_{c}"], r[f"out_got_{c}"], r[f"out_total_{c}"]
+        x = jnp.concatenate([every[(at.z + off) % NZ] for off in chunk], axis=0)
+        for y in range(NY):
+            p = jnp.dot(x, r["out"][y], preferred_element_type=F32)
+            for n in range(len(chunk)):
+                for t in range(TP):
+                    first = n * block + t * local_rows
+                    part[t, n, :, y * width : (y + 1) * width] = p[
+                        first : first + local_rows
+                    ].astype(BF16)
         copies = []
         for off in range(1, TP):
             to = (at.tp + off) % TP
-            copies.append(out_wires.copy(out_part.at[c, to], out_got.at[c, at.tp], {"tp": to}))
-        out_got[c, at.tp] = out_part[c, at.tp]
+            copies.append(wires.copy(part.at[to], arrived.at[at.tp], {"tp": to}))
+        arrived[at.tp] = part[at.tp]
         yield copies
-
-        def sum_part(b, carry):
-            parts = out_got[c, 0, b].astype(F32)
+        for n, off in enumerate(chunk):
+            sums = arrived[0, n].astype(F32)
             for t in range(1, TP):
-                parts = parts + out_got[c, t, b].astype(F32)
-            out_total[c, b] = parts.astype(BF16)
-            return carry
-
-        lax.fori_loop(0, blocks, sum_part, 0)
-        for n, off in enumerate(OUT_CHUNKS[c]):
-            for turn in range(NY):
-                y = (at.y + turn) % NY
-                source = out_total.at[c, n * NY + y]
-                if off == 0 and turn == 0:
-                    projected[at.cp] = source[...]
-                else:
-                    to = {"cp": (at.z + off) % NZ * NY + y}
-                    owners.append(out_wires.copy(source, projected.at[at.cp], to))
-
-    gather_rows(wires, steps, at, every, GATHER_SPLIT, OUT_CHUNKS, out_chunk)
+                sums = sums + arrived[t, n].astype(F32)
+            total[n] = sums.astype(BF16)
+            if off == 0:
+                projected[at.z] = total[n]
+            else:
+                to = at.along_z((at.z + off) % NZ)
+                owners.append(wires.copy(total.at[n], projected.at[at.z], to))
+
+    def att_there(off):
+        seen.add(off)
+        for c, chunk in OUT_CHUNKS.items():
+            if off in chunk and seen >= set(chunk):
+                steps.play("o2", None)
+                steps.add(out_chunk(c), f"out{c}")
+
+    steps.add(
+        far_gather(wires, lambda i: every.at[i], NZ, at.z, at.along_z, att_there), "z"
+    )
     steps.run()
     phase("out_cp")
     for c in owners:
         c.wait_recv()
     wires.drain()
+    weight_wires.drain()
     phase("norm_feed")
-    for c in range(CP):
-        cols = slice(c * width, (c + 1) * width)
-        attended[:, cols] = (tokens[:, cols].astype(F32) + projected[c].astype(F32)).astype(BF16)
+    wide = projected.shape[-1]
+    for z in range(NZ):
+        cols = slice(z * wide, (z + 1) * wide)
+        attended[:, cols] = (tokens[:, cols].astype(F32) + projected[z].astype(F32)).astype(BF16)
 
     normed = normalize(attended[...].astype(F32), r["feed_gain"][...])
     by_width, got_width, stream = r["by_width"], r["got_width"], r["stream"]
@@ -766,13 +786,18 @@
     for name in ("gate", "up", "down"):
         loads[name].wait()
     reduced = r["reduced"]
-    places = {off: (c, n) for c, chunk in enumerate(CHUNKS) for n, off in enumerate(chunk)}
+    places = {off: (c, n) for c, chunk in CHUNKS.items() for n, off in enumerate(chunk)}
+
+    def piece(name, off):
+        c, n = places[off]
+        return r[f"{name}_{c}"].at[n]
+
     def to_z(off):
         return at.along_z((at.z + off) % NZ)
 
     lines = FarScatter(
         qkv_wires,
-        lambda off: r["down_sum"].at[places[off]],
+        lambda off: piece("down_sum", off),
         reduced.at[:, pl.ds(0, DOWN_SPLIT)],
         r["down_far"],
         to_z,
@@ -780,7 +805,7 @@
     rest = pl.ds(DOWN_SPLIT, reduced.shape[1] - DOWN_SPLIT)
     z_lines = FarScatter(
         qkv_wires,
-        lambda off: r["down_part"].at[*places[off], :, :, rest],
+        lambda off: piece("down_part", off).at[:, :, rest],
         r["z_sum"],
         r["z_far"],
         to_z,
@@ -821,19 +846,19 @@
         if letter in later:
             gen = later[letter]()
         else:
-            gen = feed_chunk(qkv_wires, at, r, "ABCD".index(letter), produced, finished)
+            assert letter.lower() in there
+            gen = feed_chunk(qkv_wires, at, r, letter.lower(), produced, finished)
         steps.add(gen, letter.lower())
 
     def chunk_there(c):
         there[c] = True
-        if c == 0:
-            begin("A")
         return iter(())
 
     gather_rows(qkv_wires, steps, at, stream, GATHER_SPLIT, CHUNKS, chunk_there)
-    steps.run(lambda: len(there) == len(CHUNKS))
+    steps.play(GATHER_ORDER, begin)
+    assert len(there) == len(CHUNKS)
     steps.play(ORDER, begin)
-    steps.run()
+    assert not steps.queue
     phase("swap2")
     qkv_wires.drain()
     by_token, lowered = r["by_token"], r["lowered"]
@@ -861,7 +886,7 @@
 
 VMEM = pl.BlockSpec(memory_space=pltpu.VMEM)
 ANY = pl.BlockSpec(memory_space=pl.ANY)
-COPIES, COPIES_2 = 140, 111
+COPIES, COPIES_2, SLOTS = 157, CP, 48
 
 
 def dma(count):
@@ -886,19 +911,15 @@
     qkv = query_weight.shape[1] + key_weight.shape[1] + value_weight.shape[1]
     units = gate_weight.shape[1]
     wide, width = model // TP, model // CP
-    chunks = len(CHUNKS)
-
-    inverse = rope_base ** (-(jnp.arange(HD // 2, dtype=F32) * 2.0 / HD))
-    positions = lax.axis_index("cp") * block + jnp.arange(block, dtype=jnp.int32)
-    angles = positions.astype(F32)[:, None] * inverse[None, :]
-    cosine, sine = jnp.cos(angles), jnp.sin(angles)
+
+    pair = jnp.arange(HD, dtype=F32)[None] % (HD // 2)
+    inverse = rope_base ** (-(pair * 2.0 / HD))
 
     inputs = {
         "tokens": tokens,
         "attention_gain": attention_gain[None],
         "feed_gain": feed_gain[None],
-        "cos": jnp.concatenate([cosine, cosine], axis=1),
-        "sin": jnp.concatenate([-sine, sine], axis=1),
+        "inverse": inverse,
         "key_weight": key_weight,
         "value_weight": value_weight,
         "query_weight": query_weight,
@@ -913,6 +934,8 @@
 
     scratch = {name: buf(*inputs[name + "_weight"].shape) for name in WEIGHTS}
     scratch |= {
+        "cos": buf(block, HD, kind=F32),
+        "sin": buf(block, HD, kind=F32),
         "slices": buf(CP, local_rows, width),
         "got": buf(CP, local_rows, width),
         "columns": buf(TP, CP, local_rows, width),
@@ -920,24 +943,11 @@
         "qkv_part": buf(NZ, NY, block, qkv),
         "summed": buf(block, qkv, kind=F32),
         "shared": buf(NZ, NY, block, 2 * HD),
-        "every": buf(NZ, NY, block, wide),
-        "out_part": buf(chunks, TP, CP // chunks, local_rows, width),
-        "out_got": buf(chunks, TP, CP // chunks, local_rows, width),
-        "out_total": buf(chunks, CP // chunks, local_rows, width),
-        "projected": buf(CP, local_rows, width),
+        "every": buf(NZ, block, wide),
+        "projected": buf(NZ, local_rows, wide),
         "by_width": buf(TP, local_rows, wide),
         "got_width": buf(TP, local_rows, wide),
         "stream": buf(NZ, NY, block, wide),
-        "unit_part": buf(chunks, 2, NY, block, 2 * units),
-        "held": buf(chunks, NX, block, 2 * units),
-        "from_left": buf(chunks, NX // 2, block, 2 * units),
-        "from_right": buf(chunks, NX // 2, block, 2 * units),
-        "unit_total": buf(chunks, block, 2 * units, kind=F32),
-        "hidden": buf(chunks, 2, NX, block, units),
-        "down_part": buf(chunks, 2, NY, block, wide),
-        "down_left": buf(chunks, NY // 2, 2, block, DOWN_SPLIT),
-        "down_right": buf(chunks, NY // 2, 2, block, DOWN_SPLIT),
-        "down_sum": buf(chunks, 2, block, DOWN_SPLIT),
         "down_far": buf(8, block, DOWN_SPLIT),
         "z_far": buf(8, NY, block, wide - DOWN_SPLIT),
         "z_sum": buf(NY, block, wide - DOWN_SPLIT),
@@ -947,10 +957,31 @@
         "by_token": buf(TP, local_rows, wide),
         "lowered": buf(TP, local_rows, wide),
     }
+    scratch["out"] = buf(NY, *out_weight.shape)
+    for c, chunk in OUT_CHUNKS.items():
+        scratch |= {
+            f"out_part_{c}": buf(TP, len(chunk), local_rows, wide),
+            f"out_got_{c}": buf(TP, len(chunk), local_rows, wide),
+            f"out_total_{c}": buf(len(chunk), local_rows, wide),
+        }
+    for c, chunk in CHUNKS.items():
+        n, half = len(chunk), block // 2
+        scratch |= {
+            f"unit_part_{c}": buf(n, NX, 2, half, 2 * units),
+            f"held_{c}": buf(n, NX, half, 2 * units),
+            f"from_left_{c}": buf(NX // 2, n, half, 2 * units),
+            f"from_right_{c}": buf(NX // 2, n, half, 2 * units),
+            f"unit_total_{c}": buf(n, half, 2 * units, kind=F32),
+            f"hidden_{c}": buf(n, NX, 2, half, units),
+            f"down_part_{c}": buf(n, NY, block, wide),
+            f"down_left_{c}": buf(NY // 2, n, block, DOWN_SPLIT),
+            f"down_right_{c}": buf(NY // 2, n, block, DOWN_SPLIT),
+            f"down_sum_{c}": buf(n, block, DOWN_SPLIT),
+        }
     scratch |= scatter_scratch("q", QKV_PARTS, block)
     scratch |= {f"r{n}": dma(TP) for n in range(2)}
-    scratch |= {"load": dma(len(WEIGHTS)), "send": dma(COPIES), "recv": dma(COPIES)}
-    scratch |= {"recv_2": dma(COPIES_2)}
+    scratch |= {"load": dma(len(WEIGHTS)), "send": dma(SLOTS), "recv": dma(COPIES)}
+    scratch |= {"recv_2": dma(COPIES_2), "send_w": dma(4), "recv_w": dma(4)}
 
     names = (*inputs, "streams", *scratch)
     streams = pl.pallas_call(

time: 173 us -> 163 us (0.942)
  Pallas kernels: 170 us -> 160 us
    pallas_call x1, Pallas kernels: 170 us -> 160 us  [on_device(): pl.pallas_call(functools.partial(layer_kernel, names), out_shape=jax.Shap...]
where the time goes in v5:
time: 163 us
  Pallas kernels  160 us (98%)
    pallas_call x1, Pallas kernels, on_device(): pl.pallas_call(functools.partial(layer_kernel, names), out_shape=jax.Shap...  160 us

profile of v5, /device:TPU:1, one launch (start us, length us, event | category | flops | bytes accessed | tf_op | source)
XLA Modules:
  0.0 162.8 jit_solution(2039342621165557312)
XLA Ops:
  0.6 0.5 fusion.2.refs_3_
  1.2 160.1 %layer.1 = bf16[2,4,8192]{2,1,0:T(4,128)(2,1)} custom-call(bf16[4,8192]{1,0:T(4,128)(2,1)} %refs_0_.1, f32[1,8192]{1,0:T(1,128)} %bitcast.6, f32[1,8192]{1,0:T(1,128)} %bitcast.7, f32[1,128]{1,0:T(1,128)} %fusion.2.refs_3_, bf16[256,128]{1,0:T(8,128)(2,1)} %refs_4_.1, bf16[256,128]{1,0:T(8,128)(2,1)} %refs_5_.1, bf16[256,1024]{1,0:T(8,128)(2,1)} %refs_6_.1, ...), custom_call_target="tpu_custom_call" | custom-call | tf_op jit(solution)/shard_map/layer/pallas_call | solution.py:987
  161.2 1.6 slice_bitcast_fusion

commit v6 on v5

--- a/solution.py
+++ b/solution.py
@@ -331,7 +331,7 @@
             dst_ref=target(me),
             send_sem=send_sem.at[off],
             recv_sem=recv_sem.at[off],
-            device_id={axis: peer},
+            device_id=axis(peer) if callable(axis) else {axis: peer},
             device_id_type=MESH,
         )
 
@@ -349,9 +349,8 @@
     lax.fori_loop(1, n, wait, 0)
 
 
-Z_FIRST, Y_FIRST = "z", "y"
-QKV_PARTS = ((0, 256, Y_FIRST), (256, 256, Y_FIRST), (512, 384, Y_FIRST), (896, 384, Z_FIRST))
-QKV_ORDER = "k1 A B k2 c1 a1 k3 b1 a2 c2 k4 a3 b2 c3 a4 c4 b3 k5 o1 b4 k6"
+QKV_PARTS = ((0, 256), (256, 512), (768, 512))
+QKV_ORDER = "g2 K k1 q1 O p2 A k2 q2 B a1 k3 b1 o1 H a2 b2 k4"
 GATHER_SPLIT = 768
 DOWN_SPLIT = 768
 
@@ -415,76 +414,6 @@
         yield Now([copies[off]])
         to_y(ref.at[(at.z + NZ - off) % NZ, at.y])
     yield handed
-
-
-def scatter_part(wires, at, part, out, columns, way, bufs):
-    if way == Z_FIRST:
-        z_bufs, y_left, y_right, y_sum = bufs
-        yield from far_scatter(
-            wires, lambda i: part.at[i, :, :, columns], y_sum, z_bufs, NZ, at.z, at.along_z
-        )
-        yield from ring_scatter(
-            wires,
-            lambda j: y_sum.at[j],
-            out.at[:, columns],
-            y_left,
-            y_right,
-            NY,
-            at.y,
-            at.along_y,
-        )
-    else:
-        z_bufs, y_left, y_right, z_sum = bufs
-        yield from ring_scatter(
-            wires,
-            lambda j: part.at[:, j, :, columns],
-            z_sum,
-            y_left,
-            y_right,
-            NY,
-            at.y,
-            at.along_y,
-        )
-        yield from far_scatter(
-            wires, lambda i: z_sum.at[i], out.at[:, columns], z_bufs, NZ, at.z, at.along_z
-        )
-
-
-def scatter_scratch(prefix, parts, rows):
-    scratch = {}
-    for n, (_, width, way) in enumerate(parts):
-        if way == Z_FIRST:
-            shapes = (
-                (NZ, NY, rows, width),
-                (NY // 2, rows, width),
-                (NY // 2, rows, width),
-                (NY, rows, width),
-            )
-        else:
-            shapes = (
-                (NZ, rows, width),
-                (NY // 2, NZ, rows, width),
-                (NY // 2, NZ, rows, width),
-                (NZ, rows, width),
-            )
-        for m, shape in enumerate(shapes):
-            scratch[f"{prefix}{n}{m}"] = pltpu.VMEM(shape, BF16)
-    return scratch
-
-
-def product_into(part, x, w_ref, start):
-    width = w_ref.shape[1]
-    tile = min(width, 256)
-
-    def body(i, carry):
-        at = pl.multiple_of(i * tile, tile)
-        p = jnp.dot(x(), w_ref[:, pl.ds(at, tile)], preferred_element_type=F32)
-        part[:, :, :, pl.ds(pl.multiple_of(start + at, 128), tile)] = p.astype(BF16).reshape(
-            *part.shape[:3], tile
-        )
-        return carry
-
-    lax.fori_loop(0, width // tile, body, 0)
 
 
 def chunk_rows(ref, at, chunk):
@@ -570,7 +499,8 @@
     return (values * lax.rsqrt(mean_square + epsilon) * gain).astype(BF16)
 
 
-WEIGHTS = ("out", "key", "value", "query", "gate", "up", "down")
+WEIGHTS = ("key", "value", "query", "out", "gate", "up", "down")
+ALONG_Y = ("key", "value", "query", "out")
 
 
 def layer_kernel(names, *refs):
@@ -588,7 +518,7 @@
     greeted = greet_group("cp", CP, at.cp) + greet_group("tp", TP, at.tp)
     loads = {}
     for n, name in enumerate(WEIGHTS):
-        held = r["out"].at[at.y] if name == "out" else r[name]
+        held = r[name].at[at.y] if name in ALONG_Y else r[name]
         loads[name] = pltpu.make_async_copy(r[name + "_weight"], held, r["load"].at[n])
         loads[name].start()
 
@@ -601,29 +531,45 @@
 
     normed = normalize(tokens[...].astype(F32), r["attention_gain"][...])
     slices, got, columns = r["slices"], r["got"], r["columns"]
-    width = slices.shape[-1]
-    for c in range(CP):
-        slices[c] = normed[:, c * width : (c + 1) * width]
+    wide = slices.shape[-1]
+    for z in range(NZ):
+        slices[z] = normed[:, z * wide : (z + 1) * wide]
     phase("barrier")
     await_greetings(greeted)
 
     phase("spread_cp")
     weight_wires = Wires(r["send_w"], r["recv_w"])
-    weight_ring = ring_gather(weight_wires, lambda j: r["out"].at[j], NY, at.y, at.along_y)
-    weight_flights = []
-
-    def out_weights():
-        yield weight_flights
-        yield advance(weight_ring)
+    query_cols, out_cols = r["query"].shape[-1] // 2, r["out"].shape[-1] // 2
+
+    def gathered(*blocks):
+        rings = [ring_gather(weight_wires, b, NY, at.y, at.along_y) for b in blocks]
+        while True:
+            flights = [advance(g) for g in rings]
+            if flights[0] is None:
+                return
+            yield [c for some in flights for c in some]
+
+    weight_parts = {
+        "G": lambda: gathered(lambda j: r["key"].at[j], lambda j: r["value"].at[j]),
+        "P": lambda: gathered(lambda j: r["query"].at[j, :, pl.ds(0, query_cols)]),
+        "Q": lambda: gathered(lambda j: r["query"].at[j, :, pl.ds(query_cols, query_cols)]),
+        "O": lambda: gathered(lambda j: r["out"].at[j, :, pl.ds(0, out_cols)]),
+        "H": lambda: gathered(lambda j: r["out"].at[j, :, pl.ds(out_cols, out_cols)]),
+    }
+
+    def begin_weights(letter):
+        steps.add(weight_parts[letter](), letter.lower())
 
     def keep_slice():
-        loads["out"].wait()
-        weight_flights.extend(advance(weight_ring))
-        got[at.cp] = slices[at.cp]
+        for name in ALONG_Y:
+            loads[name].wait()
+        steps.play("G P", begin_weights)
+        got[at.z] = slices[at.z]
 
     exchange(
-        r["send"], r["recv_2"], lambda p: slices.at[p], lambda p: got.at[p], "cp", CP, at.cp, keep_slice
-    )
+        r["send"], r["recv_2"], lambda p: slices.at[p], lambda p: got.at[p], at.along_z, NZ, at.z, keep_slice
+    )
+    steps.play("g1 Q", begin_weights)
 
     phase("spread_tp")
     def keep_columns():
@@ -640,43 +586,56 @@
         rows_in[b] = jnp.concatenate(parts, axis=0).astype(BF16)
         return carry
 
-    lax.fori_loop(0, CP, in_order, 0)
+    steps.play("p1", begin_weights)
+    lax.fori_loop(0, NZ, in_order, 0)
 
     part, summed, shared = r["qkv_part"], r["summed"], r["shared"]
 
-    def x():
-        return rows_in[...].reshape(-1, width)
+    def product(name, cols, start):
+        x = rows_in[...].reshape(-1, wide)
+        w = r[name][:, :, cols].reshape(wide, -1)
+        p = jnp.dot(x, w, preferred_element_type=F32)
+        part[:, :, start : start + p.shape[1]] = p.astype(BF16).reshape(NZ, block, -1)
 
     def turned(v):
         return (v * cos[...] + pltpu.roll(v, HD // 2, 1) * sin[...]).astype(BF16)
 
-    def unit(n, out, parts, partial, prefix):
-        start, extent, way = parts[n]
-        bufs = [r[f"{prefix}{n}{m}"] for m in range(4)]
-        return scatter_part(qkv_wires, at, partial, out, pl.ds(start, extent), way, bufs)
+    def unit(n):
+        start, extent = QKV_PARTS[n]
+        cols = pl.ds(start, extent)
+        return far_scatter(
+            qkv_wires,
+            lambda i: part.at[i, :, cols],
+            summed.at[:, cols],
+            r[f"sum_{n}"],
+            NZ,
+            at.z,
+            at.along_z,
+        )
 
     def keys_and_values():
-        yield from unit(0, summed, QKV_PARTS, part, "q")
+        yield from unit(0)
         shared[at.z, at.y, :, pl.ds(0, HD)] = turned(summed[:, pl.ds(0, HD)])
         shared[at.z, at.y, :, pl.ds(HD, HD)] = summed[:, pl.ds(HD, HD)].astype(BF16)
         yield from gather_small(qkv_wires, at, shared)
 
-    phase("qkv")
-    loads["key"].wait()
-    loads["value"].wait()
-    product_into(part, x, r["key"], 0)
-    product_into(part, x, r["value"], HD)
-    steps.add(keys_and_values(), "k")
-    loads["query"].wait()
-    product_into(part, x, r["query"], 2 * HD)
+    def begin_part(letter):
+        if letter == "K":
+            product("key", slice(None), 0)
+            product("value", slice(None), HD)
+            steps.add(keys_and_values(), "k")
+        elif letter in "AB":
+            n = "KAB".index(letter)
+            start, extent = QKV_PARTS[n]
+            for col in range(0, extent, 256):
+                at_col = start - 2 * HD + col
+                product("query", slice(at_col, at_col + 256), start + col)
+            steps.add(unit(n), letter.lower())
+        else:
+            begin_weights(letter)
+
     phase("qkv_sum")
-    def query_part(letter):
-        n = "KABC".index(letter)
-        steps.add(unit(n, summed, QKV_PARTS, part, "q"), letter.lower())
-
-    steps.play("C", query_part)
-    steps.add(out_weights(), "o")
-    steps.play(QKV_ORDER, query_part)
+    steps.play(QKV_ORDER, begin_part)
     steps.begun.clear()
     qkv_wires.drain()
 
@@ -712,12 +671,13 @@
         chunk = OUT_CHUNKS[c]
         part, arrived, total = r[f"out_part_{c}"], r[f"out_got_{c}"], r[f"out_total_{c}"]
         x = jnp.concatenate([every[(at.z + off) % NZ] for off in chunk], axis=0)
+        cols = r["out"].shape[-1]
         for y in range(NY):
             p = jnp.dot(x, r["out"][y], preferred_element_type=F32)
             for n in range(len(chunk)):
                 for t in range(TP):
                     first = n * block + t * local_rows
-                    part[t, n, :, y * width : (y + 1) * width] = p[
+                    part[t, n, :, y * cols : (y + 1) * cols] = p[
                         first : first + local_rows
                     ].astype(BF16)
         copies = []
@@ -741,12 +701,13 @@
         seen.add(off)
         for c, chunk in OUT_CHUNKS.items():
             if off in chunk and seen >= set(chunk):
-                steps.play("o2", None)
+                steps.play("o2 h1 h2", None)
                 steps.add(out_chunk(c), f"out{c}")
 
     steps.add(
         far_gather(wires, lambda i: every.at[i], NZ, at.z, at.along_z, att_there), "z"
     )
+    steps.play("h1 z/1 z/2", None)
     steps.run()
     phase("out_cp")
     for c in owners:
@@ -910,7 +871,7 @@
     rows = block * CP
     qkv = query_weight.shape[1] + key_weight.shape[1] + value_weight.shape[1]
     units = gate_weight.shape[1]
-    wide, width = model // TP, model // CP
+    wide = model // TP
 
     pair = jnp.arange(HD, dtype=F32)[None] % (HD // 2)
     inverse = rope_base ** (-(pair * 2.0 / HD))
@@ -936,11 +897,11 @@
     scratch |= {
         "cos": buf(block, HD, kind=F32),
         "sin": buf(block, HD, kind=F32),
-        "slices": buf(CP, local_rows, width),
-        "got": buf(CP, local_rows, width),
-        "columns": buf(TP, CP, local_rows, width),
-        "rows_in": buf(CP, block, width),
-        "qkv_part": buf(NZ, NY, block, qkv),
+        "slices": buf(NZ, local_rows, wide),
+        "got": buf(NZ, local_rows, wide),
+        "columns": buf(TP, NZ, local_rows, wide),
+        "rows_in": buf(NZ, block, wide),
+        "qkv_part": buf(NZ, block, qkv),
         "summed": buf(block, qkv, kind=F32),
         "shared": buf(NZ, NY, block, 2 * HD),
         "every": buf(NZ, block, wide),
@@ -957,7 +918,8 @@
         "by_token": buf(TP, local_rows, wide),
         "lowered": buf(TP, local_rows, wide),
     }
-    scratch["out"] = buf(NY, *out_weight.shape)
+    for name in ALONG_Y:
+        scratch[name] = buf(NY, *inputs[name + "_weight"].shape)
     for c, chunk in OUT_CHUNKS.items():
         scratch |= {
             f"out_part_{c}": buf(TP, len(chunk), local_rows, wide),
@@ -978,10 +940,11 @@
             f"down_right_{c}": buf(NY // 2, n, block, DOWN_SPLIT),
             f"down_sum_{c}": buf(n, block, DOWN_SPLIT),
         }
-    scratch |= scatter_scratch("q", QKV_PARTS, block)
+    for n, (_, extent) in enumerate(QKV_PARTS):
+        scratch[f"sum_{n}"] = buf(NZ, block, extent)
     scratch |= {f"r{n}": dma(TP) for n in range(2)}
     scratch |= {"load": dma(len(WEIGHTS)), "send": dma(SLOTS), "recv": dma(COPIES)}
-    scratch |= {"recv_2": dma(COPIES_2), "send_w": dma(4), "recv_w": dma(4)}
+    scratch |= {"recv_2": dma(COPIES_2), "send_w": dma(24), "recv_w": dma(24)}
 
     names = (*inputs, "streams", *scratch)
     streams = pl.pallas_call(

time: 163 us -> 153 us (0.939)
  Pallas kernels: 160 us -> 151 us
    pallas_call x1, Pallas kernels: 160 us -> 151 us  [on_device(): pl.pallas_call(functools.partial(layer_kernel, names), out_shape=jax.Shap...]
where the time goes in v6:
time: 153 us
  Pallas kernels  151 us (99%)
  local copies, waits for them, and re-layouts  1.57 us (1%)
    pallas_call x1, Pallas kernels, on_device(): pl.pallas_call(functools.partial(layer_kernel, names), out_shape=jax.Shap...  151 us

profile of v6, /device:TPU:1, one launch (start us, length us, event | category | flops | bytes accessed | tf_op | source)
XLA Modules:
  0.0 153.3 jit_solution(9899210244369750487)
XLA Ops:
  0.6 0.5 fusion.2.refs_3_
  1.2 150.5 %layer.1 = bf16[2,4,8192]{2,1,0:T(4,128)(2,1)} custom-call(bf16[4,8192]{1,0:T(4,128)(2,1)} %refs_0_.1, f32[1,8192]{1,0:T(1,128)} %bitcast.6, f32[1,8192]{1,0:T(1,128)} %bitcast.7, f32[1,128]{1,0:T(1,128)} %fusion.2.refs_3_, bf16[256,128]{1,0:T(8,128)(2,1)} %refs_4_.1, bf16[256,128]{1,0:T(8,128)(2,1)} %refs_5_.1, bf16[256,1024]{1,0:T(8,128)(2,1)} %refs_6_.1, ...), custom_call_target="tpu_custom_call" | custom-call | tf_op jit(solution)/shard_map/layer/pallas_call | solution.py:950
  151.7 1.6 %slice_bitcast_fusion = (bf16[4,8192]{1,0:T(4,128)(2,1)}, bf16[4,8192]{1,0:T(4,128)(2,1)}) fusion(bf16[2,4,8192]{2,1,0:T(4,128)(2,1)} %layer.1), kind=kLoop, calls=%fused_computation | loop fusion | bytes 262144 | tf_op jit(solution)/shard_map/squeeze | solution.py:963

commit v7 on v6

--- a/solution.py
+++ b/solution.py
@@ -3,6 +3,7 @@
 
 import jax
 import jax.numpy as jnp
+import numpy as np
 from jax import lax
 from jax.experimental import pallas as pl
 from jax.experimental.pallas import tpu as pltpu
@@ -352,10 +353,10 @@
 QKV_PARTS = ((0, 256), (256, 512), (768, 512))
 QKV_ORDER = "g2 K k1 q1 O p2 A k2 q2 B a1 k3 b1 o1 H a2 b2 k4"
 GATHER_SPLIT = 768
-DOWN_SPLIT = 768
-
-
-CHUNKS = {"e": (0,), "b": (2, 6), "c": (3, 4), "d": (5,), "a": (1, 7)}
+DOWN_SPLIT = 640
+
+
+CHUNKS = {"e": (0,), "b": (1, 7), "c": (3, 4), "d": (5,), "a": (2, 6)}
 OUT_CHUNKS = {0: (0, 7, 1, 6, 2), 1: (5, 3, 4)}
 
 
@@ -421,8 +422,8 @@
     return jnp.concatenate([b.reshape(-1, b.shape[-1]) for b in blocks], axis=0)
 
 
-GATHER_ORDER = """yz/1 y0/1 z/1 yz/2 y0/2 E y7/1 y1/1 e1 y6/1 y2/1 z/2 yz/3 y7/2 e2 y1/2 y6/2 y2/2 B y5/1 y3/1 y4/1 yz/4 b1 e3 y5/2 y3/2 e4 y4/2"""
-ORDER = """b2 C D c1 d1 A b3 a1 c2 d2 b4 e5 a2 c3 d3 b5 e6 a3 b6 c4 d4 e7 a4 c5 c6 b7 d5 d6 a5 a6 e8 b8 c7 V v1 W w1 d7 a7 c8 d8 T U a8 N n1 t1 u1 n2 L l1 n3"""
+GATHER_ORDER = """yz/1 y0/1 z/1 yz/2 y0/2 E y7/1 y1/1 e1 y6/1 y2/1 z/2 yz/3 y7/2 y1/2 B e2 y6/2 y2/2 b1 y5/1 y3/1 y4/1 yz/4 e3 y5/2 y3/2 y4/2"""
+ORDER = """b2 C e4 D A c1 d1 a1 b3 e5 c2 d2 a2 b4 c3 d3 b5 e6 a3 b6 c4 d4 e7 a4 c5 c6 b7 d5 d6 a5 a6 e8 b8 c7 V v1 W w1 d7 a7 c8 d8 a8 T U N n1 t1 u1 n2 L l1 n3"""
 
 
 def feed_chunk(wires, at, r, c, produced, finished):
@@ -500,6 +501,7 @@
 
 
 WEIGHTS = ("key", "value", "query", "out", "gate", "up", "down")
+SMALL = ("tokens", "attention_gain", "feed_gain")
 ALONG_Y = ("key", "value", "query", "out")
 
 
@@ -508,7 +510,7 @@
     at = Place()
     qkv_wires, wires = Wires(r["send"], r["recv"]), Wires(r["send"], r["recv_2"])
     steps = Steps()
-    tokens = r["tokens"]
+    tokens = r["tokens_held"]
     local_rows, model = tokens.shape
     attended, mixed = r["streams"].at[0], r["streams"].at[1]
     cos, sin = r["cos"], r["sin"]
@@ -517,6 +519,10 @@
     phase("greet")
     greeted = greet_group("cp", CP, at.cp) + greet_group("tp", TP, at.tp)
     loads = {}
+    for n, name in enumerate(SMALL):
+        held = r[name + "_held"]
+        loads[name] = pltpu.make_async_copy(r[name], held, r["load"].at[len(WEIGHTS) + n])
+        loads[name].start()
     for n, name in enumerate(WEIGHTS):
         held = r[name].at[at.y] if name in ALONG_Y else r[name]
         loads[name] = pltpu.make_async_copy(r[name + "_weight"], held, r["load"].at[n])
@@ -529,7 +535,9 @@
     cos[...] = jnp.cos(angles)
     sin[...] = jnp.where(first_half, -jnp.sin(angles), jnp.sin(angles))
 
-    normed = normalize(tokens[...].astype(F32), r["attention_gain"][...])
+    for name in SMALL:
+        loads[name].wait()
+    normed = normalize(tokens[...].astype(F32), r["attention_gain_held"][...])
     slices, got, columns = r["slices"], r["got"], r["columns"]
     wide = slices.shape[-1]
     for z in range(NZ):
@@ -720,7 +728,7 @@
         cols = slice(z * wide, (z + 1) * wide)
         attended[:, cols] = (tokens[:, cols].astype(F32) + projected[z].astype(F32)).astype(BF16)
 
-    normed = normalize(attended[...].astype(F32), r["feed_gain"][...])
+    normed = normalize(attended[...].astype(F32), r["feed_gain_held"][...])
     by_width, got_width, stream = r["by_width"], r["got_width"], r["stream"]
     wide = by_width.shape[-1]
     for t in range(TP):
@@ -873,14 +881,14 @@
     units = gate_weight.shape[1]
     wide = model // TP
 
-    pair = jnp.arange(HD, dtype=F32)[None] % (HD // 2)
-    inverse = rope_base ** (-(pair * 2.0 / HD))
+    pair = np.arange(HD, dtype=np.float32)[None] % (HD // 2)
+    inverse = (np.float64(rope_base) ** (-(pair * 2.0 / HD))).astype(np.float32)
 
     inputs = {
         "tokens": tokens,
         "attention_gain": attention_gain[None],
         "feed_gain": feed_gain[None],
-        "inverse": inverse,
+        "inverse": jnp.asarray(inverse),
         "key_weight": key_weight,
         "value_weight": value_weight,
         "query_weight": query_weight,
@@ -918,6 +926,8 @@
         "by_token": buf(TP, local_rows, wide),
         "lowered": buf(TP, local_rows, wide),
     }
+    for name in SMALL:
+        scratch[name + "_held"] = buf(*inputs[name].shape, kind=inputs[name].dtype)
     for name in ALONG_Y:
         scratch[name] = buf(NY, *inputs[name + "_weight"].shape)
     for c, chunk in OUT_CHUNKS.items():
@@ -943,14 +953,14 @@
     for n, (_, extent) in enumerate(QKV_PARTS):
         scratch[f"sum_{n}"] = buf(NZ, block, extent)
     scratch |= {f"r{n}": dma(TP) for n in range(2)}
-    scratch |= {"load": dma(len(WEIGHTS)), "send": dma(SLOTS), "recv": dma(COPIES)}
+    scratch |= {"load": dma(len(WEIGHTS) + len(SMALL)), "send": dma(SLOTS), "recv": dma(COPIES)}
     scratch |= {"recv_2": dma(COPIES_2), "send_w": dma(24), "recv_w": dma(24)}
 
     names = (*inputs, "streams", *scratch)
     streams = pl.pallas_call(
         functools.partial(layer_kernel, names),
         out_shape=jax.ShapeDtypeStruct((2, *tokens.shape), BF16),
-        in_specs=[ANY if name.endswith("_weight") else VMEM for name in inputs],
+        in_specs=[VMEM if name == "inverse" else ANY for name in inputs],
         out_specs=VMEM,
         scratch_shapes=list(scratch.values()),
         compiler_params=pltpu.CompilerParams(

time: 153 us -> 151 us (0.987)
  Pallas kernels: 151 us -> 149 us
where the time goes in v7:
time: 151 us
  Pallas kernels  149 us (99%)
  local copies, waits for them, and re-layouts  1.57 us (1%)
    pallas_call x1, Pallas kernels, on_device(): pl.pallas_call(functools.partial(layer_kernel, names), out_shape=jax.Shap...  149 us

profile of v7, /device:TPU:1, one launch (start us, length us, event | category | flops | bytes accessed | tf_op | source)
XLA Modules:
  0.0 151.3 jit_solution(15561924427827539131)
XLA Ops:
  0.6 149.1 %layer.1 = bf16[2,4,8192]{2,1,0:T(4,128)(2,1)} custom-call(bf16[4,8192]{1,0:T(4,128)(2,1)} %refs_0_.1, f32[1,8192]{1,0:T(1,128)} %bitcast.6, f32[1,8192]{1,0:T(1,128)} %bitcast.7, f32[1,128]{1,0:T(1,128)} %constant.2.clone.refs_3_, bf16[256,128]{1,0:T(8,128)(2,1)} %refs_4_.1, bf16[256,128]{1,0:T(8,128)(2,1)} %refs_5_.1, bf16[256,1024]{1,0:T(8,128)(2,1)} %refs_6_.1, ...), custom_call_target="tpu_custom_call" | custom-call | tf_op jit(solution)/shard_map/layer/pallas_call | solution.py:960
  149.7 1.6 %slice_bitcast_fusion = (bf16[4,8192]{1,0:T(4,128)(2,1)}, bf16[4,8192]{1,0:T(4,128)(2,1)}) fusion(bf16[2,4,8192]{2,1,0:T(4,128)(2,1)} %layer.1), kind=kLoop, calls=%fused_computation | loop fusion | bytes 262144 | tf_op jit(solution)/shard_map/squeeze | solution.py:973

commit v8 on v7

--- a/solution.py
+++ b/solution.py
@@ -423,7 +423,7 @@
 
 
 GATHER_ORDER = """yz/1 y0/1 z/1 yz/2 y0/2 E y7/1 y1/1 e1 y6/1 y2/1 z/2 yz/3 y7/2 y1/2 B e2 y6/2 y2/2 b1 y5/1 y3/1 y4/1 yz/4 e3 y5/2 y3/2 y4/2"""
-ORDER = """b2 C e4 D A c1 d1 a1 b3 e5 c2 d2 a2 b4 c3 d3 b5 e6 a3 b6 c4 d4 e7 a4 c5 c6 b7 d5 d6 a5 a6 e8 b8 c7 V v1 W w1 d7 a7 c8 d8 a8 T U N n1 t1 u1 n2 L l1 n3"""
+ORDER = """b2 C D A e4 c1 d1 a1 b3 c2 e5 d2 a2 b4 c3 d3 b5 e6 a3 b6 c4 d4 e7 a4 c5 c6 b7 d5 d6 a5 a6 b8 e8 c7 V v1 W w1 d7 a7 c8 d8 a8 T U N n1 t1 u1 n2 L l1"""
 
 
 def feed_chunk(wires, at, r, c, produced, finished):
@@ -512,7 +512,7 @@
     steps = Steps()
     tokens = r["tokens_held"]
     local_rows, model = tokens.shape
-    attended, mixed = r["streams"].at[0], r["streams"].at[1]
+    attended, mixed = r["held_out"].at[0], r["held_out"].at[1]
     cos, sin = r["cos"], r["sin"]
 
     phase = Phases()
@@ -728,6 +728,12 @@
         cols = slice(z * wide, (z + 1) * wide)
         attended[:, cols] = (tokens[:, cols].astype(F32) + projected[z].astype(F32)).astype(BF16)
 
+    leaving = [
+        pltpu.make_async_copy(r["held_out"].at[n], r["streams"].at[n], r["leave"].at[n])
+        for n in range(2)
+    ]
+    leaving[0].start()
+
     normed = normalize(attended[...].astype(F32), r["feed_gain_held"][...])
     by_width, got_width, stream = r["by_width"], r["got_width"], r["stream"]
     wide = by_width.shape[-1]
@@ -791,16 +797,13 @@
 
     def z_first_end():
         yield from z_lines.last_round()
-        yield from ring_scatter(
-            qkv_wires,
-            lambda j: r["z_sum"].at[j],
-            reduced.at[:, rest],
-            r["z_left"],
-            r["z_right"],
-            NY,
-            at.y,
-            at.along_y,
-        )
+        terms, beside = r["z_sum"], []
+        for off in (2, 1, 3):
+            y = (at.y + off) % NY
+            beside.append(qkv_wires.copy(terms.at[y], r["z_got"].at[off], at.along_y(y)))
+        yield beside
+        arrived = [r["z_got"].at[off] for off in range(1, NY)]
+        add_rows(reduced.at[:, rest], [terms.at[at.y], *arrived])
 
     later = {
         "T": lambda: lines.turns("l"),
@@ -850,12 +853,15 @@
     for t in range(TP):
         cols = slice(t * wide, (t + 1) * wide)
         mixed[:, cols] = (attended[:, cols].astype(F32) + lowered[t].astype(F32)).astype(BF16)
+    leaving[1].start()
+    for c in leaving:
+        c.wait()
     phase(None)
 
 
 VMEM = pl.BlockSpec(memory_space=pltpu.VMEM)
 ANY = pl.BlockSpec(memory_space=pl.ANY)
-COPIES, COPIES_2, SLOTS = 157, CP, 48
+COPIES, COPIES_2, SLOTS = 157, NZ + 2 * (TP - 1) + NZ - 1, 36
 
 
 def dma(count):
@@ -920,8 +926,7 @@
         "down_far": buf(8, block, DOWN_SPLIT),
         "z_far": buf(8, NY, block, wide - DOWN_SPLIT),
         "z_sum": buf(NY, block, wide - DOWN_SPLIT),
-        "z_left": buf(NY // 2, block, wide - DOWN_SPLIT),
-        "z_right": buf(NY // 2, block, wide - DOWN_SPLIT),
+        "z_got": buf(NY, block, wide - DOWN_SPLIT),
         "reduced": buf(block, wide, kind=F32),
         "by_token": buf(TP, local_rows, wide),
         "lowered": buf(TP, local_rows, wide),
@@ -954,14 +959,15 @@
         scratch[f"sum_{n}"] = buf(NZ, block, extent)
     scratch |= {f"r{n}": dma(TP) for n in range(2)}
     scratch |= {"load": dma(len(WEIGHTS) + len(SMALL)), "send": dma(SLOTS), "recv": dma(COPIES)}
-    scratch |= {"recv_2": dma(COPIES_2), "send_w": dma(24), "recv_w": dma(24)}
+    scratch |= {"held_out": buf(2, *tokens.shape), "leave": dma(2)}
+    scratch |= {"recv_2": dma(COPIES_2), "send_w": dma(8), "recv_w": dma(24)}
 
     names = (*inputs, "streams", *scratch)
     streams = pl.pallas_call(
         functools.partial(layer_kernel, names),
         out_shape=jax.ShapeDtypeStruct((2, *tokens.shape), BF16),
         in_specs=[VMEM if name == "inverse" else ANY for name in inputs],
-        out_specs=VMEM,
+        out_specs=ANY,
         scratch_shapes=list(scratch.values()),
         compiler_params=pltpu.CompilerParams(
             collective_id=0,

time: 151 us -> 150 us (level)
  no operation moved by 1% of the time
where the time goes in v8:
time: 150 us
  Pallas kernels  148 us (99%)
  local copies, waits for them, and re-layouts  1.57 us (1%)
    pallas_call x1, Pallas kernels, on_device(): pl.pallas_call(functools.partial(layer_kernel, names), out_shape=jax.Shap...  148 us

profile of v8, /device:TPU:1, one launch (start us, length us, event | category | flops | bytes accessed | tf_op | source)
XLA Modules:
  0.0 149.9 jit_solution(9121527247741186597)
XLA Ops:
  0.6 147.7 %layer.1 = bf16[2,4,8192]{2,1,0:T(4,128)(2,1)} custom-call(bf16[4,8192]{1,0:T(4,128)(2,1)} %refs_0_.1, f32[1,8192]{1,0:T(1,128)} %bitcast.6, f32[1,8192]{1,0:T(1,128)} %bitcast.7, f32[1,128]{1,0:T(1,128)} %constant.2.clone.refs_3_, bf16[256,128]{1,0:T(8,128)(2,1)} %refs_4_.1, bf16[256,128]{1,0:T(8,128)(2,1)} %refs_5_.1, bf16[256,1024]{1,0:T(8,128)(2,1)} %refs_6_.1, ...), custom_call_target="tpu_custom_call" | custom-call | tf_op jit(solution)/shard_map/layer/pallas_call | solution.py:966
  148.4 1.6 %slice_bitcast_fusion = (bf16[4,8192]{1,0:T(4,128)(2,1)}, bf16[4,8192]{1,0:T(4,128)(2,1)}) fusion(bf16[2,4,8192]{2,1,0:T(4,128)(2,1)} %layer.1), kind=kLoop, calls=%fused_computation | loop fusion | bytes 262144 | tf_op jit(solution)/shard_map/squeeze | solution.py:979

commit v9 on v8

--- a/solution.py
+++ b/solution.py
@@ -66,16 +66,14 @@
         self.queue, self.begun = collections.deque(), set()
 
     def add(self, gen, name="line", step=0):
-        with jax.named_scope(f"{name}_{step}"):
-            needs = advance(gen)
+        needs = advance(gen)
         if needs is not None:
             self.queue.append((needs, gen, name, step + 1))
 
     def go_on(self, entry):
         needs, gen, name, step = entry
-        with jax.named_scope(f"wait_{name}_{step}"):
-            for c in needs:
-                c.wait_recv()
+        for c in needs:
+            c.wait_recv()
         self.add(gen, name, step)
 
     def run(self, until=lambda: False):
@@ -83,7 +81,7 @@
             self.go_on(self.queue.popleft())
 
     def play(self, order, begin):
-        for word in order.split():
+        for word in (w for part in order for w in part.split()):
             if word.isupper():
                 if word not in self.begun:
                     self.begun.add(word)
@@ -98,18 +96,6 @@
                 entry = self.queue[found[0]]
                 del self.queue[found[0]]
                 self.go_on(entry)
-
-
-class Phases:
-    def __init__(self):
-        self.scope = None
-
-    def __call__(self, name):
-        if self.scope:
-            self.scope.__exit__(None, None, None)
-        self.scope = jax.named_scope(name) if name else None
-        if self.scope:
-            self.scope.__enter__()
 
 
 class Place:
@@ -351,7 +337,13 @@
 
 
 QKV_PARTS = ((0, 256), (256, 512), (768, 512))
-QKV_ORDER = "g2 K k1 q1 O p2 A k2 q2 B a1 k3 b1 o1 H a2 b2 k4"
+QKV_ORDER = (
+    "g2 K k1 q1",
+    "O p2 A k2",
+    "q2 B a1 k3",
+    "b1 o1 H a2",
+    "b2 k4",
+)
 GATHER_SPLIT = 768
 DOWN_SPLIT = 640
 
@@ -422,30 +414,52 @@
     return jnp.concatenate([b.reshape(-1, b.shape[-1]) for b in blocks], axis=0)
 
 
-GATHER_ORDER = """yz/1 y0/1 z/1 yz/2 y0/2 E y7/1 y1/1 e1 y6/1 y2/1 z/2 yz/3 y7/2 y1/2 B e2 y6/2 y2/2 b1 y5/1 y3/1 y4/1 yz/4 e3 y5/2 y3/2 y4/2"""
-ORDER = """b2 C D A e4 c1 d1 a1 b3 c2 e5 d2 a2 b4 c3 d3 b5 e6 a3 b6 c4 d4 e7 a4 c5 c6 b7 d5 d6 a5 a6 b8 e8 c7 V v1 W w1 d7 a7 c8 d8 a8 T U N n1 t1 u1 n2 L l1"""
+GATHER_ORDER = (
+    "yz/1 y0/1 z/1 yz/2",
+    "y0/2 E y7/1 y1/1",
+    "e1 y6/1 y2/1 z/2",
+    "yz/3 y7/2 y1/2 B",
+    "e2 y6/2 y2/2 b1",
+    "y5/1 y3/1 y4/1 yz/4",
+    "e3 y5/2 y3/2 y4/2",
+)
+ORDER = (
+    "b2 C D A",
+    "e4 c1 d1 a1",
+    "b3 c2 e5 d2",
+    "a2 b4 c3 d3",
+    "b5 e6 a3 b6",
+    "c4 d4 e7 a4",
+    "c5 c6 b7 d5",
+    "d6 a5 a6 b8",
+    "e8 c7 V v1",
+    "W w1 d7 a7",
+    "c8 d8 a8 T",
+    "U N n1 t1",
+    "u1 n2 L l1",
+)
 
 
 def feed_chunk(wires, at, r, c, produced, finished):
     partner = at.partner()
-    units = r["gate"].shape[1]
+    units = r.gate.shape[1]
     part, held, total, hidden, down_part = (
         r[f"{name}_{c}"] for name in ("unit_part", "held", "unit_total", "hidden", "down_part")
     )
 
     def tile(w_ref, col, width, start):
         p = jnp.dot(
-            chunk_rows(r["stream"], at, CHUNKS[c]), w_ref[:, pl.ds(col, width)], preferred_element_type=F32
+            chunk_rows(r.stream, at, CHUNKS[c]), w_ref[:, pl.ds(col, width)], preferred_element_type=F32
         )
         cols = pl.ds(start + col, width)
         part[:, :, :, :, cols] = p.astype(BF16).reshape(*part.shape[:4], width)
 
     for t in range(units // 256):
-        tile(r["gate"], t * 256, 256, 0)
-        tile(r["up"], t * 256, 256, units)
+        tile(r.gate, t * 256, 256, 0)
+        tile(r.up, t * 256, 256, units)
     if units % 256:
-        tile(r["gate"], units // 256 * 256, units % 256, 0)
-        tile(r["up"], units // 256 * 256, units % 256, units)
+        tile(r.gate, units // 256 * 256, units % 256, 0)
+        tile(r.up, units // 256 * 256, units % 256, units)
     yield [wires.copy(part.at[:, :, 1 - at.core], held, partner)]
     add_rows(held, [held, part.at[:, :, at.core]])
     yield from ring_scatter(
@@ -475,7 +489,7 @@
     def down(i, carry):
         cols = pl.ds(pl.multiple_of(i * 256, 256), 256)
         p = jnp.dot(
-            hidden[...].reshape(-1, units), r["down"][:, cols], preferred_element_type=F32
+            hidden[...].reshape(-1, units), r.down[:, cols], preferred_element_type=F32
         )
         down_part[:, :, :, cols] = p.astype(BF16).reshape(*down_part.shape[:3], 256)
         return carry
@@ -505,49 +519,49 @@
 ALONG_Y = ("key", "value", "query", "out")
 
 
+class Refs(dict):
+    __getattr__ = dict.__getitem__
+
+
 def layer_kernel(names, *refs):
-    r = dict(zip(names, refs))
+    r = Refs(zip(names, refs))
     at = Place()
-    qkv_wires, wires = Wires(r["send"], r["recv"]), Wires(r["send"], r["recv_2"])
+    qkv_wires, wires = Wires(r.send, r.recv), Wires(r.send, r.recv_2)
     steps = Steps()
-    tokens = r["tokens_held"]
+    tokens = r.tokens_held
     local_rows, model = tokens.shape
-    attended, mixed = r["held_out"].at[0], r["held_out"].at[1]
-    cos, sin = r["cos"], r["sin"]
-
-    phase = Phases()
-    phase("greet")
+    attended, mixed = r.held_out.at[0], r.held_out.at[1]
+    cos, sin = r.cos, r.sin
+
     greeted = greet_group("cp", CP, at.cp) + greet_group("tp", TP, at.tp)
     loads = {}
     for n, name in enumerate(SMALL):
         held = r[name + "_held"]
-        loads[name] = pltpu.make_async_copy(r[name], held, r["load"].at[len(WEIGHTS) + n])
+        loads[name] = pltpu.make_async_copy(r[name], held, r.load.at[len(WEIGHTS) + n])
         loads[name].start()
     for n, name in enumerate(WEIGHTS):
         held = r[name].at[at.y] if name in ALONG_Y else r[name]
-        loads[name] = pltpu.make_async_copy(r[name + "_weight"], held, r["load"].at[n])
+        loads[name] = pltpu.make_async_copy(r[name + "_weight"], held, r.load.at[n])
         loads[name].start()
 
     block = cos.shape[0]
     positions = at.cp * block + lax.broadcasted_iota(jnp.int32, (block, HD), 0)
-    angles = positions.astype(F32) * r["inverse"][...]
+    angles = positions.astype(F32) * r.inverse[...]
     first_half = lax.broadcasted_iota(jnp.int32, (block, HD), 1) < HD // 2
     cos[...] = jnp.cos(angles)
     sin[...] = jnp.where(first_half, -jnp.sin(angles), jnp.sin(angles))
 
     for name in SMALL:
         loads[name].wait()
-    normed = normalize(tokens[...].astype(F32), r["attention_gain_held"][...])
-    slices, got, columns = r["slices"], r["got"], r["columns"]
+    normed = normalize(tokens[...].astype(F32), r.attention_gain_held[...])
+    slices, got, columns = r.slices, r.got, r.columns
     wide = slices.shape[-1]
     for z in range(NZ):
         slices[z] = normed[:, z * wide : (z + 1) * wide]
-    phase("barrier")
     await_greetings(greeted)
 
-    phase("spread_cp")
-    weight_wires = Wires(r["send_w"], r["recv_w"])
-    query_cols, out_cols = r["query"].shape[-1] // 2, r["out"].shape[-1] // 2
+    weight_wires = Wires(r.send_w, r.recv_w)
+    query_cols, out_cols = r.query.shape[-1] // 2, r.out.shape[-1] // 2
 
     def gathered(*blocks):
         rings = [ring_gather(weight_wires, b, NY, at.y, at.along_y) for b in blocks]
@@ -558,11 +572,11 @@
             yield [c for some in flights for c in some]
 
     weight_parts = {
-        "G": lambda: gathered(lambda j: r["key"].at[j], lambda j: r["value"].at[j]),
-        "P": lambda: gathered(lambda j: r["query"].at[j, :, pl.ds(0, query_cols)]),
-        "Q": lambda: gathered(lambda j: r["query"].at[j, :, pl.ds(query_cols, query_cols)]),
-        "O": lambda: gathered(lambda j: r["out"].at[j, :, pl.ds(0, out_cols)]),
-        "H": lambda: gathered(lambda j: r["out"].at[j, :, pl.ds(out_cols, out_cols)]),
+        "G": lambda: gathered(lambda j: r.key.at[j], lambda j: r.value.at[j]),
+        "P": lambda: gathered(lambda j: r.query.at[j, :, pl.ds(0, query_cols)]),
+        "Q": lambda: gathered(lambda j: r.query.at[j, :, pl.ds(query_cols, query_cols)]),
+        "O": lambda: gathered(lambda j: r.out.at[j, :, pl.ds(0, out_cols)]),
+        "H": lambda: gathered(lambda j: r.out.at[j, :, pl.ds(out_cols, out_cols)]),
     }
 
     def begin_weights(letter):
@@ -571,33 +585,31 @@
     def keep_slice():
         for name in ALONG_Y:
             loads[name].wait()
-        steps.play("G P", begin_weights)
+        steps.play(("G P",), begin_weights)
         got[at.z] = slices[at.z]
 
     exchange(
-        r["send"], r["recv_2"], lambda p: slices.at[p], lambda p: got.at[p], at.along_z, NZ, at.z, keep_slice
-    )
-    steps.play("g1 Q", begin_weights)
-
-    phase("spread_tp")
+        r.send, r.recv_2, lambda p: slices.at[p], lambda p: got.at[p], at.along_z, NZ, at.z, keep_slice
+    )
+    steps.play(("g1 Q",), begin_weights)
+
     def keep_columns():
         columns[at.tp] = got[...]
 
     exchange(
-        r["send"], r["r0"], lambda p: got, lambda p: columns.at[p], "tp", TP, at.tp, keep_columns
-    )
-    phase("relayout")
-    rows_in = r["rows_in"]
+        r.send, r.r0, lambda p: got, lambda p: columns.at[p], "tp", TP, at.tp, keep_columns
+    )
+    rows_in = r.rows_in
 
     def in_order(b, carry):
         parts = [columns[t, b].astype(F32) for t in range(TP)]
         rows_in[b] = jnp.concatenate(parts, axis=0).astype(BF16)
         return carry
 
-    steps.play("p1", begin_weights)
+    steps.play(("p1",), begin_weights)
     lax.fori_loop(0, NZ, in_order, 0)
 
-    part, summed, shared = r["qkv_part"], r["summed"], r["shared"]
+    part, summed, shared = r.qkv_part, r.summed, r.shared
 
     def product(name, cols, start):
         x = rows_in[...].reshape(-1, wide)
@@ -642,13 +654,11 @@
         else:
             begin_weights(letter)
 
-    phase("qkv_sum")
     steps.play(QKV_ORDER, begin_part)
     steps.begun.clear()
     qkv_wires.drain()
 
-    phase("attend")
-    every = r["every"]
+    every = r.every
     heads = (summed.shape[1] - 2 * HD) // HD
     block = summed.shape[0]
     query = jnp.concatenate(
@@ -671,17 +681,16 @@
     for h in range(heads):
         every[at.z, :, h * HD : (h + 1) * HD] = mean[h * block : (h + 1) * block]
 
-    phase("gather_att")
-    projected = r["projected"]
+    projected = r.projected
     owners, seen = [], set()
 
     def out_chunk(c):
         chunk = OUT_CHUNKS[c]
         part, arrived, total = r[f"out_part_{c}"], r[f"out_got_{c}"], r[f"out_total_{c}"]
         x = jnp.concatenate([every[(at.z + off) % NZ] for off in chunk], axis=0)
-        cols = r["out"].shape[-1]
+        cols = r.out.shape[-1]
         for y in range(NY):
-            p = jnp.dot(x, r["out"][y], preferred_element_type=F32)
+            p = jnp.dot(x, r.out[y], preferred_element_type=F32)
             for n in range(len(chunk)):
                 for t in range(TP):
                     first = n * block + t * local_rows
@@ -709,44 +718,41 @@
         seen.add(off)
         for c, chunk in OUT_CHUNKS.items():
             if off in chunk and seen >= set(chunk):
-                steps.play("o2 h1 h2", None)
+                steps.play(("o2 h1 h2",), None)
                 steps.add(out_chunk(c), f"out{c}")
 
     steps.add(
         far_gather(wires, lambda i: every.at[i], NZ, at.z, at.along_z, att_there), "z"
     )
-    steps.play("h1 z/1 z/2", None)
+    steps.play(("h1 z/1 z/2",), None)
     steps.run()
-    phase("out_cp")
     for c in owners:
         c.wait_recv()
     wires.drain()
     weight_wires.drain()
-    phase("norm_feed")
     wide = projected.shape[-1]
     for z in range(NZ):
         cols = slice(z * wide, (z + 1) * wide)
         attended[:, cols] = (tokens[:, cols].astype(F32) + projected[z].astype(F32)).astype(BF16)
 
     leaving = [
-        pltpu.make_async_copy(r["held_out"].at[n], r["streams"].at[n], r["leave"].at[n])
+        pltpu.make_async_copy(r.held_out.at[n], r.streams.at[n], r.leave.at[n])
         for n in range(2)
     ]
     leaving[0].start()
 
-    normed = normalize(attended[...].astype(F32), r["feed_gain_held"][...])
-    by_width, got_width, stream = r["by_width"], r["got_width"], r["stream"]
+    normed = normalize(attended[...].astype(F32), r.feed_gain_held[...])
+    by_width, got_width, stream = r.by_width, r.got_width, r.stream
     wide = by_width.shape[-1]
     for t in range(TP):
         by_width[t] = normed[:, t * wide : (t + 1) * wide]
 
-    phase("swap1")
     def keep_width():
         got_width[at.tp] = by_width[at.tp]
 
     exchange(
-        r["send"],
-        r["r1"],
+        r.send,
+        r.r1,
         lambda p: by_width.at[p],
         lambda p: got_width.at[p],
         "tp",
@@ -754,13 +760,12 @@
         at.tp,
         keep_width,
     )
-    phase("gather_feed")
     stream[at.z, at.y] = jnp.concatenate(
         [got_width[t].astype(F32) for t in range(TP)], axis=0
     ).astype(BF16)
     for name in ("gate", "up", "down"):
         loads[name].wait()
-    reduced = r["reduced"]
+    reduced = r.reduced
     places = {off: (c, n) for c, chunk in CHUNKS.items() for n, off in enumerate(chunk)}
 
     def piece(name, off):
@@ -774,15 +779,15 @@
         qkv_wires,
         lambda off: piece("down_sum", off),
         reduced.at[:, pl.ds(0, DOWN_SPLIT)],
-        r["down_far"],
+        r.down_far,
         to_z,
     )
     rest = pl.ds(DOWN_SPLIT, reduced.shape[1] - DOWN_SPLIT)
     z_lines = FarScatter(
         qkv_wires,
         lambda off: piece("down_part", off).at[:, :, rest],
-        r["z_sum"],
-        r["z_far"],
+        r.z_sum,
+        r.z_far,
         to_z,
     )
     there = {}
@@ -797,12 +802,12 @@
 
     def z_first_end():
         yield from z_lines.last_round()
-        terms, beside = r["z_sum"], []
+        terms, beside = r.z_sum, []
         for off in (2, 1, 3):
             y = (at.y + off) % NY
-            beside.append(qkv_wires.copy(terms.at[y], r["z_got"].at[off], at.along_y(y)))
+            beside.append(qkv_wires.copy(terms.at[y], r.z_got.at[off], at.along_y(y)))
         yield beside
-        arrived = [r["z_got"].at[off] for off in range(1, NY)]
+        arrived = [r.z_got.at[off] for off in range(1, NY)]
         add_rows(reduced.at[:, rest], [terms.at[at.y], *arrived])
 
     later = {
@@ -831,9 +836,8 @@
     assert len(there) == len(CHUNKS)
     steps.play(ORDER, begin)
     assert not steps.queue
-    phase("swap2")
     qkv_wires.drain()
-    by_token, lowered = r["by_token"], r["lowered"]
+    by_token, lowered = r.by_token, r.lowered
     for t in range(TP):
         by_token[t] = reduced[pl.ds(t * local_rows, local_rows), :].astype(BF16)
 
@@ -841,8 +845,8 @@
         lowered[at.tp] = by_token[at.tp]
 
     exchange(
-        r["send"],
-        r["r0"],
+        r.send,
+        r.r0,
         lambda p: by_token.at[p],
         lambda p: lowered.at[p],
         "tp",
@@ -856,7 +860,6 @@
     leaving[1].start()
     for c in leaving:
         c.wait()
-    phase(None)
 
 
 VMEM = pl.BlockSpec(memory_space=pltpu.VMEM)
@@ -890,47 +893,47 @@
     pair = np.arange(HD, dtype=np.float32)[None] % (HD // 2)
     inverse = (np.float64(rope_base) ** (-(pair * 2.0 / HD))).astype(np.float32)
 
-    inputs = {
-        "tokens": tokens,
-        "attention_gain": attention_gain[None],
-        "feed_gain": feed_gain[None],
-        "inverse": jnp.asarray(inverse),
-        "key_weight": key_weight,
-        "value_weight": value_weight,
-        "query_weight": query_weight,
-        "out_weight": out_weight,
-        "gate_weight": gate_weight,
-        "up_weight": up_weight,
-        "down_weight": down_weight,
-    }
+    inputs = dict(
+        tokens=tokens,
+        attention_gain=attention_gain[None],
+        feed_gain=feed_gain[None],
+        inverse=jnp.asarray(inverse),
+        key_weight=key_weight,
+        value_weight=value_weight,
+        query_weight=query_weight,
+        out_weight=out_weight,
+        gate_weight=gate_weight,
+        up_weight=up_weight,
+        down_weight=down_weight,
+    )
 
     def buf(*shape, kind=BF16):
         return pltpu.VMEM(shape, kind)
 
     scratch = {name: buf(*inputs[name + "_weight"].shape) for name in WEIGHTS}
-    scratch |= {
-        "cos": buf(block, HD, kind=F32),
-        "sin": buf(block, HD, kind=F32),
-        "slices": buf(NZ, local_rows, wide),
-        "got": buf(NZ, local_rows, wide),
-        "columns": buf(TP, NZ, local_rows, wide),
-        "rows_in": buf(NZ, block, wide),
-        "qkv_part": buf(NZ, block, qkv),
-        "summed": buf(block, qkv, kind=F32),
-        "shared": buf(NZ, NY, block, 2 * HD),
-        "every": buf(NZ, block, wide),
-        "projected": buf(NZ, local_rows, wide),
-        "by_width": buf(TP, local_rows, wide),
-        "got_width": buf(TP, local_rows, wide),
-        "stream": buf(NZ, NY, block, wide),
-        "down_far": buf(8, block, DOWN_SPLIT),
-        "z_far": buf(8, NY, block, wide - DOWN_SPLIT),
-        "z_sum": buf(NY, block, wide - DOWN_SPLIT),
-        "z_got": buf(NY, block, wide - DOWN_SPLIT),
-        "reduced": buf(block, wide, kind=F32),
-        "by_token": buf(TP, local_rows, wide),
-        "lowered": buf(TP, local_rows, wide),
-    }
+    scratch |= dict(
+        cos=buf(block, HD, kind=F32),
+        sin=buf(block, HD, kind=F32),
+        slices=buf(NZ, local_rows, wide),
+        got=buf(NZ, local_rows, wide),
+        columns=buf(TP, NZ, local_rows, wide),
+        rows_in=buf(NZ, block, wide),
+        qkv_part=buf(NZ, block, qkv),
+        summed=buf(block, qkv, kind=F32),
+        shared=buf(NZ, NY, block, 2 * HD),
+        every=buf(NZ, block, wide),
+        projected=buf(NZ, local_rows, wide),
+        by_width=buf(TP, local_rows, wide),
+        got_width=buf(TP, local_rows, wide),
+        stream=buf(NZ, NY, block, wide),
+        down_far=buf(8, block, DOWN_SPLIT),
+        z_far=buf(8, NY, block, wide - DOWN_SPLIT),
+        z_sum=buf(NY, block, wide - DOWN_SPLIT),
+        z_got=buf(NY, block, wide - DOWN_SPLIT),
+        reduced=buf(block, wide, kind=F32),
+        by_token=buf(TP, local_rows, wide),
+        lowered=buf(TP, local_rows, wide),
+    )
     for name in SMALL:
         scratch[name + "_held"] = buf(*inputs[name].shape, kind=inputs[name].dtype)
     for name in ALONG_Y:

time: 150 us -> 150 us (level)
  no operation moved by 1% of the time
where the time goes in v9:
time: 150 us
  Pallas kernels  148 us (99%)
  local copies, waits for them, and re-layouts  1.57 us (1%)
    pallas_call x1, Pallas kernels, on_device(): pl.pallas_call(functools.partial(layer_kernel, names), out_shape=jax.Shap...  148 us

profile of v9, /device:TPU:1, one launch (start us, length us, event | category | flops | bytes accessed | tf_op | source)
XLA Modules:
  0.0 149.9 jit_solution(9121527247741186597)
XLA Ops:
  0.6 147.7 %layer.1 = bf16[2,4,8192]{2,1,0:T(4,128)(2,1)} custom-call(bf16[4,8192]{1,0:T(4,128)(2,1)} %refs_0_.1, f32[1,8192]{1,0:T(1,128)} %bitcast.6, f32[1,8192]{1,0:T(1,128)} %bitcast.7, f32[1,128]{1,0:T(1,128)} %constant.2.clone.refs_3_, bf16[256,128]{1,0:T(8,128)(2,1)} %refs_4_.1, bf16[256,128]{1,0:T(8,128)(2,1)} %refs_5_.1, bf16[256,1024]{1,0:T(8,128)(2,1)} %refs_6_.1, ...), custom_call_target="tpu_custom_call" | custom-call | tf_op jit(solution)/shard_map/layer/pallas_call | solution.py:969
  148.4 1.6 %slice_bitcast_fusion = (bf16[4,8192]{1,0:T(4,128)(2,1)}, bf16[4,8192]{1,0:T(4,128)(2,1)}) fusion(bf16[2,4,8192]{2,1,0:T(4,128)(2,1)} %layer.1), kind=kLoop, calls=%fused_computation | loop fusion | bytes 262144 | tf_op jit(solution)/shard_map/squeeze | solution.py:982
